TPU v7x, 32 devices: a whole 2x2x4 slice. The times are simulated.
32 devices in a mesh: ctx: 8 (over z, x), fsdp: 4 (over y, core).
Axes of the slice: x: 2, y: 2, z: 4, core: 2. Of those that a mesh axis runs over, the one named last changes fastest.
Arguments:
- layer_input: bfloat16 [4, 1024, 896], P('fsdp', 'ctx'), may hold values from -6 to 6
- seq_ids: int32 [4, 1024], P('fsdp', 'ctx'), may hold values from 0 to 1, as said below
- positions: int32 [4, 1024], P('fsdp', 'ctx'), may hold values from 0 to 895, as said below
- norm_gain: bfloat16 [896], P('fsdp'), may hold values from 0.5 to 1.5
- w_query: bfloat16 [896, 896], P('fsdp'), may hold values from -0.1875 to 0.1875
- b_query: bfloat16 [896], P('fsdp'), may hold values from -3 to 3
- w_key: bfloat16 [896, 128], P('fsdp'), may hold values from -0.1875 to 0.1875
- b_key: bfloat16 [128], P('fsdp'), may hold values from -3 to 3
- w_value: bfloat16 [896, 128], P('fsdp'), may hold values from -0.1875 to 0.1875
- b_value: bfloat16 [128], P('fsdp'), may hold values from -3 to 3
- w_output: bfloat16 [896, 896], P('fsdp'), may hold values from -2 to 2
- mlp_gain: bfloat16 [896], P('fsdp'), may hold values from 0.5 to 1.5
- w_gate: bfloat16 [896, 4864], P(None, 'fsdp'), may hold values from -0.1875 to 0.1875
- w_up: bfloat16 [896, 4864], P(None, 'fsdp'), may hold values from -0.1875 to 0.1875
- w_down: bfloat16 [4864, 896], P('fsdp'), may hold values from -0.078125 to 0.078125
- cotangent: bfloat16 [4, 1024, 896], P('fsdp', 'ctx'), may hold values from -6 to 6
Outputs:
- block_out: bfloat16 [4, 1024, 896], P('fsdp', 'ctx')
- input_grad: bfloat16 [4, 1024, 896], P('fsdp', 'ctx')
- norm_gain_grad: float32 [896], P('fsdp')
- w_query_grad: float32 [896, 896], P('fsdp')
- b_query_grad: float32 [896], P('fsdp')
- w_key_grad: float32 [896, 128], P('fsdp')
- b_key_grad: float32 [128], P('fsdp')
- w_value_grad: float32 [896, 128], P('fsdp')
- b_value_grad: float32 [128], P('fsdp')
- w_output_grad: float32 [896, 896], P('fsdp')
- mlp_gain_grad: float32 [896], P('fsdp')
- w_gate_grad: float32 [896, 4864], P(None, 'fsdp')
- w_up_grad: float32 [896, 4864], P(None, 'fsdp')
- w_down_grad: float32 [4864, 896], P('fsdp')
- lse: float32 [4, 14, 1024], P('fsdp', None, 'ctx')
Inputs may be any that keep to these rules, and one draw needn't show every extreme that they name: Each row holds two documents: seq_ids is 0 on its first r positions and 1 on the rest, with 128 <= r <= 256; in the first row r = 128. positions count from 0 at the start of each document of the row.
All inputs are finite; a program needn't handle non-finite values.
Results may differ from a plain program's by a relative error of at most 0.035.
Values may be sent and summed in bfloat16 or wider, within the bound.
A program may use at most 256 MiB of HBM per device.

v0:
```python
import functools
import math

import jax
import jax.numpy as jnp
from jax import lax
from jax.experimental import pallas as pl
from jax.experimental.pallas import tpu as pltpu
from jax.sharding import PartitionSpec as P

H = 14
KV = 2
HD = 64


EPSILON = 1e-06
ROPE_BASE = 1000000.0
MASK_FILL = -1e30
MESH = pl.DeviceIdType.MESH
VMEM = pl.BlockSpec(memory_space=pltpu.VMEM)
f32 = jnp.float32
bf16 = jnp.bfloat16


def rope_tables(positions, head_dim):
    half = head_dim // 2
    freq = ROPE_BASE ** (-(jnp.arange(half, dtype=jnp.float32) * 2.0 / head_dim))
    angle = positions.astype(jnp.float32)[:, None] * freq[None, :]
    return (jnp.cos(angle)[:, None, :], jnp.sin(angle)[:, None, :])


def rotate(values, cosine, sine_table):
    half = values.shape[-1] // 2
    leading, trailing = (values[..., :half], values[..., half:])
    return jnp.concatenate(
        [leading * cosine - trailing * sine_table, trailing * cosine + leading * sine_table], -1
    )


def rotate_back(grads, cosine, sine_table):
    half = grads.shape[-1] // 2
    leading, trailing = (grads[..., :half], grads[..., half:])
    return jnp.concatenate(
        [leading * cosine + trailing * sine_table, trailing * cosine - leading * sine_table], -1
    )


def norm_back(values, inverse, gain, grads):
    scaled = values * inverse
    weighted = grads * gain
    grad_values = inverse * (weighted - scaled * jnp.mean(weighted * scaled, -1, keepdims=True))
    return (grad_values, jnp.sum(grads * scaled, 0))


def remote(src, dst, send_sem, recv_sem, device):
    return pltpu.make_async_remote_copy(
        src_ref=src, dst_ref=dst, send_sem=send_sem, recv_sem=recv_sem, device_id=device,
        device_id_type=MESH,
    )


def where_am_i():
    c, f = lax.axis_index("ctx"), lax.axis_index("fsdp")
    c2 = c + 1 - 2 * (c % 2)
    m = f + 1 - 2 * (f % 2)
    n = (f + 2) % 4
    return c, f, c2, m, n


def greet(devices):
    barrier = pltpu.get_barrier_semaphore()
    for device in devices:
        pl.semaphore_signal(barrier, inc=1, device_id=device, device_id_type=MESH)
    pl.semaphore_wait(barrier, len(devices))


def gather_start(items, ss, rs, place):
    c, f, _, m, n = place
    h = c % 2
    for i, (src, dst) in enumerate(items):
        half = src.shape[0] // 2
        rows = pl.ds(h * half, half)
        remote(src.at[rows], dst(f).at[rows], ss.at[i, 1], rs.at[i, 1], (c, n)).start()
    for i, (src, dst) in enumerate(items):
        remote(src, dst(f), ss.at[i, 0], rs.at[i, 0], (c, m)).start()
        dst(f)[...] = src[...]


def gather_finish(items, ss, rs, place):
    c, f, c2, m, n = place
    h = c % 2
    far = (m + 2) % 4
    for i, (src, dst) in enumerate(items):
        half = src.shape[0] // 2
        mine = dst(n).at[pl.ds(h * half, half)]
        remote(mine, mine, ss.at[i, 1], rs.at[i, 1], (c, n)).wait_recv()
        remote(mine, mine, ss.at[i, 2], rs.at[i, 2], (c2, f)).start()
        remote(mine, mine, ss.at[i, 3], rs.at[i, 3], (c, m)).start()
    for i, (src, dst) in enumerate(items):
        half = src.shape[0] // 2
        other = dst(n).at[pl.ds((1 - h) * half, half)]
        remote(other, other, ss.at[i, 2], rs.at[i, 2], (c2, f)).wait_recv()
        remote(other, other, ss.at[i, 4], rs.at[i, 4], (c, m)).start()
    for i, (src, dst) in enumerate(items):
        half = src.shape[0] // 2
        mine, other = pl.ds(h * half, half), pl.ds((1 - h) * half, half)
        remote(src, dst(m), ss.at[i, 0], rs.at[i, 0], (c, m)).wait()
        remote(src.at[mine], dst(f).at[mine], ss.at[i, 1], rs.at[i, 1], (c, n)).wait_send()
        remote(src.at[mine], dst(n).at[mine], ss.at[i, 2], rs.at[i, 2], (c2, f)).wait_send()
        remote(src.at[mine], dst(far).at[mine], ss.at[i, 3], rs.at[i, 3], (c, m)).wait()
        remote(src.at[other], dst(far).at[other], ss.at[i, 4], rs.at[i, 4], (c, m)).wait()


def tokens_start(items, ss, rs, place):
    c, f, _, m, n = place
    for i, (src, dst) in enumerate(items):
        half = src.shape[0] // 2
        for j in range(2):
            rows = pl.ds(j * half, half)
            remote(src.at[rows], dst(f, rows), ss.at[i, 1 + j], rs.at[i, 1 + j], (c, n)).start()
    for i, (src, dst) in enumerate(items):
        rows = pl.ds(0, src.shape[0])
        remote(src, dst(f, rows), ss.at[i, 0], rs.at[i, 0], (c, m)).start()
        dst(f, rows)[...] = src[...]


def tokens_finish(items, ss, rs, place):
    c, f, _, m, n = place
    far = (m + 2) % 4
    for i, (src, dst) in enumerate(items):
        half = src.shape[0] // 2
        for j in range(2):
            here = dst(n, pl.ds(j * half, half))
            remote(here, here, ss.at[i, 1 + j], rs.at[i, 1 + j], (c, n)).wait_recv()
            remote(here, here, ss.at[i, 3 + j], rs.at[i, 3 + j], (c, m)).start()
    for i, (src, dst) in enumerate(items):
        half = src.shape[0] // 2
        remote(src, dst(m, pl.ds(0, src.shape[0])), ss.at[i, 0], rs.at[i, 0], (c, m)).wait()
        for j in range(2):
            rows = pl.ds(j * half, half)
            remote(src.at[rows], dst(f, rows), ss.at[i, 1 + j], rs.at[i, 1 + j], (c, n)).wait_send()
            remote(src.at[rows], dst(far, rows), ss.at[i, 3 + j], rs.at[i, 3 + j], (c, m)).wait()


def gather_sems(count):
    return [pltpu.SemaphoreType.DMA((count, 5)), pltpu.SemaphoreType.DMA((count, 5))]


def comm_call(body, out_shape, scratch, ident):
    def call(*args):
        return pl.pallas_call(
            body,
            out_shape=out_shape,
            in_specs=[VMEM] * len(args),
            out_specs=jax.tree.map(lambda _: VMEM, out_shape),
            scratch_shapes=scratch,
            compiler_params=pltpu.CompilerParams(
                collective_id=ident, has_side_effects=True, vmem_limit_bytes=48 << 20
            ),
        )(*args)

    return call


def front_body(
    ctx, depth, wq, wk, wv, wo, small, seg, wp_o, wo_o, small_o, seg_o, ss, rs, small_ss, small_rs, seg_ss, seg_rs
):
    place = where_am_i()
    c, f, _, m, n = place
    far = (m + 2) % 4
    peers = [lax.rem(c + k, ctx) for k in range(1, ctx)]
    greet([(p, f) for p in peers] + [(c, m), (c, n), (c, far)])
    width = wq.shape[1]
    narrow = wk.shape[1]

    def rows(g):
        return pl.ds(pl.multiple_of(g * depth, 16), depth)

    items = [
        (wq, lambda g: wp_o.at[rows(g), pl.ds(0, width)]),
        (wk, lambda g: wp_o.at[rows(g), pl.ds(width, narrow)]),
        (wv, lambda g: wp_o.at[rows(g), pl.ds(width + narrow, narrow)]),
        (wo, lambda g: wo_o.at[rows(g)]),
    ]
    copies = [
        remote(small, small_o.at[f], small_ss.at[k], small_rs.at[k], (c, g)) for k, g in enumerate((m, n, far))
    ]
    for copy in copies:
        copy.start()
    for k, p in enumerate(peers):
        remote(seg, seg_o.at[c], seg_ss.at[k], seg_rs.at[k], (p, f)).start()
    gather_start(items, ss, rs, place)
    small_o[f] = small[...]
    seg_o[c] = seg[...]
    gather_finish(items, ss, rs, place)
    for k, g in enumerate((m, n, far)):
        remote(small, small_o.at[g], small_ss.at[k], small_rs.at[k], (c, g)).wait()
    for k, p in enumerate(peers):
        giver = lax.rem(c + ctx - 1 - k, ctx)
        remote(seg, seg_o.at[giver], seg_ss.at[k], seg_rs.at[k], (p, f)).wait()


def spread_start(src, dst, ss, rs, place, lines):
    c, f, c2, _, _ = place
    for k in range(1, lines):
        p = lax.rem(c // 2 + k, lines) * 2 + c % 2
        remote(src, dst.at[c], ss.at[0, k], rs.at[0, k], (p, f)).start()
    remote(src, dst.at[c], ss.at[1, 0], rs.at[1, 0], (c2, f)).start()


def spread_finish(src, dst, ss, rs, place, lines):
    c, f, c2, _, _ = place
    for k in range(1, lines):
        giver = lax.rem(c // 2 + lines - k, lines) * 2 + c % 2
        block = dst.at[giver]
        remote(block, block, ss.at[0, k], rs.at[0, k], (c2, f)).wait_recv()
        remote(block, block, ss.at[1, k], rs.at[1, k], (c2, f)).start()
    for k in range(lines):
        giver = lax.rem(c2 // 2 + lines - k, lines) * 2 + c2 % 2
        remote(src, dst.at[giver], ss.at[1, k], rs.at[1, k], (c2, f)).wait()
        if k:
            remote(src, dst.at[c], ss.at[0, k], rs.at[0, k], (c2, f)).wait_send()


def line_devices(place, lines):
    c, f, c2, _, _ = place
    return [(lax.rem(c // 2 + k, lines) * 2 + c % 2, f) for k in range(1, lines)] + [(c2, f)]


def kv_body(lines, kv, kv_o, ss, rs):
    place = where_am_i()
    greet(line_devices(place, lines))
    spread_start(kv, kv_o, ss, rs, place, lines)
    kv_o[place[0]] = kv[...]
    spread_finish(kv, kv_o, ss, rs, place, lines)


def ag_body(x, x_o, ss, rs):
    place = where_am_i()
    c, _, _, m, n = place
    greet([(c, m), (c, n)])
    items = [(x, lambda g, rows: x_o.at[g, rows])]
    tokens_start(items, ss, rs, place)
    tokens_finish(items, ss, rs, place)


def project_body(x, vec, x_o, vec_o, ss, rs, held, vs, vr):
    place = where_am_i()
    c, _, _, m, n = place
    far = (m + 2) % 4
    greet([(c, m), (c, n), (c, far)])
    items = [(x, lambda g, rows: x_o.at[g, rows])]
    tokens_start(items, ss, rs, place)
    copies = [remote(vec, held.at[k], vs.at[k], vr.at[k], (c, g)) for k, g in enumerate((m, n, far))]
    for copy in copies:
        copy.start()
    tokens_finish(items, ss, rs, place)
    total = vec[...]
    for k, copy in enumerate(copies):
        copy.wait()
        total = total + held[k]
    vec_o[...] = total


def rs_body(part, out, near, sums, far_in, ss, rs):
    c, f, _, m, n = where_am_i()
    far = (m + 2) % 4
    greet([(c, m), (c, n)])
    first = remote(part.at[far], near.at[0], ss.at[0], rs.at[0], (c, m))
    second = remote(part.at[m], near.at[1], ss.at[1], rs.at[1], (c, m))
    first.start()
    second.start()
    first.wait()
    sums[...] = (part[n].astype(f32) + near[0].astype(f32)).astype(bf16)
    across = remote(sums, far_in, ss.at[2], rs.at[2], (c, n))
    across.start()
    second.wait()
    mine = part[f].astype(f32) + near[1].astype(f32)
    across.wait()
    out[...] = mine + far_in[...].astype(f32)


def dkv_body(ctx, part, ghl, sl, out, ghl_o, sl_o, held, ss, rs, gs, gr, as_, ar):
    place = where_am_i()
    c, f, _, m, n = place
    far = (m + 2) % 4
    peers = [lax.rem(c + k, ctx) for k in range(1, ctx)]
    greet([(p, f) for p in peers] + [(c, m), (c, n), (c, far)])
    for k, p in enumerate(peers):
        remote(part.at[p], held.at[k], ss.at[k], rs.at[k], (p, f)).start()
    for k, g in enumerate((n, far, m)):
        remote(sl.at[g], sl_o.at[f], as_.at[k], ar.at[k], (c, g)).start()
    items = [(ghl, lambda g, rows: ghl_o.at[g, rows])]
    tokens_start(items, gs, gr, place)
    sl_o[f] = sl[f]
    total = part[c].astype(f32)
    tokens_finish(items, gs, gr, place)
    for k, p in enumerate(peers):
        remote(part.at[p], held.at[k], ss.at[k], rs.at[k], (p, f)).wait()
        total = total + held[k].astype(f32)
    for k, g in enumerate((n, far, m)):
        remote(sl.at[g], sl_o.at[g], as_.at[k], ar.at[k], (c, g)).wait()
    out[...] = total


def over_last(a, b):
    return lax.dot_general(a, b, (((1,), (1,)), ((), ())), preferred_element_type=f32)


def over_first(a, b):
    return lax.dot_general(a, b, (((0,), (0,)), ((), ())), preferred_element_type=f32)


def plain_dot(a, b):
    return jnp.dot(a, b, preferred_element_type=f32)


def hidden_units(x, cot, wg, wu, wd):
    gate, up, g_act = over_last(wg, x), over_last(wu, x), over_last(wd, cot)
    sg = jax.nn.sigmoid(gate)
    silu = gate * sg
    act = (silu * up).astype(bf16)
    g_gate = (g_act * up * (sg * (1.0 + gate * (1.0 - sg)))).astype(bf16)
    g_up = (g_act * silu).astype(bf16)
    return act, g_gate, g_up


def hidden_body(
    chunk, block, x_h, c_h, wg_h, wu_h, wd_h, og_h, ou_h, od_h, xs, cs, wg, wu, wd, acc, in_sem, w_sem, out_sem
):
    rows = x_h.shape[0]
    steps, blocks, held = rows // chunk, wg.shape[0] // block, xs.shape[0] // chunk
    loads = [
        pltpu.make_async_copy(src, dst, w_sem.at[j])
        for j, (src, dst) in enumerate(((wg_h, wg), (wu_h, wu), (wd_h, wd)))
    ]

    def tokens(i):
        src = pl.ds(pl.multiple_of(i * chunk, chunk), chunk)
        dst = pl.ds(pl.multiple_of(i % held * chunk, chunk), chunk)
        return [
            pltpu.make_async_copy(x_h.at[src], xs.at[dst], in_sem.at[i % held, 0]),
            pltpu.make_async_copy(c_h.at[src], cs.at[dst], in_sem.at[i % held, 1]),
        ]

    def results(b, slot):
        at = pl.ds(pl.multiple_of(b * block, 16), block)
        return [
            pltpu.make_async_copy(acc.at[slot, j], out.at[at], out_sem.at[slot, j])
            for j, out in enumerate((og_h, ou_h, od_h))
        ]

    resident = held == steps
    for copy in tokens(0) + loads:
        copy.start()
    for i in range(1, held if resident else 1):
        for copy in tokens(i):
            copy.start()
    for copy in loads:
        copy.wait()
    slots = acc.shape[0]

    @pl.loop(0, blocks)
    def _(b):
        slot = b % slots
        at = pl.ds(pl.multiple_of(b * block, 16), block)

        @pl.when(b >= slots)
        def _():
            for copy in results(b - slots, slot):
                copy.wait()

        @pl.loop(0, steps)
        def _(i):
            if resident:

                @pl.when(b == 0)
                def _():
                    for copy in tokens(i):
                        copy.wait()

            else:
                for copy in tokens(i):
                    copy.wait()

                @pl.when((i + 1 < steps) | (b + 1 < blocks))
                def _():
                    for copy in tokens(lax.rem(i + 1, steps)):
                        copy.start()

            t = pl.ds(pl.multiple_of(i % held * chunk, chunk), chunk)
            x, cot = xs[t], cs[t]
            act, g_gate, g_up = hidden_units(x, cot, wg[at], wu[at], wd[at])

            @pl.when(i == 0)
            def _():
                acc[slot, 0] = plain_dot(g_gate, x)
                acc[slot, 1] = plain_dot(g_up, x)
                acc[slot, 2] = plain_dot(act, cot)

            @pl.when(i > 0)
            def _():
                acc[slot, 0] += plain_dot(g_gate, x)
                acc[slot, 1] += plain_dot(g_up, x)
                acc[slot, 2] += plain_dot(act, cot)

        for copy in results(b, slot):
            copy.start()

    for b in range(max(0, blocks - slots), blocks):
        for copy in results(b, b % slots):
            copy.wait()


def hidden_grads(x, cot, wg, wu, wd):
    rows, width = x.shape
    units = wg.shape[0]
    chunk = math.gcd(rows, 1024)
    block = units // 2
    held = min(rows // chunk, 4)
    any_spec = pl.BlockSpec(memory_space=pl.ANY)
    dma = pltpu.SemaphoreType.DMA
    return pl.pallas_call(
        functools.partial(hidden_body, chunk, block),
        out_shape=(jax.ShapeDtypeStruct((units, width), f32),) * 3,
        in_specs=[any_spec] * 5,
        out_specs=(any_spec,) * 3,
        scratch_shapes=[pltpu.VMEM((held * chunk, width), bf16)] * 2
        + [pltpu.VMEM((units, width), bf16)] * 3
        + [pltpu.VMEM((2, 3, block, width), f32), dma((held, 2)), dma((3,)), dma((2, 3))],
        compiler_params=pltpu.CompilerParams(vmem_limit_bytes=60 << 20),
        cost_estimate=pl.CostEstimate(
            flops=12 * rows * width * units, bytes_accessed=4 * rows * width + 18 * units * width, transcendentals=0
        ),
        name="hidden_grads",
    )(x, cot, wg, wu, wd)


def shards(
    layer_input,
    seq_ids,
    positions,
    norm_gain,
    w_query,
    b_query,
    w_key,
    b_key,
    w_value,
    b_value,
    w_output,
    mlp_gain,
    w_gate,
    w_up,
    w_down,
    cotangent,
):
    tok = layer_input.shape[1]
    width = layer_input.shape[2]
    group = H // KV
    query_width = H * HD
    key_width = KV * HD
    score_scale = HD ** (-0.5)
    ctx = lax.axis_size("ctx")
    fsdp = lax.axis_size("fsdp")
    depth = width // fsdp
    lines = ctx // 2
    c, f = lax.axis_index("ctx"), lax.axis_index("fsdp")
    seq_length = ctx * tok
    dma = pltpu.SemaphoreType.DMA
    sds = jax.ShapeDtypeStruct
    input_rows = layer_input[0]
    grad_out = cotangent[0]
    own_segment = seq_ids[0]
    own_positions = positions[0]
    query_rows = c * tok + jnp.arange(tok, dtype=jnp.int32)

    cot_all = lax.all_gather(grad_out, ("ctx", "fsdp"), axis=0, tiled=True)

    def padded(v):
        return jnp.pad(v, (0, 256 - v.shape[0]))

    small = jnp.stack([padded(v) for v in (norm_gain, mlp_gain, b_query, b_key, b_value)])
    small = jnp.pad(small, ((0, 11), (0, 0)))
    seg_tile = jnp.broadcast_to(own_segment[None], (8, tok))
    w_project, wo_full, small_all, seg_all = comm_call(
        functools.partial(front_body, ctx, depth),
        (
            sds((width, query_width + 2 * key_width), bf16),
            sds((query_width, width), bf16),
            sds((fsdp, 16, 256), bf16),
            sds((ctx, 8, tok), jnp.int32),
        ),
        gather_sems(4) + [dma((3,)), dma((3,)), dma((ctx - 1,)), dma((ctx - 1,))],
        0,
    )(w_query, w_key, w_value, w_output, small, seg_tile)
    all_segments = seg_all[:, 0].reshape(seq_length)
    small_all = small_all.astype(f32)
    gain_first = small_all[:, 0, :depth].reshape(width)
    gain_second = small_all[:, 1, :depth].reshape(width)
    kd = key_width // fsdp
    b_project = jnp.concatenate(
        [
            small_all[:, 2, :depth].reshape(query_width),
            small_all[:, 3, :kd].reshape(key_width),
            small_all[:, 4, :kd].reshape(key_width),
        ]
    )
    residual_in = input_rows.astype(f32)
    inverse_first = lax.rsqrt(jnp.mean(residual_in * residual_in, -1, keepdims=True) + EPSILON)
    normed_first = (residual_in * inverse_first * gain_first).astype(bf16)
    projected = jnp.dot(normed_first, w_project, preferred_element_type=f32) + b_project
    cosine, sine_table = rope_tables(own_positions, HD)
    query = rotate(projected[:, :query_width].reshape(tok, H, HD), cosine, sine_table)
    query = query.astype(bf16).reshape(tok, KV, group, HD)
    key_rot = rotate(
        projected[:, query_width : query_width + key_width].reshape(tok, KV, HD), cosine, sine_table
    )
    value_low = projected[:, query_width + key_width :].astype(bf16)
    key_value = jnp.concatenate([key_rot.astype(bf16).reshape(tok, key_width), value_low], 1)
    kv_all = comm_call(
        functools.partial(kv_body, lines), sds((ctx, tok, 2 * key_width), bf16), [dma((2, lines)), dma((2, lines))], 1
    )(key_value).reshape(seq_length, 2 * key_width)
    keys = kv_all[:, :key_width].reshape(seq_length, KV, HD)
    values = kv_all[:, key_width:].reshape(seq_length, KV, HD)
    key_rows = jnp.arange(seq_length, dtype=jnp.int32)
    allowed = (key_rows[None, :] <= query_rows[:, None]) & (all_segments[None, :] == own_segment[:, None])
    raw_scores = jnp.einsum("tkgd,nkd->kgtn", query, keys, preferred_element_type=f32) * score_scale
    highest = jnp.max(jnp.where(allowed, raw_scores, MASK_FILL), -1)
    exp_scores = jnp.where(allowed, jnp.exp(raw_scores - highest[..., None]), 0.0)
    running_sum = jnp.sum(exp_scores, -1)
    accumulated = jnp.einsum("kgtn,nkd->tkgd", exp_scores.astype(bf16), values, preferred_element_type=f32)
    log_total = highest + jnp.log(running_sum)
    attention = accumulated / jnp.transpose(running_sum, (2, 0, 1))[..., None]
    attention_low = attention.reshape(tok, query_width).astype(bf16)
    hidden_state = residual_in + jnp.dot(attention_low, wo_full, preferred_element_type=f32)
    inverse_second = lax.rsqrt(jnp.mean(hidden_state * hidden_state, -1, keepdims=True) + EPSILON)
    normed_second = (hidden_state * inverse_second * gain_second).astype(bf16)
    x_all = lax.all_gather(normed_second, ("ctx", "fsdp"), axis=0, tiled=True)
    x_group = comm_call(
        ag_body, sds((fsdp, tok, width), bf16), gather_sems(1), 2
    )(normed_second).reshape(fsdp * tok, width)
    cot_group = lax.dynamic_slice_in_dim(cot_all, c * fsdp * tok, fsdp * tok, 0)

    def ffn(x, cot):
        gate = jnp.dot(x, w_gate, preferred_element_type=f32)
        up = jnp.dot(x, w_up, preferred_element_type=f32)
        g_act = lax.dot_general(cot, w_down, (((1,), (1,)), ((), ())), preferred_element_type=f32)
        sg = jax.nn.sigmoid(gate)
        act = (gate * sg * up).astype(bf16)
        g_gate = (g_act * up * sg * (1.0 + gate * (1.0 - sg))).astype(bf16)
        g_up = (g_act * gate * sg).astype(bf16)
        return act, g_gate, g_up

    act, g_gate, g_up = ffn(x_group, cot_group)
    g_normed_part = (over_last(g_gate, w_gate) + over_last(g_up, w_up)).astype(bf16)
    grad_normed2 = comm_call(
        rs_body,
        sds((tok, width), f32),
        [
            pltpu.VMEM((2, tok, width), bf16),
            pltpu.VMEM((tok, width), bf16),
            pltpu.VMEM((tok, width), bf16),
            dma((3,)),
            dma((3,)),
        ],
        3,
    )(g_normed_part.reshape(fsdp, tok, width))
    down_part = jnp.dot(act, w_down, preferred_element_type=f32).astype(bf16)
    down_out = lax.psum_scatter(down_part, "fsdp", scatter_dimension=0, tiled=True).astype(f32)
    block_out = (hidden_state + down_out).astype(bf16)[None]

    hidden_back, second_gain_grad = norm_back(hidden_state, inverse_second, gain_second, grad_normed2)
    grad_hidden = grad_out.astype(f32) + hidden_back
    grad_hidden_low = grad_hidden.astype(bf16)
    grad_attention = over_last(grad_hidden_low, wo_full).astype(bf16)
    grad_attention = grad_attention.reshape(tok, KV, group, HD)
    delta_rows = jnp.einsum("tkgd,tkgd->kgt", grad_attention.astype(f32), attention)
    probs = jnp.where(allowed, jnp.exp(raw_scores - log_total[..., None]), 0.0)
    grad_values = jnp.einsum("kgtn,tkgd->nkd", probs.astype(bf16), grad_attention, preferred_element_type=f32)
    grad_probs = jnp.einsum("tkgd,nkd->kgtn", grad_attention, values, preferred_element_type=f32)
    grad_scores = (probs * (grad_probs - delta_rows[..., None])).astype(bf16)
    grad_query = jnp.einsum("kgtn,nkd->tkgd", grad_scores, keys, preferred_element_type=f32) * score_scale
    grad_keys = jnp.einsum("kgtn,tkgd->nkd", grad_scores, query, preferred_element_type=f32) * score_scale
    grad_pairs = jnp.concatenate(
        [grad_keys.reshape(seq_length, key_width), grad_values.reshape(seq_length, key_width)], 1
    ).astype(bf16)
    slices = jnp.concatenate(
        [
            normed_first.reshape(tok, fsdp, depth).transpose(1, 0, 2),
            attention_low.reshape(tok, fsdp, depth).transpose(1, 0, 2),
        ],
        1,
    )
    grad_pairs, ghl_group, slice_group = comm_call(
        functools.partial(dkv_body, ctx),
        (
            sds((tok, 2 * key_width), f32),
            sds((fsdp, tok, width), bf16),
            sds((fsdp, 2 * tok, depth), bf16),
        ),
        [pltpu.VMEM((ctx - 1, tok, 2 * key_width), bf16), dma((ctx - 1,)), dma((ctx - 1,))]
        + gather_sems(1)
        + [dma((3,)), dma((3,))],
        4,
    )(grad_pairs.reshape(ctx, tok, 2 * key_width), grad_hidden_low, slices)
    grad_q_pre = (
        rotate_back(grad_query.reshape(tok, H, HD), cosine, sine_table).reshape(tok, query_width).astype(bf16)
    )
    grad_k_pre = (
        rotate_back(grad_pairs[:, :key_width].reshape(tok, KV, HD), cosine, sine_table)
        .reshape(tok, key_width)
        .astype(bf16)
    )
    grad_v_pre = grad_pairs[:, key_width:].astype(bf16)
    grad_project = jnp.concatenate([grad_q_pre, grad_k_pre, grad_v_pre], 1)
    grad_normed1 = over_last(grad_project, w_project)
    bias_grad = jnp.sum(grad_project.astype(f32), 0)
    input_back, first_gain_grad = norm_back(residual_in, inverse_first, gain_first, grad_normed1)
    input_grad = (grad_hidden + input_back).astype(bf16)[None]
    vectors = jnp.concatenate([first_gain_grad, second_gain_grad, bias_grad])
    vectors = jnp.pad(vectors, (0, 3072 - vectors.shape[0])).reshape(8, 384)
    gp_group, vectors = comm_call(
        project_body,
        (sds((fsdp, tok, grad_project.shape[1]), bf16), sds(vectors.shape, f32)),
        gather_sems(1) + [pltpu.VMEM((3,) + vectors.shape, f32), dma((3,)), dma((3,))],
        5,
    )(grad_project, vectors)
    gp_group = gp_group.reshape(fsdp * tok, grad_project.shape[1])
    vectors = vectors.reshape(3072)
    normed_slice = slice_group[:, :tok].reshape(fsdp * tok, depth)
    attention_slice = slice_group[:, tok:].reshape(fsdp * tok, depth)
    project_grad = over_first(normed_slice, gp_group)
    output_grad = over_first(attention_slice, ghl_group.reshape(fsdp * tok, width))

    def piece(start, size):
        share = size // fsdp
        return lax.dynamic_slice_in_dim(vectors, start + f * share, share, 0)

    columns = project_grad.shape[1] + width
    starts = ((0, width), (width, width), (2 * width, query_width), (2 * width + query_width, key_width),
              (2 * width + query_width + key_width, key_width))
    own = jnp.concatenate([piece(*at) for at in starts])
    own = jnp.pad(own, (0, columns - own.shape[0]))
    weight_grads = jnp.concatenate(
        [jnp.concatenate([project_grad, output_grad], 1), jnp.broadcast_to(own[None], (16, columns))], 0
    ).astype(bf16)
    weight_grads = lax.psum(weight_grads, "ctx")
    weight_grads = weight_grads.astype(f32)
    own = weight_grads[depth]
    weight_grads = weight_grads[:depth]
    ends = [0]
    for _, size in starts:
        ends.append(ends[-1] + size // fsdp)
    own = [own[ends[i] : ends[i + 1]] for i in range(5)]

    gate_grad, up_grad, down_grad = hidden_grads(x_all, cot_all, w_gate.T, w_up.T, w_down)
    return (
        block_out,
        input_grad,
        own[0],
        weight_grads[:, :query_width],
        own[2],
        weight_grads[:, query_width : query_width + key_width],
        own[3],
        weight_grads[:, query_width + key_width : query_width + 2 * key_width],
        own[4],
        weight_grads[:, query_width + 2 * key_width :],
        own[1],
        gate_grad.T,
        up_grad.T,
        down_grad,
        log_total.reshape(H, tok)[None],
    )


def solution(mesh):
    in_specs = (
        P("fsdp", "ctx", None),
        P("fsdp", "ctx"),
        P("fsdp", "ctx"),
        P("fsdp"),
        P("fsdp", None),
        P("fsdp"),
        P("fsdp", None),
        P("fsdp"),
        P("fsdp", None),
        P("fsdp"),
        P("fsdp", None),
        P("fsdp"),
        P(None, "fsdp"),
        P(None, "fsdp"),
        P("fsdp", None),
        P("fsdp", "ctx", None),
    )
    out_specs = (
        P("fsdp", "ctx", None),
        P("fsdp", "ctx", None),
        P("fsdp"),
        P("fsdp", None),
        P("fsdp"),
        P("fsdp", None),
        P("fsdp"),
        P("fsdp", None),
        P("fsdp"),
        P("fsdp", None),
        P("fsdp"),
        P(None, "fsdp"),
        P(None, "fsdp"),
        P("fsdp", None),
        P("fsdp", None, "ctx"),
    )
    return jax.shard_map(shards, mesh=mesh, in_specs=in_specs, out_specs=out_specs, check_vma=False)
```

profile of v0, /device:TPU:0, one launch (start us, length us, event | category | flops | bytes accessed | tf_op | source)
XLA Modules:
  0.0 289.0 jit_solution(14165135327757693257)
XLA Ops:
  8.1 0.7 all-gather.6.cloned.1.call-update
  8.8 0.7 pad.29
  9.5 0.7 pad.30
  10.1 0.7 pad.31
  10.8 0.7 pad.32
  12.8 1.0 copy-done.7
  13.8 1.0 copy-done.8
  14.8 0.8 copy-done.9
  15.6 0.8 copy-done.10
  16.5 26.2 %shard_map.271 = (bf16[896,1152]{1,0:T(8,128)(2,1)S(1)}, bf16[896,896]{1,0:T(8,128)(2,1)S(1)}, bf16[4,16,256]{2,1,0:T(8,128)(2,1)S(1)}, s32[8,8,128]{2,1,0:T(8,128)S(1)}) custom-call(bf16[224,896]{1,0:T(8,128)(2,1)S(1)} %copy-done.7, bf16[224,128]{1,0:T(8,128)(2,1)S(1)} %copy-done.9, bf16[224,128]{1,0:T(8,128)(2,1)S(1)} %copy-done.10, ...), custom_call_target="tpu_custom_call" | custom-call | tf_op jit(solution)/shard_map/pallas_call | solution.py:151
  42.6 1.1 copy-done
  44.2 1.1 fusion.38
  45.3 1.5 convolution_add_fusion
  47.3 16.5 %shard_map.272 = bf16[8,128,256]{2,1,0:T(8,128)(2,1)S(1)} custom-call(bf16[128,256]{1,0:T(8,128)(2,1)S(1)} %pad_maximum_fusion.8.kv), custom_call_target="tpu_custom_call" | custom-call | tf_op jit(solution)/shard_map/pallas_call | solution.py:151
  63.9 0.7 fusion.61
  65.0 1.8 copy.50
  67.2 1.2 fusion.2
  68.4 1.5 fusion.8
  70.0 1.4 copy-done.11
  71.4 2.3 fusion.64
  74.2 0.8 multiply_convert_fusion.7.x
  75.2 0.9 copy-done.3
  76.1 10.9 %shard_map.273 = bf16[4,128,896]{2,1,0:T(8,128)(2,1)S(1)} custom-call(bf16[128,896]{1,0:T(8,128)(2,1)S(1)} %copy-done.3), custom_call_target="tpu_custom_call" | custom-call | tf_op jit(solution)/shard_map/pallas_call | solution.py:151
  87.0 3.3 %fusion.65 = f32[512,1216]{0,1:T(8,128)S(1)} fusion(bf16[512,896]{1,0:T(8,128)(2,1)S(1)} %bitcast.191, bf16[896,1216]{0,1:T(8,128)(2,1)} %param.28), kind=kOutput, calls=%fused_computation.130 | convolution fusion | flops 1115684864 | bytes 5586944 | tf_op jit(solution)/shard_map/dot_general | solution.py:545
  90.3 1.5 fusion.66
  91.8 1.4 copy-done.47
  93.3 2.5 convolution_convert_fusion
  96.2 0.9 copy.62
  98.5 0.8 fusion.39
  99.3 1.0 pad_maximum_fusion.2.sl
  100.4 3.7 %fusion.33 = f32[512,1216]{0,1:T(8,128)S(1)} fusion(bf16[1216,896]{1,0:T(8,128)(2,1)} %wd_h.1, bf16[1,4096,896]{2,1,0:T(8,128)(2,1)} %all-gather.6.cloned.1.call-done, s32[]{:T(128)S(6)} %select_n.30), kind=kOutput, calls=%fused_computation.41 | convolution fusion | flops 1115684864 | bytes 5586948 | tf_op jit(solution)/shard_map/dot_general | solution.py:547
  104.1 3.9 %fusion.18 = f32[512,896]{1,0:T(8,128)S(1)} fusion(bf16[896,1216]{0,1:T(8,128)(2,1)S(1)} %copy-done.40, f32[512,1216]{0,1:T(8,128)S(1)} %copy-done.46, f32[512,1216]{0,1:T(8,128)S(1)} %fusion.33, f32[512,1216]{0,1:T(8,128)} %copy-done.47), kind=kOutput, calls=%fused_computation.29 | convolution fusion | flops 1121910784 | bytes 11485184 | tf_op jit(solution)/shard_map/dot_general | solution.py:307
  108.0 1.6 add_convert_fusion
  109.7 14.3 %shard_map.274 = f32[128,896]{1,0:T(8,128)S(1)} custom-call(bf16[4,128,896]{2,1,0:T(8,128)(2,1)S(1)} %bitcast.190), custom_call_target="tpu_custom_call" | custom-call | tf_op jit(solution)/shard_map/pallas_call | solution.py:151
  124.0 0.7 multiply_reduce_fusion
  124.8 1.2 fusion.57.ghl
  126.0 1.3 convolution_convert_fusion.1
  127.3 1.8 copy.54
  129.1 1.2 fusion.37
  130.3 5.6 %fusion.1 = bf16[2,7,128,1024]{2,3,1,0:T(8,128)(2,1)S(1)} fusion(f32[2,1024,128,7]{2,1,3,0:T(8,128)} %copy-done.11, f32[2,7,128]{2,1,0:T(8,128)S(1)} %fusion.37, f32[2,7,128]{2,1,0:T(8,128)S(1)} %log_add_fusion, pred[128,1024]{0,1:T(8,128)(4,1)S(1)} %copy-done.20, bf16[1024,2,64,1]{0,2,3,1:T(8,128)(2,1)} %bitcast.212, bf16[128,2,7,64]{0,3,2,1:T(8,128)(2,1)} %bitcast.208), kind=kOutput, calls=%fused_computation.2 | convolution fusion | flops 245891072 | bytes 11646976 | tf_op jit(solution)/shard_map/tkgd,nkd->kgtn/dot_general | solution.py:580
  136.0 1.5 convolution_multiply_fusion
  137.5 1.3 fusion.29
  138.8 5.3 %fusion.26 = bf16[2,64,1024]{2,1,0:T(8,128)(2,1)} fusion(bf16[128,2,7,64]{0,3,2,1:T(8,128)(2,1)S(1)} %bitcast.209, f32[2,1024,128,7]{2,1,3,0:T(8,128)} %copy-done.11, f32[2,7,128]{2,1,0:T(8,128)S(1)} %log_add_fusion, pred[128,1024]{0,1:T(8,128)(4,1)S(1)} %copy-done.20), kind=kOutput, calls=%fused_computation.36 | convolution fusion | flops 242352128 | bytes 7969792 | tf_op jit(solution)/shard_map/kgtn,tkgd->nkd/dot_general | solution.py:579
  144.0 0.8 copy.89
  144.8 1.8 copy.58
  146.6 1.7 copy.90
  148.3 1.8 copy.59
  150.1 1.1 pad_maximum_fusion.1.part
  151.3 19.2 %shard_map.275 = (f32[128,256]{1,0:T(8,128)S(1)}, bf16[4,128,896]{2,1,0:T(8,128)(2,1)S(1)}, bf16[4,256,224]{2,1,0:T(8,128)(2,1)S(1)}) custom-call(bf16[8,128,256]{2,1,0:T(8,128)(2,1)S(1)} %pad_maximum_fusion.1.part, bf16[128,896]{1,0:T(8,128)(2,1)S(1)} %fusion.57.ghl, bf16[4,256,224]{2,1,0:T(8,128)(2,1)S(1)} %pad_maximum_fusion.2.sl), custom_call_target="tpu_custom_call" | custom-call | tf_op jit(solution)/shard_map/pallas_call | solution.py:151
  170.6 0.9 copy-done.4
  171.5 0.8 copy-done.5
  173.7 0.8 copy.64
  174.6 0.7 pad_maximum_fusion.10
  175.4 1.0 convert_reduce_fusion
  176.7 2.5 multiply_reduce_fusion.1
  179.2 10.8 %shard_map.276 = (bf16[4,128,1152]{2,1,0:T(8,128)(2,1)S(1)}, f32[8,384]{1,0:T(8,128)S(1)}) custom-call(bf16[128,1152]{1,0:T(8,128)(2,1)S(1)} %get-tuple-element.64.x, f32[8,384]{1,0:T(8,128)S(1)} %reshape.251.vec), custom_call_target="tpu_custom_call" | custom-call | tf_op jit(solution)/shard_map/pallas_call | solution.py:151
  190.3 1.6 fusion.17
  192.4 1.1 pad_maximum_fusion
  193.6 77.6 %hidden_grads.1 = (f32[1216,896]{1,0:T(8,128)}, f32[1216,896]{1,0:T(8,128)}, f32[1216,896]{1,0:T(8,128)}) custom-call(bf16[4096,896]{1,0:T(8,128)(2,1)} %all-gather.4.cloned.1.call-done.x_h, bf16[4096,896]{1,0:T(8,128)(2,1)} %bitcast.227, bf16[1216,896]{1,0:T(8,128)(2,1)} %bitcast.228, bf16[1216,896]{1,0:T(8,128)(2,1)} %bitcast.229, bf16[1216,896]{1,0:T(8,128)(2,1)} %wd_h.1), custom_call_target="tpu_custom_call" | custom-call | flops 53552873472 | bytes 34291712 | tf_op jit(solution)/shard_map/hidden_grads/pallas_call | solution.py:423
  271.3 1.9 fusion.43
  273.3 3.9 %all-reduce.10.cloned.1.call-done = bf16[240,2048]{1,0:T(8,128)(2,1)} async-done(((bf16[240,2048]{1,0:T(8,128)(2,1)}), bf16[240,2048]{1,0:T(8,128)(2,1)}) %all-reduce.10.cloned.1.call-update) | async-done | bytes 983056 | tf_op jit(solution)/shard_map/psum | solution.py:647
  277.1 1.5 convert_element_type.157
  279.2 1.3 fusion.59
  280.5 0.7 fusion.60
  (160 shorter events, 9.5 us)
Async XLA Ops:
  8.0 92.3 %all-gather.6.cloned.1.call-start = ((), (), s32[]{:S(2)}) async-start(), calls=%async_computation.4 | async-start | bytes 7569408 | tf_op jit(solution)/shard_map/all_gather | solution.py:477
  8.7 184.8 %all-gather.4.cloned.1.call-start = ((), (), s32[]{:S(2)}) async-start(), calls=%async_computation.3 | async-start | bytes 7569408 | tf_op jit(solution)/shard_map/all_gather | solution.py:538
  12.8 1.0 copy-start.7
  13.8 1.0 copy-start.8
  14.8 0.8 copy-start.9
  15.6 0.8 copy-start.10
  42.6 1.2 copy-start
  43.8 3.2 %copy-start.44 = (s32[1,128]{1,0:T(1,128)S(1)}, s32[1,128]{1,0:T(1,128)}, u32[]{:S(2)}) copy-start(s32[1,128]{1,0:T(1,128)} %param.18) | copy-start | bytes 1540
  45.3 18.6 %copy-start.35 = (f32[128]{0:T(128)}, f32[128]{0:T(128)S(1)}, u32[]{:S(2)}) copy-start(f32[128]{0:T(128)S(1)} %add_rsqrt_fusion.1) | copy-start | bytes 1540
  46.8 20.0 %copy-start.37 = (s32[1,128]{1,0:T(1,128)S(1)}, s32[1,128]{1,0:T(1,128)}, u32[]{:S(2)}) copy-start(s32[1,128]{1,0:T(1,128)} %param.17) | copy-start | bytes 1540
  64.8 3.6 %copy-start.17 = (bf16[1024,128]{0,1:T(8,128)(2,1)}, bf16[1024,128]{0,1:T(8,128)(2,1)S(1)}, u32[]{:S(2)}) copy-start(bf16[1024,128]{0,1:T(8,128)(2,1)S(1)} %copy.51) | copy-start | bytes 786436
  67.1 2.9 copy-start.19
  67.2 1.2 copy-start.25
  67.2 1.2 copy-start.27
  68.4 3.0 %copy-start.11 = (f32[2,1024,128,7]{2,1,3,0:T(8,128)}, f32[2,1024,128,7]{2,1,3,0:T(8,128)S(1)}, u32[]{:S(2)}) copy-start(f32[2,1024,128,7]{2,1,3,0:T(8,128)S(1)} %get-tuple-element.94) | copy-start | bytes 22020100
  68.4 3.0 %copy-start.30 = (bf16[1024,128]{0,1:T(8,128)(2,1)S(1)}, bf16[1024,128]{0,1:T(8,128)(2,1)}, u32[]{:S(2)}) copy-start(bf16[1024,128]{0,1:T(8,128)(2,1)} %copy.50) | copy-start | bytes 786436
  71.4 2.3 copy-start.1
  71.4 2.3 copy-start.14
  74.2 49.8 %copy-start.12 = (f32[128,896]{1,0:T(8,128)}, f32[128,896]{1,0:T(8,128)S(1)}, u32[]{:S(2)}) copy-start(f32[128,896]{1,0:T(8,128)S(1)} %get-tuple-element.98) | copy-start | bytes 1376260
  74.2 16.0 %copy-start.32 = (f32[128]{0:T(128)}, f32[128]{0:T(128)S(1)}, u32[]{:S(2)}) copy-start(f32[128]{0:T(128)S(1)} %add_rsqrt_fusion) | copy-start | bytes 1540
  75.1 196.2 %reduce-scatter.2.cloned.1.call-start = ((), (), s32[]{:S(2)}) async-start(), calls=%async_computation.1 | async-start | bytes 1146880 | tf_op jit(solution)/shard_map/reduce_scatter | solution.py:569
  75.1 0.9 copy-start.3
  87.0 3.3 %copy-start.42 = (bf16[896,1216]{0,1:T(8,128)(2,1)S(1)}, bf16[896,1216]{0,1:T(8,128)(2,1)}, u32[]{:S(2)}) copy-start(bf16[896,1216]{0,1:T(8,128)(2,1)} %param.29) | copy-start | bytes 6537220
  90.3 1.5 copy-start.45
  90.3 3.0 %copy-start.41 = (bf16[1216,896]{1,0:T(8,128)(2,1)S(1)}, bf16[1216,896]{1,0:T(8,128)(2,1)}, u32[]{:S(2)}) copy-start(bf16[1216,896]{1,0:T(8,128)(2,1)} %wd_h.1) | copy-start | bytes 6537220
  91.8 1.5 copy-start.47
  95.8 181.3 %all-reduce.10.cloned.1.call-start = ((), (), s32[]{:S(2)}) async-start(), calls=%async_computation.2 | async-start | bytes 1966080 | tf_op jit(solution)/shard_map/psum | solution.py:647
  100.4 3.7 %copy-start.40 = (bf16[896,1216]{0,1:T(8,128)(2,1)S(1)}, bf16[896,1216]{0,1:T(8,128)(2,1)}, u32[]{:S(2)}) copy-start(bf16[896,1216]{0,1:T(8,128)(2,1)} %param.28) | copy-start | bytes 6537220
  100.4 3.7 %copy-start.46 = (f32[512,1216]{0,1:T(8,128)S(1)}, f32[512,1216]{0,1:T(8,128)}, u32[]{:S(2)}) copy-start(f32[512,1216]{0,1:T(8,128)} %copy-done.45) | copy-start | bytes 7471108
  104.1 3.9 %copy-start.43 = (bf16[896,1216]{0,1:T(8,128)(2,1)S(1)}, bf16[896,1216]{0,1:T(8,128)(2,1)}, u32[]{:S(2)}) copy-start(bf16[896,1216]{0,1:T(8,128)(2,1)} %param.29) | copy-start | bytes 6537220
  108.0 16.0 %copy-start.33 = (f32[128]{0:T(128)S(1)}, f32[128]{0:T(128)}, u32[]{:S(2)}) copy-start(f32[128]{0:T(128)} %copy-done.32) | copy-start | bytes 1540
  108.0 16.8 %copy-start.21 = (bf16[1,128,896]{2,1,0:T(8,128)(2,1)S(1)}, bf16[1,128,896]{2,1,0:T(8,128)(2,1)}, u32[]{:S(2)}) copy-start(bf16[1,128,896]{2,1,0:T(8,128)(2,1)} %param.31) | copy-start | bytes 688132
  109.7 16.4 %copy-start.2 = (bf16[896,896]{1,0:T(8,128)(2,1)S(1)}, bf16[896,896]{1,0:T(8,128)(2,1)}, u32[]{:S(2)}) copy-start(bf16[896,896]{1,0:T(8,128)(2,1)} %copy-done) | copy-start | bytes 4816900
  124.8 5.5 %copy-start.20 = (pred[128,1024]{0,1:T(8,128)(4,1)S(1)}, pred[128,1024]{0,1:T(8,128)(4,1)}, u32[]{:S(2)}) copy-start(pred[128,1024]{0,1:T(8,128)(4,1)} %copy-done.19) | copy-start | bytes 393220
  124.8 4.3 %copy-start.38 = (f32[128]{0:T(128)}, f32[128]{0:T(128)S(1)}, u32[]{:S(2)}) copy-start(f32[128]{0:T(128)S(1)} %broadcast_multiply_fusion.1) | copy-start | bytes 1540
  130.3 5.7 %copy-start.18 = (bf16[1024,128]{0,1:T(8,128)(2,1)S(1)}, bf16[1024,128]{0,1:T(8,128)(2,1)}, u32[]{:S(2)}) copy-start(bf16[1024,128]{0,1:T(8,128)(2,1)} %copy-done.17) | copy-start | bytes 786436
  136.0 1.5 copy-start.26
  136.0 1.5 copy-start.28
  137.5 1.3 copy-start.29
  150.1 22.8 %copy-start.23 = (f32[2,64,7,128]{3,1,2,0:T(8,128)S(1)}, f32[2,64,7,128]{3,1,2,0:T(8,128)}, u32[]{:S(2)}) copy-start(f32[2,64,7,128]{3,1,2,0:T(8,128)} %convolution_multiply_fusion) | copy-start | bytes 1376260
  150.1 26.5 %copy-start.36 = (f32[128]{0:T(128)S(1)}, f32[128]{0:T(128)}, u32[]{:S(2)}) copy-start(f32[128]{0:T(128)} %copy-done.35) | copy-start | bytes 1540
  170.5 0.9 copy-start.4
  171.5 0.8 copy-start.5
  173.0 6.2 %copy-start.31 = (f32[896]{0:T(1024)S(1)}, f32[896]{0:T(1024)}, u32[]{:S(2)}) copy-start(f32[896]{0:T(1024)} %get-tuple-element.54) | copy-start | bytes 10756
  173.7 16.6 %copy-start.6 = (bf16[4,256,224]{2,1,0:T(8,128)(2,1)S(1)}, bf16[4,256,224]{2,1,0:T(8,128)(2,1)}, u32[]{:S(2)}) copy-start(bf16[4,256,224]{2,1,0:T(8,128)(2,1)} %copy-done.5) | copy-start | bytes 1376260
  193.5 77.8 %copy-start.13 = (f32[128,896]{1,0:T(8,128)S(1)}, f32[128,896]{1,0:T(8,128)}, u32[]{:S(2)}) copy-start(f32[128,896]{1,0:T(8,128)} %copy-done.12) | copy-start | bytes 1376260
  193.5 77.7 %copy-start.15 = (bf16[1,128,896]{2,1,0:T(8,128)(2,1)S(1)}, bf16[1,128,896]{2,1,0:T(8,128)(2,1)}, u32[]{:S(2)}) copy-start(bf16[1,128,896]{2,1,0:T(8,128)(2,1)} %param.16) | copy-start | bytes 688132
  193.5 77.7 %copy-start.22 = (bf16[1,128,896]{2,1,0:T(8,128)(2,1)S(1)}, bf16[1,128,896]{2,1,0:T(8,128)(2,1)}, u32[]{:S(2)}) copy-start(bf16[1,128,896]{2,1,0:T(8,128)(2,1)} %param.31) | copy-start | bytes 688132
  193.6 77.7 %copy-start.24 = (f32[128,896]{1,0:T(8,128)S(1)}, f32[128,896]{1,0:T(8,128)}, u32[]{:S(2)}) copy-start(f32[128,896]{1,0:T(8,128)} %get-tuple-element.99) | copy-start | bytes 1376260
  193.6 77.7 %copy-start.34 = (f32[128]{0:T(128)S(1)}, f32[128]{0:T(128)}, u32[]{:S(2)}) copy-start(f32[128]{0:T(128)} %copy-done.32) | copy-start | bytes 1540
  193.6 77.7 %copy-start.39 = (f32[128]{0:T(128)S(1)}, f32[128]{0:T(128)}, u32[]{:S(2)}) copy-start(f32[128]{0:T(128)} %copy-done.38) | copy-start | bytes 1540
  277.1 2.1 copy-start.16
Sparse Core Ops, SparseCore 0:
  11.7 83.8 all-gather.5
  99.1 79.7 all-gather.3
  193.6 83.4 all-reduce.9
Sparse Core Ops, SparseCore 1:
  95.9 29.0 reduce-scatter.1
where the time goes:
time: 292 us; the launch traced here: 289 us
  Pallas kernels  176 us (60%)
  matrix products  41.5 us (14%)
  local copies, waits for them, and re-layouts  33.7 us (12%)
  other arithmetic  17.1 us (6%)
  between operations  16.1 us (6%)
  waiting for transfers between devices  4.68 us (2%)
    pallas_call x6, Pallas kernels, call(): pl.pallas_call(body, out_shape=out_shape, in_specs=[VMEM] * len(args), ou...  97.9 us
    pallas_call x1, Pallas kernels, hidden_grads(): pl.pallas_call(functools.partial(hidden_body, chunk, block), out_shape=(j...  77.6 us
    unnamed x99, local copies, waits for them, and re-layouts  13.8 us
    dot_general x4, matrix products, over_last(): lax.dot_general(a, b, (((1,), (1,)), ((), ())), preferred_element_type=f32)  9.26 us
  transfers between devices with their start and end apart: 4, of which 1 were waited for; matrix products, arithmetic and copies ran while one was open for 27% of the time, Pallas kernels for 61%

commit v1 on v0

--- a/solution.py
+++ b/solution.py
@@ -7,6 +7,7 @@
 from jax.experimental import pallas as pl
 from jax.experimental.pallas import tpu as pltpu
 from jax.sharding import PartitionSpec as P
+
 
 H = 14
 KV = 2
@@ -227,21 +228,98 @@
     return [(lax.rem(c // 2 + k, lines) * 2 + c % 2, f) for k in range(1, lines)] + [(c2, f)]
 
 
-def kv_body(lines, kv, kv_o, ss, rs):
-    place = where_am_i()
-    greet(line_devices(place, lines))
-    spread_start(kv, kv_o, ss, rs, place, lines)
-    kv_o[place[0]] = kv[...]
-    spread_finish(kv, kv_o, ss, rs, place, lines)
-
-
-def ag_body(x, x_o, ss, rs):
+def kv_body(lines, kv, cot, kv_o, cot_o, ss, rs, ts, tr):
     place = where_am_i()
     c, _, _, m, n = place
+    greet(line_devices(place, lines) + [(c, m), (c, n)])
+    spread_start(kv, kv_o, ss, rs, place, lines)
+    items = [(cot, lambda g, rows: cot_o.at[g, rows])]
+    tokens_start(items, ts, tr, place)
+    kv_o[c] = kv[...]
+    spread_finish(kv, kv_o, ss, rs, place, lines)
+    tokens_finish(items, ts, tr, place)
+
+
+def gates(gate, up, g_act):
+    sg = jax.nn.sigmoid(gate)
+    silu = gate * sg
+    act = (silu * up).astype(bf16)
+    g_gate = (g_act * up * (sg * (1.0 + gate * (1.0 - sg)))).astype(bf16)
+    g_up = (g_act * silu).astype(bf16)
+    return act, g_gate, g_up
+
+
+def mid_body(x, cot, wg_h, wu_h, wd_h, gn_o, down_o, xg, wg, wu, wd, act, back, near, sums, far_in, ws, ss, rs, ns, nr):
+    place = where_am_i()
+    c, f, _, m, n = place
+    far = (m + 2) % 4
+    tok, width = x.shape
+    loads = [
+        pltpu.make_async_copy(src, dst, ws.at[j])
+        for j, (src, dst) in enumerate(((wg_h, wg), (wu_h, wu), (wd_h, wd)))
+    ]
+    for copy in loads:
+        copy.start()
     greet([(c, m), (c, n)])
-    items = [(x, lambda g, rows: x_o.at[g, rows])]
-    tokens_start(items, ss, rs, place)
-    tokens_finish(items, ss, rs, place)
+    half = tok // 2
+    own = remote(x, xg.at[f], ss.at[0], rs.at[0], (c, m))
+    own.start()
+    for j in range(2):
+        rows = pl.ds(j * half, half)
+        remote(x.at[rows], xg.at[f, rows], ss.at[1 + j], rs.at[1 + j], (c, n)).start()
+    xg[f] = x[...]
+    for copy in loads:
+        copy.wait()
+    own.wait()
+
+    def forward(pair):
+        at = pl.ds(pair * 2, 2)
+        xs = xg[at].reshape(2 * tok, width)
+        cs = cot[at].reshape(2 * tok, width)
+        parts = gates(over_last(xs, wg[...]), over_last(xs, wu[...]), over_last(cs, wd[...]))
+        for j, part in enumerate(parts):
+            act[j] = part
+
+    def backward():
+        return plain_dot(act[1], wg[...]) + plain_dot(act[2], wu[...])
+
+    def down(pair):
+        down_o[pl.ds(pair * 2, 2)] = plain_dot(act[0], wd[...]).astype(bf16).reshape(2, tok, width)
+
+    y = f // 2
+    core = f % 2
+    forward(y)
+    for j in range(2):
+        here = xg.at[n, pl.ds(j * half, half)]
+        remote(here, here, ss.at[1 + j], rs.at[1 + j], (c, n)).wait_recv()
+        remote(here, here, ss.at[3 + j], rs.at[3 + j], (c, m)).start()
+    back[...] = backward().reshape(2, tok, width)
+    near[0] = back[1 - core].astype(bf16)
+    to_mate = remote(near.at[0], near.at[1], ns.at[0], nr.at[0], (c, m))
+    to_mate.start()
+    mine = back[core]
+    down(y)
+    gn_o[...] = mine
+    for j in range(2):
+        rows = pl.ds(j * half, half)
+        remote(x.at[rows], xg.at[far, rows], ss.at[3 + j], rs.at[3 + j], (c, m)).wait_recv()
+    forward(1 - y)
+    back[...] = backward().reshape(2, tok, width)
+    near[2] = back[1 - core].astype(bf16)
+    first = remote(near.at[2], near.at[3], ns.at[1], nr.at[1], (c, m))
+    first.start()
+    first.wait()
+    sums[...] = (back[core] + near[3].astype(f32)).astype(bf16)
+    across = remote(sums, far_in, ns.at[2], nr.at[2], (c, n))
+    across.start()
+    down(1 - y)
+    to_mate.wait()
+    for j in range(2):
+        rows = pl.ds(j * half, half)
+        remote(x.at[rows], xg.at[f, rows], ss.at[1 + j], rs.at[1 + j], (c, n)).wait_send()
+        remote(x.at[rows], xg.at[far, rows], ss.at[3 + j], rs.at[3 + j], (c, m)).wait_send()
+    across.wait()
+    gn_o[...] += near[1].astype(f32) + far_in[...].astype(f32)
 
 
 def project_body(x, vec, x_o, vec_o, ss, rs, held, vs, vr):
@@ -260,24 +338,6 @@
         copy.wait()
         total = total + held[k]
     vec_o[...] = total
-
-
-def rs_body(part, out, near, sums, far_in, ss, rs):
-    c, f, _, m, n = where_am_i()
-    far = (m + 2) % 4
-    greet([(c, m), (c, n)])
-    first = remote(part.at[far], near.at[0], ss.at[0], rs.at[0], (c, m))
-    second = remote(part.at[m], near.at[1], ss.at[1], rs.at[1], (c, m))
-    first.start()
-    second.start()
-    first.wait()
-    sums[...] = (part[n].astype(f32) + near[0].astype(f32)).astype(bf16)
-    across = remote(sums, far_in, ss.at[2], rs.at[2], (c, n))
-    across.start()
-    second.wait()
-    mine = part[f].astype(f32) + near[1].astype(f32)
-    across.wait()
-    out[...] = mine + far_in[...].astype(f32)
 
 
 def dkv_body(ctx, part, ghl, sl, out, ghl_o, sl_o, held, ss, rs, gs, gr, as_, ar):
@@ -316,13 +376,7 @@
 
 
 def hidden_units(x, cot, wg, wu, wd):
-    gate, up, g_act = over_last(wg, x), over_last(wu, x), over_last(wd, cot)
-    sg = jax.nn.sigmoid(gate)
-    silu = gate * sg
-    act = (silu * up).astype(bf16)
-    g_gate = (g_act * up * (sg * (1.0 + gate * (1.0 - sg)))).astype(bf16)
-    g_up = (g_act * silu).astype(bf16)
-    return act, g_gate, g_up
+    return gates(over_last(wg, x), over_last(wu, x), over_last(wd, cot))
 
 
 def hidden_body(
@@ -517,9 +571,13 @@
     )
     value_low = projected[:, query_width + key_width :].astype(bf16)
     key_value = jnp.concatenate([key_rot.astype(bf16).reshape(tok, key_width), value_low], 1)
-    kv_all = comm_call(
-        functools.partial(kv_body, lines), sds((ctx, tok, 2 * key_width), bf16), [dma((2, lines)), dma((2, lines))], 1
-    )(key_value).reshape(seq_length, 2 * key_width)
+    kv_all, cot_group = comm_call(
+        functools.partial(kv_body, lines),
+        (sds((ctx, tok, 2 * key_width), bf16), sds((fsdp, tok, width), bf16)),
+        [dma((2, lines)), dma((2, lines))] + gather_sems(1),
+        1,
+    )(key_value, grad_out)
+    kv_all = kv_all.reshape(seq_length, 2 * key_width)
     keys = kv_all[:, :key_width].reshape(seq_length, KV, HD)
     values = kv_all[:, key_width:].reshape(seq_length, KV, HD)
     key_rows = jnp.arange(seq_length, dtype=jnp.int32)
@@ -536,37 +594,39 @@
     inverse_second = lax.rsqrt(jnp.mean(hidden_state * hidden_state, -1, keepdims=True) + EPSILON)
     normed_second = (hidden_state * inverse_second * gain_second).astype(bf16)
     x_all = lax.all_gather(normed_second, ("ctx", "fsdp"), axis=0, tiled=True)
-    x_group = comm_call(
-        ag_body, sds((fsdp, tok, width), bf16), gather_sems(1), 2
-    )(normed_second).reshape(fsdp * tok, width)
-    cot_group = lax.dynamic_slice_in_dim(cot_all, c * fsdp * tok, fsdp * tok, 0)
-
-    def ffn(x, cot):
-        gate = jnp.dot(x, w_gate, preferred_element_type=f32)
-        up = jnp.dot(x, w_up, preferred_element_type=f32)
-        g_act = lax.dot_general(cot, w_down, (((1,), (1,)), ((), ())), preferred_element_type=f32)
-        sg = jax.nn.sigmoid(gate)
-        act = (gate * sg * up).astype(bf16)
-        g_gate = (g_act * up * sg * (1.0 + gate * (1.0 - sg))).astype(bf16)
-        g_up = (g_act * gate * sg).astype(bf16)
-        return act, g_gate, g_up
-
-    act, g_gate, g_up = ffn(x_group, cot_group)
-    g_normed_part = (over_last(g_gate, w_gate) + over_last(g_up, w_up)).astype(bf16)
-    grad_normed2 = comm_call(
-        rs_body,
-        sds((tok, width), f32),
-        [
-            pltpu.VMEM((2, tok, width), bf16),
+    units = w_down.shape[0]
+    any_spec = pl.BlockSpec(memory_space=pltpu.HBM)
+    wg_t, wu_t = w_gate.T, w_up.T
+    grad_normed2, down_part = pl.pallas_call(
+        mid_body,
+        out_shape=(sds((tok, width), f32), sds((fsdp, tok, width), bf16)),
+        in_specs=[VMEM, VMEM, any_spec, any_spec, any_spec],
+        out_specs=(VMEM, VMEM),
+        scratch_shapes=[pltpu.VMEM((fsdp, tok, width), bf16)]
+        + [pltpu.VMEM((units, width), bf16)] * 3
+        + [
+            pltpu.VMEM((3, 2 * tok, units), bf16),
+            pltpu.VMEM((2, tok, width), f32),
+            pltpu.VMEM((4, tok, width), bf16),
             pltpu.VMEM((tok, width), bf16),
             pltpu.VMEM((tok, width), bf16),
             dma((3,)),
+            dma((5,)),
+            dma((5,)),
+            dma((3,)),
             dma((3,)),
         ],
-        3,
-    )(g_normed_part.reshape(fsdp, tok, width))
-    down_part = jnp.dot(act, w_down, preferred_element_type=f32).astype(bf16)
-    down_out = lax.psum_scatter(down_part, "fsdp", scatter_dimension=0, tiled=True).astype(f32)
+        compiler_params=pltpu.CompilerParams(
+            collective_id=2, has_side_effects=True, vmem_limit_bytes=40 << 20
+        ),
+        cost_estimate=pl.CostEstimate(
+            flops=12 * fsdp * tok * width * units, bytes_accessed=6 * units * width, transcendentals=0
+        ),
+        name="mid",
+    )(normed_second, cot_group, wg_t, wu_t, w_down)
+    down_part = down_part.reshape(fsdp * tok, width)
+    down_out = lax.psum_scatter(down_part, "fsdp", scatter_dimension=0, tiled=True)
+    down_out = down_out.astype(f32)
     block_out = (hidden_state + down_out).astype(bf16)[None]
 
     hidden_back, second_gain_grad = norm_back(hidden_state, inverse_second, gain_second, grad_normed2)
@@ -653,7 +713,7 @@
         ends.append(ends[-1] + size // fsdp)
     own = [own[ends[i] : ends[i + 1]] for i in range(5)]
 
-    gate_grad, up_grad, down_grad = hidden_grads(x_all, cot_all, w_gate.T, w_up.T, w_down)
+    gate_grad, up_grad, down_grad = hidden_grads(x_all, cot_all, wg_t, wu_t, w_down)
     return (
         block_out,
         input_grad,
@@ -709,4 +769,5 @@
         P("fsdp", None),
         P("fsdp", None, "ctx"),
     )
+
     return jax.shard_map(shards, mesh=mesh, in_specs=in_specs, out_specs=out_specs, check_vma=False)

time: 292 us -> 476 us (1.63)
  waiting for transfers between devices: 4.68 us -> 216 us
  matrix products: 41.5 us -> 22.5 us
  Pallas kernels: 176 us -> 168 us
    all_gather x1, waiting for transfers between devices: 0.02 us -> 74.5 us  [shards(): cot_all = lax.all_gather(grad_out, ('ctx', 'fsdp'), axis=0, tiled=True)]
    psum x1, waiting for transfers between devices: 3.89 us -> 73.7 us  [shards(): weight_grads = lax.psum(weight_grads, 'ctx')]
    all_gather x1, waiting for transfers between devices: 0.02 us -> 66.3 us  [shards(): x_all = lax.all_gather(normed_second, ('ctx', 'fsdp'), axis=0, tiled=True)]
    pallas_call x6 -> x4, Pallas kernels: 97.9 us -> 66.1 us  [call(): pl.pallas_call(body, out_shape=out_shape, in_specs=[VMEM] * len(args), ou...]
    pallas_call x0 -> x1, Pallas kernels: none -> 24.5 us  [shards(): pl.pallas_call(mid_body, out_shape=(sds((tok, width), f32), sds((fsdp, to...]
    dot_general x4 -> x0, matrix products: 11 us -> none  [the longest x1 3.69 us: ffn(): lax.dot_general(cot, w_down, (((1,), (1,)), ((), ())), preferred_element_...]
    dot_general x4 -> x2, matrix products: 9.26 us -> 3.04 us  [over_last(): lax.dot_general(a, b, (((1,), (1,)), ((), ())), preferred_element_type=f32)]
    unnamed x99 -> x115, local copies, waits for them, and re-layouts: 13.8 us -> 14.9 us
  transfers between devices with their start and end apart: 4 -> 4, of which waited for: 1 -> 3; matrix products, arithmetic and copies ran while one was open for 27% -> 2% of each run, Pallas kernels for 61% -> 0%
where the time goes in v1:
time: 476 us; the launch traced here: 475 us
  waiting for transfers between devices  216 us (45%)
  Pallas kernels  168 us (35%)
  local copies, waits for them, and re-layouts  35.9 us (8%)
  matrix products  22.5 us (5%)
  between operations  16.2 us (3%)
  other arithmetic  16 us (3%)
    pallas_call x1, Pallas kernels, hidden_grads(): pl.pallas_call(functools.partial(hidden_body, chunk, block), out_shape=(j...  77.5 us
    all_gather x1, waiting for transfers between devices, shards(): cot_all = lax.all_gather(grad_out, ('ctx', 'fsdp'), axis=0, tiled=True)  74.5 us
    psum x1, waiting for transfers between devices, shards(): weight_grads = lax.psum(weight_grads, 'ctx')  73.7 us
    all_gather x1, waiting for transfers between devices, shards(): x_all = lax.all_gather(normed_second, ('ctx', 'fsdp'), axis=0, tiled=True)  66.3 us
    pallas_call x4, Pallas kernels, call(): pl.pallas_call(body, out_shape=out_shape, in_specs=[VMEM] * len(args), ou...  66.1 us
    pallas_call x1, Pallas kernels, shards(): pl.pallas_call(mid_body, out_shape=(sds((tok, width), f32), sds((fsdp, to...  24.5 us
    unnamed x115, local copies, waits for them, and re-layouts  14.9 us
  transfers between devices with their start and end apart: 4, of which 3 were waited for; matrix products, arithmetic and copies ran while one was open for 2% of the time, Pallas kernels for 0%

profile of v1, /device:TPU:0, one launch (start us, length us, event | category | flops | bytes accessed | tf_op | source)
XLA Modules:
  0.0 475.3 jit_solution(8662539040437344052)
XLA Ops:
  8.1 0.7 pad.29
  8.8 0.7 pad.30
  9.5 0.7 pad.31
  10.1 0.7 pad.32
  10.8 0.7 pad.33
  11.5 0.7 broadcast_in_dim.25.seg
  12.2 1.0 copy-done.7
  13.2 1.0 copy-done.8
  14.2 0.8 copy-done.9
  15.0 0.8 copy-done.10
  15.8 24.5 %shard_map.271 = (bf16[896,1152]{1,0:T(8,128)(2,1)S(1)}, bf16[896,896]{1,0:T(8,128)(2,1)S(1)}, bf16[4,16,256]{2,1,0:T(8,128)(2,1)S(1)}, s32[8,8,128]{2,1,0:T(8,128)S(1)}) custom-call(bf16[224,896]{1,0:T(8,128)(2,1)S(1)} %copy-done.7, bf16[224,128]{1,0:T(8,128)(2,1)S(1)} %copy-done.9, bf16[224,128]{1,0:T(8,128)(2,1)S(1)} %copy-done.10, ...), custom_call_target="tpu_custom_call" | custom-call | tf_op jit(solution)/shard_map/pallas_call | solution.py:152
  40.3 1.1 copy-done
  41.9 1.1 fusion.34
  43.0 1.5 convolution_add_fusion
  45.1 14.5 %shard_map.272 = (bf16[8,128,256]{2,1,0:T(8,128)(2,1)S(1)}, bf16[4,128,896]{2,1,0:T(8,128)(2,1)S(1)}) custom-call(bf16[128,256]{1,0:T(8,128)(2,1)S(1)} %pad_maximum_fusion.8.kv, bf16[128,896]{1,0:T(8,128)(2,1)S(1)} %bitcast.176), custom_call_target="tpu_custom_call" | custom-call | tf_op jit(solution)/shard_map/pallas_call | solution.py:152
  59.6 0.8 fusion.53
  60.6 1.1 copy.51
  61.7 1.0 copy.52
  62.6 1.1 subtract_convert_fusion.1
  63.8 0.9 copy.50
  64.9 1.2 fusion.2
  66.2 1.5 fusion.8
  67.7 2.3 fusion.56
  71.2 1.7 copy-done.11
  72.8 1.6 copy-done.12
  74.5 1.6 copy-done.13
  76.1 1.2 copy-done.15
  77.3 24.5 %mid.1 = (f32[128,896]{1,0:T(8,128)S(1)}, bf16[4,128,896]{2,1,0:T(8,128)(2,1)}) custom-call(bf16[128,896]{1,0:T(8,128)(2,1)S(1)} %multiply_convert_fusion.1.x, bf16[4,128,896]{2,1,0:T(8,128)(2,1)S(1)} %copy-done.15, bf16[1216,896]{1,0:T(8,128)(2,1)S(1)} %bitcast.179, bf16[1216,896]{1,0:T(8,128)(2,1)S(1)} %bitcast.181, bf16[1216,896]{1,0:T(8,128)(2,1)S(1)} %copy-done.13), custom_call_target="tpu_custom_call" | custom-call | flops 6694109184 | bytes 6537216 | tf_op jit(solution)/shard_map/mid/pallas_call | solution.py:600
  101.8 0.8 multiply_reduce_fusion
  102.6 1.2 fusion.49.ghl
  104.6 1.2 fusion.33
  105.9 5.7 %fusion.1 = bf16[2,7,128,1024]{2,3,1,0:T(8,128)(2,1)S(1)} fusion(f32[2,1024,128,7]{2,1,3,0:T(8,128)} %copy-done.16, f32[2,7,128]{2,1,0:T(8,128)S(1)} %fusion.33, f32[2,7,128]{2,1,0:T(8,128)S(1)} %log_add_fusion, pred[128,1024]{0,1:T(8,128)(4,1)S(1)} %copy-done.26, bf16[1024,2,64,1]{0,2,3,1:T(8,128)(2,1)} %bitcast.203, bf16[128,2,7,64]{0,3,2,1:T(8,128)(2,1)S(1)} %bitcast.199), kind=kOutput, calls=%fused_computation.2 | convolution fusion | flops 245891072 | bytes 11646976 | tf_op jit(solution)/shard_map/tkgd,nkd->kgtn/dot_general | solution.py:640
  111.6 1.5 convolution_multiply_fusion
  113.1 1.4 fusion.28
  114.6 3.2 fusion.25
  118.4 0.9 copy.60
  119.6 1.0 copy.90
  120.6 0.9 copy.59
  121.5 1.8 copy.62
  123.3 1.3 copy.92
  124.6 1.2 copy.61
  125.8 1.1 pad_maximum_fusion.1.part
  126.9 0.8 fusion.35
  127.7 1.0 pad_maximum_fusion.2.sl
  128.8 16.3 %shard_map.273 = (f32[128,256]{1,0:T(8,128)S(1)}, bf16[4,128,896]{2,1,0:T(8,128)(2,1)S(1)}, bf16[4,256,224]{2,1,0:T(8,128)(2,1)S(1)}) custom-call(bf16[8,128,256]{2,1,0:T(8,128)(2,1)S(1)} %pad_maximum_fusion.1.part, bf16[128,896]{1,0:T(8,128)(2,1)S(1)} %fusion.49.ghl, bf16[4,256,224]{2,1,0:T(8,128)(2,1)S(1)} %pad_maximum_fusion.2.sl), custom_call_target="tpu_custom_call" | custom-call | tf_op jit(solution)/shard_map/pallas_call | solution.py:152
  145.1 0.9 copy-done.5
  146.2 0.8 copy.64
  147.3 1.0 convert_reduce_fusion
  148.3 2.4 multiply_reduce_fusion.1
  150.8 10.8 %shard_map.274 = (bf16[4,128,1152]{2,1,0:T(8,128)(2,1)S(1)}, f32[8,384]{1,0:T(8,128)S(1)}) custom-call(bf16[128,1152]{1,0:T(8,128)(2,1)S(1)} %get-tuple-element.72.x, f32[8,384]{1,0:T(8,128)S(1)} %reshape.247.vec), custom_call_target="tpu_custom_call" | custom-call | tf_op jit(solution)/shard_map/pallas_call | solution.py:152
  162.1 1.6 fusion.17
  164.0 1.1 pad_maximum_fusion
  165.8 0.7 all-gather.4.cloned.1.call-update
  166.5 0.7 all-gather.6.cloned.1.call-update
  167.2 0.6 add.140
  167.8 73.7 %all-reduce.10.cloned.1.call-done = bf16[240,2048]{1,0:T(8,128)(2,1)} async-done(((bf16[240,2048]{1,0:T(8,128)(2,1)}), bf16[240,2048]{1,0:T(8,128)(2,1)}) %all-reduce.10.cloned.1.call-update) | async-done | bytes 983056 | tf_op jit(solution)/shard_map/psum | solution.py:707
  241.5 1.5 convert_element_type.137
  243.6 1.4 fusion.50
  245.0 1.5 fusion.52
  246.6 1.3 fusion.51
  247.9 1.9 fusion.39
  249.8 66.3 %all-gather.4.cloned.1.call-done.x_h = bf16[4096,896]{1,0:T(8,128)(2,1)} async-done(((bf16[128,896]{1,0:T(8,128)(2,1)}), bf16[4096,896]{1,0:T(8,128)(2,1)}) %all-gather.4.cloned.1.call-update) | async-done | bytes 7340048 | tf_op jit(solution)/shard_map/all_gather | solution.py:596
  316.1 74.5 %all-gather.6.cloned.1.call-done = bf16[1,4096,896]{2,1,0:T(8,128)(2,1)} async-done(((bf16[1,128,896]{2,1,0:T(8,128)(2,1)}), bf16[1,4096,896]{2,1,0:T(8,128)(2,1)}) %all-gather.6.cloned.1.call-update) | async-done | bytes 7340048 | tf_op jit(solution)/shard_map/all_gather | solution.py:531
  390.6 77.5 %hidden_grads.1 = (f32[1216,896]{1,0:T(8,128)}, f32[1216,896]{1,0:T(8,128)}, f32[1216,896]{1,0:T(8,128)}) custom-call(bf16[4096,896]{1,0:T(8,128)(2,1)} %all-gather.4.cloned.1.call-done.x_h, bf16[4096,896]{1,0:T(8,128)(2,1)} %bitcast.218, bf16[1216,896]{1,0:T(8,128)(2,1)} %bitcast.178, bf16[1216,896]{1,0:T(8,128)(2,1)} %bitcast.180, bf16[1216,896]{1,0:T(8,128)(2,1)} %wd_h.3), custom_call_target="tpu_custom_call" | custom-call | flops 53552873472 | bytes 34291712 | tf_op jit(solution)/shard_map/hidden_grads/pallas_call | solution.py:477
  (170 shorter events, 6.7 us)
Async XLA Ops:
  8.0 37.0 %copy-start.3 = (bf16[1,128,896]{2,1,0:T(8,128)(2,1)S(1)}, bf16[1,128,896]{2,1,0:T(8,128)(2,1)}, u32[]{:S(2)}) copy-start(bf16[1,128,896]{2,1,0:T(8,128)(2,1)} %param.31) | copy-start | bytes 688132
  8.0 233.5 %all-reduce.10.cloned.1.call-start = ((), (), s32[]{:S(2)}) async-start(), calls=%async_computation.2 | async-start | bytes 1966080 | tf_op jit(solution)/shard_map/psum | solution.py:707
  12.2 1.0 copy-start.7
  13.2 1.0 copy-start.8
  14.2 0.8 copy-start.9
  15.0 0.8 copy-start.10
  15.8 28.9 %copy-start.53 = (s32[1,128]{1,0:T(1,128)S(1)}, s32[1,128]{1,0:T(1,128)}, u32[]{:S(2)}) copy-start(s32[1,128]{1,0:T(1,128)} %param.18) | copy-start | bytes 1540
  40.3 1.2 copy-start
  41.9 1.1 copy-start.41
  43.0 21.7 %copy-start.50 = (s32[1,128]{1,0:T(1,128)S(1)}, s32[1,128]{1,0:T(1,128)}, u32[]{:S(2)}) copy-start(s32[1,128]{1,0:T(1,128)} %param.17) | copy-start | bytes 1540
  43.0 21.9 %copy-start.48 = (f32[128]{0:T(128)}, f32[128]{0:T(128)S(1)}, u32[]{:S(2)}) copy-start(f32[128]{0:T(128)S(1)} %add_rsqrt_fusion.1) | copy-start | bytes 1540
  44.9 21.2 %copy-start.35 = (f32[128,32]{0,1:T(8,128)}, f32[128,32]{0,1:T(8,128)S(1)}, u32[]{:S(2)}) copy-start(f32[128,32]{0,1:T(8,128)S(1)} %get-tuple-element.100) | copy-start | bytes 49156
  59.6 1.0 copy-start.14
  61.7 4.4 copy-start.23
  63.8 2.4 copy-start.29
  63.8 2.4 copy-start.31
  64.9 2.8 copy-start.25
  66.1 3.8 copy-start.16
  66.1 1.5 copy-start.38
  67.7 46.9 %copy-start.43 = (f32[2,7,128]{2,1,0:T(8,128)}, f32[2,7,128]{2,1,0:T(8,128)S(1)}, u32[]{:S(2)}) copy-start(f32[2,7,128]{2,1,0:T(8,128)S(1)} %log_add_fusion) | copy-start | bytes 21508
  67.7 2.5 copy-start.1
  67.7 2.6 copy-start.19
  70.0 0.9 copy-start.34
  70.9 30.9 %copy-start.17 = (f32[128,896]{1,0:T(8,128)}, f32[128,896]{1,0:T(8,128)S(1)}, u32[]{:S(2)}) copy-start(f32[128,896]{1,0:T(8,128)S(1)} %get-tuple-element.106) | copy-start | bytes 1376260
  70.9 31.6 %copy-start.46 = (f32[128]{0:T(128)}, f32[128]{0:T(128)S(1)}, u32[]{:S(2)}) copy-start(f32[128]{0:T(128)S(1)} %add_rsqrt_fusion) | copy-start | bytes 1540
  71.0 31.5 %copy-start.39 = (f32[896]{0:T(1024)}, f32[896]{0:T(1024)S(1)}, u32[]{:S(2)}) copy-start(f32[896]{0:T(1024)S(1)} %mul.311) | copy-start | bytes 10756
  71.1 30.6 %copy-start.6 = (bf16[128,896]{1,0:T(8,128)(2,1)}, bf16[128,896]{1,0:T(8,128)(2,1)S(1)}, u32[]{:S(2)}) copy-start(bf16[128,896]{1,0:T(8,128)(2,1)S(1)} %multiply_convert_fusion.1.x) | copy-start | bytes 688132
  71.1 1.7 copy-start.11
  72.8 1.6 copy-start.12
  74.5 1.6 copy-start.13
  76.1 1.2 copy-start.15
  77.3 26.5 %copy-start.2 = (bf16[896,896]{1,0:T(8,128)(2,1)S(1)}, bf16[896,896]{1,0:T(8,128)(2,1)}, u32[]{:S(2)}) copy-start(bf16[896,896]{1,0:T(8,128)(2,1)} %copy-done) | copy-start | bytes 4816900
  101.8 4.0 copy-start.26
  102.6 2.0 copy-start.51
  104.6 7.0 %copy-start.33 = (bf16[128,896]{0,1:T(8,128)(2,1)}, bf16[128,896]{0,1:T(8,128)(2,1)S(1)}, u32[]{:S(2)}) copy-start(bf16[128,896]{0,1:T(8,128)(2,1)S(1)} %copy.54) | copy-start | bytes 688132
  104.6 10.0 %slice-start = ((s8[7340032]{0:T(1024)(128)(4,1)}), s8[4194304]{0:T(1024)(128)(4,1)S(1)}, s32[]{:S(2)}) async-start(s8[7340032]{0:T(1024)(128)(4,1)} %bitcast.182), calls=%async_computation.5 | async-start | bytes 8388608
  105.8 5.7 %copy-start.24 = (bf16[1024,128]{0,1:T(8,128)(2,1)S(1)}, bf16[1024,128]{0,1:T(8,128)(2,1)}, u32[]{:S(2)}) copy-start(bf16[1024,128]{0,1:T(8,128)(2,1)} %copy-done.23) | copy-start | bytes 786436
  105.8 8.7 %slice-start.1 = ((s8[7340032]{0:T(1024)(128)(4,1)}), s8[3145728]{0:T(1024)(128)(4,1)S(1)}, s32[]{:S(2)}) async-start(s8[7340032]{0:T(1024)(128)(4,1)} %bitcast.182), calls=%async_computation.6 | async-start | bytes 6291456
  111.6 1.5 copy-start.30
  111.6 1.5 copy-start.32
  114.6 3.8 copy-start.20
  125.8 20.3 %copy-start.27 = (f32[2,64,7,128]{3,1,2,0:T(8,128)S(1)}, f32[2,64,7,128]{3,1,2,0:T(8,128)}, u32[]{:S(2)}) copy-start(f32[2,64,7,128]{3,1,2,0:T(8,128)} %convolution_multiply_fusion) | copy-start | bytes 1376260
  125.8 20.3 %copy-start.36 = (f32[128,32]{0,1:T(8,128)S(1)}, f32[128,32]{0,1:T(8,128)}, u32[]{:S(2)}) copy-start(f32[128,32]{0,1:T(8,128)} %copy-done.35) | copy-start | bytes 49156
  126.9 20.2 %copy-start.37 = (f32[128,32]{0,1:T(8,128)S(1)}, f32[128,32]{0,1:T(8,128)}, u32[]{:S(2)}) copy-start(f32[128,32]{0,1:T(8,128)} %copy-done.35) | copy-start | bytes 49156
  126.9 21.4 %copy-start.42 = (f32[896]{0:T(1024)S(1)}, f32[896]{0:T(1024)}, u32[]{:S(2)}) copy-start(f32[896]{0:T(1024)} %copy-done.41) | copy-start | bytes 10756
  126.9 21.4 %copy-start.49 = (f32[128]{0:T(128)S(1)}, f32[128]{0:T(128)}, u32[]{:S(2)}) copy-start(f32[128]{0:T(128)} %copy-done.48) | copy-start | bytes 1540
  126.9 23.9 %copy-start.45 = (f32[896]{0:T(1024)S(1)}, f32[896]{0:T(1024)}, u32[]{:S(2)}) copy-start(f32[896]{0:T(1024)} %get-tuple-element.62) | copy-start | bytes 10756
  145.1 0.9 copy-start.5
  150.8 16.5 %copy-start.44 = (f32[2,7,128]{2,1,0:T(8,128)S(1)}, f32[2,7,128]{2,1,0:T(8,128)}, u32[]{:S(2)}) copy-start(f32[2,7,128]{2,1,0:T(8,128)} %copy-done.43) | copy-start | bytes 21508
  165.1 82.8 %copy-start.4 = (bf16[1,128,896]{2,1,0:T(8,128)(2,1)S(1)}, bf16[1,128,896]{2,1,0:T(8,128)(2,1)}, u32[]{:S(2)}) copy-start(bf16[1,128,896]{2,1,0:T(8,128)(2,1)} %param.31) | copy-start | bytes 688132
  165.1 82.8 %copy-start.18 = (f32[128,896]{1,0:T(8,128)S(1)}, f32[128,896]{1,0:T(8,128)}, u32[]{:S(2)}) copy-start(f32[128,896]{1,0:T(8,128)} %copy-done.17) | copy-start | bytes 1376260
  165.1 82.8 %copy-start.21 = (bf16[1,128,896]{2,1,0:T(8,128)(2,1)S(1)}, bf16[1,128,896]{2,1,0:T(8,128)(2,1)}, u32[]{:S(2)}) copy-start(bf16[1,128,896]{2,1,0:T(8,128)(2,1)} %param.16) | copy-start | bytes 688132
  165.1 82.8 %copy-start.28 = (f32[128,896]{1,0:T(8,128)S(1)}, f32[128,896]{1,0:T(8,128)}, u32[]{:S(2)}) copy-start(f32[128,896]{1,0:T(8,128)} %get-tuple-element.107) | copy-start | bytes 1376260
  165.1 82.8 %copy-start.40 = (f32[896]{0:T(1024)S(1)}, f32[896]{0:T(1024)}, u32[]{:S(2)}) copy-start(f32[896]{0:T(1024)} %copy-done.39) | copy-start | bytes 10756
  165.1 82.8 %copy-start.47 = (f32[128]{0:T(128)S(1)}, f32[128]{0:T(128)}, u32[]{:S(2)}) copy-start(f32[128]{0:T(128)} %copy-done.46) | copy-start | bytes 1540
  165.1 82.8 %copy-start.52 = (f32[128]{0:T(128)S(1)}, f32[128]{0:T(128)}, u32[]{:S(2)}) copy-start(f32[128]{0:T(128)} %copy-done.51) | copy-start | bytes 1540
  165.1 82.7 %reduce-scatter.2.cloned.1.call-start = ((), (), s32[]{:S(2)}) async-start(), calls=%async_computation.1 | async-start | bytes 1146880 | tf_op jit(solution)/shard_map/reduce_scatter | solution.py:628
  165.7 150.4 %all-gather.4.cloned.1.call-start = ((), (), s32[]{:S(2)}) async-start(), calls=%async_computation.3 | async-start | bytes 7569408 | tf_op jit(solution)/shard_map/all_gather | solution.py:596
  166.5 224.1 %all-gather.6.cloned.1.call-start = ((), (), s32[]{:S(2)}) async-start(), calls=%async_computation.4 | async-start | bytes 7569408 | tf_op jit(solution)/shard_map/all_gather | solution.py:531
  241.5 5.1 %copy-start.22 = (bf16[240,2048]{1,0:T(8,128)(2,1)S(1)}, bf16[240,2048]{1,0:T(8,128)(2,1)}, u32[]{:S(2)}) copy-start(bf16[240,2048]{1,0:T(8,128)(2,1)} %all-reduce.10.cloned.1.call-done) | copy-start | bytes 2949124
Sparse Core Ops, SparseCore 0:
  165.3 76.2 all-reduce.9
  244.4 71.6 all-gather.3
  319.0 71.5 all-gather.5
Sparse Core Ops, SparseCore 1:
  168.2 22.7 reduce-scatter.1

commit v2 on v1

v2 whole, which is shorter than its diff:
```python
import functools
import math

import jax
import jax.numpy as jnp
from jax import lax
from jax.experimental import pallas as pl
from jax.experimental.pallas import tpu as pltpu
from jax.sharding import PartitionSpec as P


H = 14
KV = 2
HD = 64


EPSILON = 1e-06
ROPE_BASE = 1000000.0
MASK_FILL = -1e30
MESH = pl.DeviceIdType.MESH
VMEM = pl.BlockSpec(memory_space=pltpu.VMEM)
f32 = jnp.float32
bf16 = jnp.bfloat16


def rope_tables(positions, head_dim):
    half = head_dim // 2
    freq = ROPE_BASE ** (-(jnp.arange(half, dtype=jnp.float32) * 2.0 / head_dim))
    angle = positions.astype(jnp.float32)[None, :] * freq[:, None]
    return jnp.cos(angle), jnp.sin(angle)


def remote(src, dst, send_sem, recv_sem, device):
    return pltpu.make_async_remote_copy(
        src_ref=src, dst_ref=dst, send_sem=send_sem, recv_sem=recv_sem, device_id=device,
        device_id_type=MESH,
    )


def where_am_i():
    c, f = lax.axis_index("ctx"), lax.axis_index("fsdp")
    c2 = c + 1 - 2 * (c % 2)
    m = f + 1 - 2 * (f % 2)
    n = (f + 2) % 4
    return c, f, c2, m, n


def greet(devices):
    barrier = pltpu.get_barrier_semaphore()
    for device in devices:
        pl.semaphore_signal(barrier, inc=1, device_id=device, device_id_type=MESH)
    pl.semaphore_wait(barrier, len(devices))


def gather_start(items, ss, rs, place):
    c, f, _, m, n = place
    h = c % 2
    for i, (src, dst) in enumerate(items):
        half = src.shape[0] // 2
        rows = pl.ds(h * half, half)
        remote(src.at[rows], dst(f).at[rows], ss.at[i, 1], rs.at[i, 1], (c, n)).start()
    for i, (src, dst) in enumerate(items):
        remote(src, dst(f), ss.at[i, 0], rs.at[i, 0], (c, m)).start()
        pltpu.make_async_copy(src, dst(f), ss.at[i, 5]).start()


def gather_finish(items, ss, rs, place):
    c, f, c2, m, n = place
    h = c % 2
    far = (m + 2) % 4
    for i, (src, dst) in enumerate(items):
        half = src.shape[0] // 2
        mine = dst(n).at[pl.ds(h * half, half)]
        remote(mine, mine, ss.at[i, 1], rs.at[i, 1], (c, n)).wait_recv()
        remote(mine, mine, ss.at[i, 2], rs.at[i, 2], (c2, f)).start()
        remote(mine, mine, ss.at[i, 3], rs.at[i, 3], (c, m)).start()
    for i, (src, dst) in enumerate(items):
        half = src.shape[0] // 2
        other = dst(n).at[pl.ds((1 - h) * half, half)]
        remote(other, other, ss.at[i, 2], rs.at[i, 2], (c2, f)).wait_recv()
        remote(other, other, ss.at[i, 4], rs.at[i, 4], (c, m)).start()
    for i, (src, dst) in enumerate(items):
        half = src.shape[0] // 2
        mine, other = pl.ds(h * half, half), pl.ds((1 - h) * half, half)
        remote(src, dst(m), ss.at[i, 0], rs.at[i, 0], (c, m)).wait()
        remote(src.at[mine], dst(f).at[mine], ss.at[i, 1], rs.at[i, 1], (c, n)).wait_send()
        remote(src.at[mine], dst(n).at[mine], ss.at[i, 2], rs.at[i, 2], (c2, f)).wait_send()
        remote(src.at[mine], dst(far).at[mine], ss.at[i, 3], rs.at[i, 3], (c, m)).wait()
        remote(src.at[other], dst(far).at[other], ss.at[i, 4], rs.at[i, 4], (c, m)).wait()
        pltpu.make_async_copy(src, dst(f), ss.at[i, 5]).wait()


def tokens_start(items, ss, rs, place):
    c, f, _, m, n = place
    for i, (src, dst) in enumerate(items):
        half = src.shape[0] // 2
        for j in range(2):
            rows = pl.ds(j * half, half)
            remote(src.at[rows], dst(f, rows), ss.at[i, 1 + j], rs.at[i, 1 + j], (c, n)).start()
    for i, (src, dst) in enumerate(items):
        rows = pl.ds(0, src.shape[0])
        remote(src, dst(f, rows), ss.at[i, 0], rs.at[i, 0], (c, m)).start()
        dst(f, rows)[...] = src[...]


def tokens_finish(items, ss, rs, place):
    c, f, _, m, n = place
    far = (m + 2) % 4
    for i, (src, dst) in enumerate(items):
        half = src.shape[0] // 2
        for j in range(2):
            here = dst(n, pl.ds(j * half, half))
            remote(here, here, ss.at[i, 1 + j], rs.at[i, 1 + j], (c, n)).wait_recv()
            remote(here, here, ss.at[i, 3 + j], rs.at[i, 3 + j], (c, m)).start()
    for i, (src, dst) in enumerate(items):
        half = src.shape[0] // 2
        remote(src, dst(m, pl.ds(0, src.shape[0])), ss.at[i, 0], rs.at[i, 0], (c, m)).wait()
        for j in range(2):
            rows = pl.ds(j * half, half)
            remote(src.at[rows], dst(f, rows), ss.at[i, 1 + j], rs.at[i, 1 + j], (c, n)).wait_send()
            remote(src.at[rows], dst(far, rows), ss.at[i, 3 + j], rs.at[i, 3 + j], (c, m)).wait()


def gather_sems(count):
    return [pltpu.SemaphoreType.DMA((count, 6)), pltpu.SemaphoreType.DMA((count, 6))]


def spread_start(src, dst, ss, rs, place, lines):
    c, f, c2, _, _ = place
    for k in range(1, lines):
        p = lax.rem(c // 2 + k, lines) * 2 + c % 2
        remote(src, dst.at[c], ss.at[0, k], rs.at[0, k], (p, f)).start()
    remote(src, dst.at[c], ss.at[1, 0], rs.at[1, 0], (c2, f)).start()


def spread_finish(src, dst, ss, rs, place, lines):
    c, f, c2, _, _ = place
    for k in range(1, lines):
        giver = lax.rem(c // 2 + lines - k, lines) * 2 + c % 2
        block = dst.at[giver]
        remote(block, block, ss.at[0, k], rs.at[0, k], (c2, f)).wait_recv()
        remote(block, block, ss.at[1, k], rs.at[1, k], (c2, f)).start()
    for k in range(lines):
        giver = lax.rem(c2 // 2 + lines - k, lines) * 2 + c2 % 2
        remote(src, dst.at[giver], ss.at[1, k], rs.at[1, k], (c2, f)).wait()
        if k:
            remote(src, dst.at[c], ss.at[0, k], rs.at[0, k], (c2, f)).wait_send()


def line_devices(place, lines):
    c, f, c2, _, _ = place
    return [(lax.rem(c // 2 + k, lines) * 2 + c % 2, f) for k in range(1, lines)] + [(c2, f)]


def gates(gate, up, g_act):
    sg = jax.nn.sigmoid(gate)
    silu = gate * sg
    act = (silu * up).astype(bf16)
    g_gate = (g_act * up * (sg * (1.0 + gate * (1.0 - sg)))).astype(bf16)
    g_up = (g_act * silu).astype(bf16)
    return act, g_gate, g_up


class Spread:
    def __init__(self, place, lines, x, group, full, sems):
        self.place, self.lines, self.x, self.group, self.full = place, lines, x, group, full
        self.half = x.shape[0] // 2
        self.line_s, self.line_r, self.pair_s, self.pair_r, self.y_s, self.y_r, self.mate_s, self.mate_r = sems

    def column(self, k):
        c = self.place[0]
        return lax.rem(c // 2 + self.lines - k, self.lines) * 2 + c % 2

    def ahead(self, k):
        c = self.place[0]
        return lax.rem(c // 2 + k, self.lines) * 2 + c % 2

    def each(self, first, act):
        if self.lines <= 4:
            for k in range(first, self.lines):
                act(k)
        else:
            pl.loop(first, self.lines)(act)

    def view(self, b, g, j):
        return self.full.at[b, g, pl.ds(j * self.half, self.half)]

    def source(self, way):
        _, _, _, _, n = self.place
        rows = pl.ds((0 if way == 0 else 1) * self.half, self.half)
        return self.x.at[rows] if way < 2 else self.group.at[n, rows]

    def slot(self, b, way):
        _, f, _, _, n = self.place
        return self.view(b, n if way == 2 else f, 0 if way == 0 else 1)

    def line(self, way, k):
        c, f, _, _, _ = self.place
        return remote(
            self.source(way), self.slot(c, way), self.line_s.at[way, k], self.line_r.at[way, k], (self.ahead(k), f)
        )

    def arrived(self, way, k):
        here = self.slot(self.column(k), way)
        f = self.place[1]
        return remote(here, here, self.line_s.at[way, k], self.line_r.at[way, k], (self.ahead(k), f))

    def pair(self, way, k):
        c, f, c2, _, _ = self.place
        here = self.slot(self.column(k), way) if not isinstance(k, int) or k else None
        src = self.source(way) if here is None else here
        dst = self.slot(c, way) if here is None else here
        return remote(src, dst, self.pair_s.at[way, k], self.pair_r.at[way, k], (c2, f))

    def other(self, k):
        b = self.column(k)
        return b + 1 - 2 * (b % 2)

    def paired(self, way, k):
        _, f, c2, _, _ = self.place
        here = self.slot(self.other(k), way)
        return remote(here, here, self.pair_s.at[way, k], self.pair_r.at[way, k], (c2, f))

    def block(self, side, k):
        return self.other(k) if side else self.column(k)

    def across(self, side, k):
        c, _, _, _, n = self.place
        here = self.slot(self.block(side, k), 0)
        return remote(here, here, self.y_s.at[side, k], self.y_r.at[side, k], (c, n))

    def crossed(self, side, k):
        c, _, _, _, n = self.place
        here = self.view(self.block(side, k), n, 0)
        return remote(here, here, self.y_s.at[side, k], self.y_r.at[side, k], (c, n))

    def hand(self, way, side, k):
        c, _, _, m, n = self.place
        b = self.block(side, k)
        here = self.view(b, n, 0) if way == 3 else self.slot(b, way)
        return remote(here, here, self.mate_s.at[way, side, k], self.mate_r.at[way, side, k], (c, m))

    def handed(self, way, side, k):
        c, _, _, m, _ = self.place
        far = (m + 2) % 4
        b = self.block(side, k)
        here = self.view(b, far if way > 1 else m, 1 if way in (1, 2) else 0)
        return remote(here, here, self.mate_s.at[way, side, k], self.mate_r.at[way, side, k], (c, m))

    def start(self, way):
        self.each(1, lambda k: self.line(way, k).start())
        self.pair(way, 0).start()

    def on_line(self, way):
        def act(k):
            self.arrived(way, k).wait_recv()
            self.pair(way, k).start()
            self.hand(way, 0, k).start()
            if way == 0:
                self.across(0, k).start()

        self.each(1, act)

    def on_pair(self, way):
        def act(k):
            self.paired(way, k).wait_recv()
            self.hand(way, 1, k).start()
            if way == 0:
                self.across(1, k).start()

        self.each(0, act)

    def on_y(self, side):
        def act(k):
            self.crossed(side, k).wait_recv()
            self.hand(3, side, k).start()

        self.each(1 - side, act)

    def finish(self):
        for way in range(3):
            self.each(1, lambda k: self.line(way, k).wait_send())
            self.each(0, lambda k: self.pair(way, k).wait_send())
        for side in range(2):
            self.each(1 - side, lambda k: self.across(side, k).wait_send())
            for way in range(4):
                self.each(1 - side, lambda k: self.hand(way, side, k).wait_send())
                self.each(1 - side, lambda k: self.handed(way, side, k).wait_recv())


def spread_sems(lines):
    dma = pltpu.SemaphoreType.DMA
    return [dma(shape) for shape in ((3, lines), (3, lines), (2, lines), (4, 2, lines)) for _ in range(2)]


def mid_body(
    lines, x, cot, hid, wg_h, wu_h, wd_h, gn_o, block_o, x_o,
    xg, wg, wu, wd, act, back, near, sums, far_in, ws, os, ss, rs, ns, nr, *spread
):
    place = where_am_i()
    c, f, _, m, n = place
    far = (m + 2) % 4
    tok, width = x.shape
    loads = [
        pltpu.make_async_copy(src, dst, ws.at[j])
        for j, (src, dst) in enumerate(((wg_h, wg), (wu_h, wu), (wd_h, wd)))
    ]
    for copy in loads:
        copy.start()
    greet(line_devices(place, lines) + [(c, m), (c, n)])
    half = tok // 2
    own = remote(x, xg.at[f], ss.at[0], rs.at[0], (c, m))
    own.start()
    for j in range(2):
        rows = pl.ds(j * half, half)
        remote(x.at[rows], xg.at[f, rows], ss.at[1 + j], rs.at[1 + j], (c, n)).start()
    everyone = Spread(place, lines, x, xg, x_o, spread)
    everyone.start(0)
    everyone.start(1)
    xg[f] = x[...]
    for copy in loads:
        copy.wait()
    own.wait()

    def forward(pair):
        at = pl.ds(pair * 2, 2)
        xs = xg[at].reshape(2 * tok, width)
        cs = cot[at].reshape(2 * tok, width)
        parts = gates(over_last(xs, wg[...]), over_last(xs, wu[...]), over_last(cs, wd[...]))
        for j, part in enumerate(parts):
            act[j] = part

    def backward():
        return plain_dot(act[1], wg[...]) + plain_dot(act[2], wu[...])

    def down():
        return plain_dot(act[0], wd[...])

    y = f // 2
    core = f % 2

    def swap(j):
        return remote(near.at[2 * j], near.at[2 * j + 1], ns.at[j], nr.at[j], (c, m))

    def give(j, value):
        back[...] = value.reshape(2, tok, width)
        near[2 * j] = back[1 - core].astype(bf16)
        swap(j).start()

    def cross(j):
        return remote(sums.at[j], far_in.at[j], ns.at[4 + j], nr.at[4 + j], (c, n))

    def send_over(j, j_swap):
        swap(j_swap).wait()
        sums[j] = (back[core] + near[2 * j_swap + 1].astype(f32)).astype(bf16)
        cross(j).start()

    forward(y)
    for j in range(2):
        here = xg.at[n, pl.ds(j * half, half)]
        remote(here, here, ss.at[1 + j], rs.at[1 + j], (c, n)).wait_recv()
        remote(here, here, ss.at[3 + j], rs.at[3 + j], (c, m)).start()
    everyone.start(2)
    give(0, backward())
    gn_o[...] = back[core]
    give(1, down())
    down_own = hid[...] + back[core]
    everyone.on_line(0)
    for j in range(2):
        rows = pl.ds(j * half, half)
        remote(x.at[rows], xg.at[far, rows], ss.at[3 + j], rs.at[3 + j], (c, m)).wait_recv()
    keep = pltpu.make_async_copy(xg, x_o.at[c], os)
    keep.start()
    forward(1 - y)
    give(2, backward())
    send_over(0, 2)
    everyone.on_line(1)
    give(3, down())
    send_over(1, 3)
    everyone.on_pair(0)
    everyone.on_pair(1)
    everyone.on_y(0)
    cross(0).wait()
    swap(0).wait()
    gn_o[...] += near[1].astype(f32) + far_in[0].astype(f32)
    everyone.on_line(2)
    cross(1).wait()
    swap(1).wait()
    block_o[...] = (down_own + near[3].astype(f32) + far_in[1].astype(f32)).astype(bf16)
    everyone.on_y(1)
    everyone.on_pair(2)
    for j in range(2):
        rows = pl.ds(j * half, half)
        remote(x.at[rows], xg.at[f, rows], ss.at[1 + j], rs.at[1 + j], (c, n)).wait_send()
        remote(x.at[rows], xg.at[far, rows], ss.at[3 + j], rs.at[3 + j], (c, m)).wait_send()
    keep.wait()
    everyone.finish()


def turn(values, cos, sin, size):
    half = size // 2
    pieces = []
    for at in range(0, values.shape[0], size):
        lead, trail = values[at : at + half], values[at + half : at + size]
        pieces += [lead * cos - trail * sin, trail * cos + lead * sin]
    return jnp.concatenate(pieces, 0)


def key_bias(first, count, c, pos):
    tok = pos.shape[1]
    keys = lax.broadcasted_iota(jnp.int32, (count, tok), 0) + first
    queries = lax.broadcasted_iota(jnp.int32, (count, tok), 1) + c * tok
    allowed = (keys <= queries) & (keys >= queries - pos[...])
    return jnp.where(allowed, 0.0, MASK_FILL)


def front_body(
    lines, step,
    inp, cot, v0, v1, v2, v3, v4, pos, cos_r, sin_r, wq, wk, wv, wo,
    wp_o, wo_o, gains_o, n1_o, q_o, kv_o, cot_o, att_o, lse_o, hid_o, n2_o,
    kv, small, small_g, ms, mr, gs, gr, ks, kr, ts, tr,
):
    place = where_am_i()
    c, f, _, m, n = place
    far = (m + 2) % 4
    greet(line_devices(place, lines) + [(c, m), (c, n), (c, far)])
    tok, _ = inp.shape
    depth, query_width = wq.shape
    key_width = wk.shape[1]
    group = H // KV
    scale = HD ** (-0.5)

    def rows(g):
        return pl.ds(pl.multiple_of(g * depth, 16), depth)

    small[...] = jnp.zeros_like(small)
    for k, v in enumerate((v0, v1, v2, v3, v4)):
        small[k : k + 1, : v.shape[0]] = v[...].astype(f32).reshape(1, v.shape[0])
    smalls = [remote(small, small_g.at[f], ms.at[k], mr.at[k], (c, g)) for k, g in enumerate((m, n, far))]
    for copy in smalls:
        copy.start()
    project = [
        (wq, lambda g: wp_o.at[rows(g), pl.ds(0, query_width)]),
        (wk, lambda g: wp_o.at[rows(g), pl.ds(query_width, key_width)]),
        (wv, lambda g: wp_o.at[rows(g), pl.ds(query_width + key_width, key_width)]),
    ]
    output = [(wo, lambda g: wo_o.at[rows(g)])]
    gather_start(project, gs.at[pl.ds(0, 3)], gr.at[pl.ds(0, 3)], place)
    values = inp[...].astype(f32)
    unit = values * lax.rsqrt(jnp.mean(values * values, -1, keepdims=True) + EPSILON)
    small_g[f] = small[...]
    for k, g in enumerate((m, n, far)):
        remote(small, small_g.at[g], ms.at[k], mr.at[k], (c, g)).wait()

    def vector(row, size):
        return jnp.concatenate([small_g[g, row : row + 1, :size] for g in range(4)], 1)

    gains_o[0:1] = vector(0, depth)
    gains_o[1:2] = vector(1, depth)
    bias = jnp.concatenate([vector(2, depth), vector(3, key_width // 4), vector(4, key_width // 4)], 1)
    normed = unit * gains_o[0:1]
    n1_o[...] = normed.T.astype(bf16)
    gather_start(output, gs.at[pl.ds(3, 1)], gr.at[pl.ds(3, 1)], place)
    gather_finish(project, gs.at[pl.ds(0, 3)], gr.at[pl.ds(0, 3)], place)
    projected = plain_dot(normed.astype(bf16), wp_o[...]) + bias
    cos, sin = cos_r[...], sin_r[...]
    keys = turn(projected[:, query_width : query_width + key_width].T, cos, sin, HD)
    kv[:, :key_width] = keys.T.astype(bf16)
    kv[:, key_width:] = projected[:, query_width + key_width :].astype(bf16)
    spread_start(kv, kv_o, ks, kr, place, lines)
    kv_o[c] = kv[...]
    q_o[...] = turn(projected[:, :query_width].T, cos, sin, HD).astype(bf16)
    items = [(cot, lambda g, at: cot_o.at[g, at])]
    tokens_start(items, ts, tr, place)
    gather_finish(output, gs.at[pl.ds(3, 1)], gr.at[pl.ds(3, 1)], place)
    spread_finish(kv, kv_o, ks, kr, place, lines)
    for g in range(KV):
        queries = heads(q_o, g, group, HD)

        def visit(i, state):
            highest, total, acc = state
            at = pl.ds(i * step, step)
            both = kv_o[at].reshape(step * tok, 2 * key_width)
            seen = both[:, g * HD : (g + 1) * HD]
            carried = both[:, key_width + g * HD : key_width + (g + 1) * HD]
            mask = key_bias(i * step * tok, step * tok, c, pos)
            scores = plain_dot(seen, queries) * scale + jnp.concatenate([mask] * group, 1)
            top = jnp.maximum(highest, jnp.max(scores, 0, keepdims=True))
            exps = jnp.exp(scores - top)
            shrink = jnp.exp(highest - top)
            total = total * shrink + jnp.sum(exps, 0, keepdims=True)
            acc = acc * shrink + over_first(carried, exps.astype(bf16))
            return top, total, acc

        state = (
            jnp.full((1, group * tok), MASK_FILL, f32),
            jnp.zeros((1, group * tok), f32),
            jnp.zeros((HD, group * tok), f32),
        )
        blocks = kv_o.shape[0] // step
        if blocks <= 2:
            for i in range(blocks):
                state = visit(i, state)
        else:
            state = lax.fori_loop(0, blocks, visit, state)
        highest, total, acc = state
        attention = acc / total
        logs = highest + jnp.log(total)
        for j in range(group):
            at = slice(j * tok, (j + 1) * tok)
            h = g * group + j
            att_o[h * HD : (h + 1) * HD] = attention[:, at]
            lse_o[h : h + 1] = logs[:, at]
    hidden = values + plain_dot(att_o[...].T.astype(bf16), wo_o[...])
    hid_o[...] = hidden
    inverse = lax.rsqrt(jnp.mean(hidden * hidden, -1, keepdims=True) + EPSILON)
    n2_o[...] = (hidden * inverse * gains_o[1:2]).astype(bf16)
    tokens_finish(items, ts, tr, place)


def heads(ref, g, group, size):
    return jnp.concatenate([ref[pl.ds((g * group + j) * size, size)] for j in range(group)], 1)


def turn_back(grads, cos, sin, size):
    half = size // 2
    pieces = []
    for at in range(0, grads.shape[0], size):
        lead, trail = grads[at : at + half], grads[at + half : at + size]
        pieces += [lead * cos + trail * sin, trail * cos - lead * sin]
    return jnp.concatenate(pieces, 0)


def norm_grad(values, gain, grads):
    inverse = lax.rsqrt(jnp.mean(values * values, -1, keepdims=True) + EPSILON)
    scaled = values * inverse
    weighted = grads * gain
    back = inverse * (weighted - scaled * jnp.mean(weighted * scaled, -1, keepdims=True))
    return back, jnp.sum(grads * scaled, 0, keepdims=True)


def back_body(
    ctx, step,
    gn, hid, gains, cot, wo, att_t, q_t, kv, pos, lse, cos_r, sin_r, n1_t, inp, wp,
    inp_o, sums_o,
    gh, do_t, part, dq, held, ghl, ghl_g, low_t, n1_g, low_g, gp, gp_g, vec, vec_g,
    ks, kr, ts, tr, as_, ar, vs, vr,
):
    place = where_am_i()
    c, f, _, m, n = place
    far = (m + 2) % 4
    peers = [lax.rem(c + k, ctx) for k in range(1, ctx)]
    greet([(p, f) for p in peers] + [(c, m), (c, n), (c, far)])
    tok, width = cot.shape
    group = H // KV
    depth = n1_g.shape[1]
    scale = HD ** (-0.5)

    def rows(g):
        return pl.ds(pl.multiple_of(g * depth, 16), depth)

    def swaps():
        return [
            remote(src.at[rows(g)], dst.at[f], as_.at[j, k], ar.at[j, k], (c, g))
            for j, (src, dst) in enumerate(((n1_t, n1_g), (low_t, low_g)))
            for k, g in enumerate((n, far, m))
        ]

    low_t[...] = att_t[...].astype(bf16)
    back, gain_two = norm_grad(hid[...], gains[1:2], gn[...])
    gh[...] = cot[...].astype(f32) + back
    ghl[...] = gh[...].astype(bf16)
    items = [(ghl, lambda g, at: ghl_g.at[g, at])]
    tokens_start(items, ts.at[0], tr.at[0], place)
    for copy in swaps():
        copy.start()
    n1_g[f] = n1_t[rows(f)]
    low_g[f] = low_t[rows(f)]
    do_t[...] = over_last(wo[...], ghl[...]).astype(bf16)
    key_width = KV * HD
    for g in range(KV):
        queries, grads = heads(q_t, g, group, HD), heads(do_t, g, group, HD)
        delta = jnp.sum(grads.astype(f32) * heads(att_t, g, group, HD), 0, keepdims=True)
        total = jnp.concatenate([lse[pl.ds(g * group + j, 1)] for j in range(group)], 1)

        @pl.loop(0, kv.shape[0] // step)
        def _(i):
            at = pl.ds(i * step, step)
            both = kv[at].reshape(step * tok, 2 * key_width)
            keys = both[:, g * HD : (g + 1) * HD]
            values = both[:, key_width + g * HD : key_width + (g + 1) * HD]
            bias = key_bias(i * step * tok, step * tok, c, pos)
            scores = plain_dot(keys, queries) * scale + jnp.concatenate([bias] * group, 1)
            probs = jnp.exp(scores - total)
            g_probs = plain_dot(values, grads)
            g_scores = (probs * (g_probs - delta)).astype(bf16)
            g_keys = over_last(g_scores, queries) * scale
            g_values = over_last(probs.astype(bf16), grads)
            part[at, :, g * HD : (g + 1) * HD] = g_keys.astype(bf16).reshape(step, tok, HD)
            part[at, :, key_width + g * HD : key_width + (g + 1) * HD] = g_values.astype(bf16).reshape(
                step, tok, HD
            )
            g_queries = over_first(keys, g_scores) * scale

            @pl.when(i == 0)
            def _():
                dq[g] = g_queries

            @pl.when(i > 0)
            def _():
                dq[g] += g_queries

    owners = [remote(part.at[p], held.at[k], ks.at[k], kr.at[k], (p, f)) for k, p in enumerate(peers)]
    for copy in owners:
        copy.start()
    tokens_finish(items, ts.at[0], tr.at[0], place)
    for copy in swaps():
        copy.wait()
    cos, sin = cos_r[...], sin_r[...]
    g_q = [
        turn_back(dq[g, :, j * tok : (j + 1) * tok], cos, sin, HD) for g in range(KV) for j in range(group)
    ]
    g_q = jnp.concatenate(g_q, 0)
    query_width = g_q.shape[0]
    gp[:, :query_width] = g_q.T.astype(bf16)
    columns = gp.shape[1]
    low_all = jnp.concatenate([low_g[g] for g in range(4)], 1)
    sums_o[pl.ds(0, depth), pl.ds(columns, width)] = plain_dot(low_all, ghl_g[...].reshape(4 * tok, width)).astype(
        bf16
    )
    pairs = part[c].astype(f32)
    for k, copy in enumerate(owners):
        copy.wait()
        pairs = pairs + held[k].astype(f32)
    g_k = turn_back(pairs[:, :key_width].T, cos, sin, HD)
    gp[:, query_width : query_width + key_width] = g_k.T.astype(bf16)
    gp[:, query_width + key_width :] = pairs[:, key_width:].astype(bf16)
    items = [(gp, lambda g, at: gp_g.at[g, at])]
    tokens_start(items, ts.at[1], tr.at[1], place)
    g_normed = over_last(gp[...], wp[...])
    values = inp[...].astype(f32)
    back, gain_one = norm_grad(values, gains[0:1], g_normed)
    inp_o[...] = (gh[...] + back).astype(bf16)
    vec[...] = jnp.zeros_like(vec)
    vec[0:1, :width] = gain_one
    vec[1:2, :width] = gain_two
    vec[2:3, :columns] = jnp.sum(gp[...].astype(f32), 0, keepdims=True)
    vectors = [remote(vec, vec_g.at[k], vs.at[k], vr.at[k], (c, g)) for k, g in enumerate((m, n, far))]
    for copy in vectors:
        copy.start()
    tokens_finish(items, ts.at[1], tr.at[1], place)
    n1_all = jnp.concatenate([n1_g[g] for g in range(4)], 1)
    sums_o[pl.ds(0, depth), pl.ds(0, columns)] = plain_dot(n1_all, gp_g[...].reshape(4 * tok, columns)).astype(bf16)
    total = vec[...]
    for k, copy in enumerate(vectors):
        copy.wait()
        total = total + vec_g[k]
    sums_o[pl.ds(depth, 16)] = jnp.concatenate([total, total], 0).astype(bf16)


def over_last(a, b):
    return lax.dot_general(a, b, (((1,), (1,)), ((), ())), preferred_element_type=f32)


def over_first(a, b):
    return lax.dot_general(a, b, (((0,), (0,)), ((), ())), preferred_element_type=f32)


def plain_dot(a, b):
    return jnp.dot(a, b, preferred_element_type=f32)


def hidden_units(x, cot, wg, wu, wd):
    return gates(over_last(wg, x), over_last(wu, x), over_last(wd, cot))


def hidden_body(
    chunk, block, x_h, c_h, wg_h, wu_h, wd_h, og_h, ou_h, od_h, xs, cs, wg, wu, wd, acc, in_sem, w_sem, out_sem
):
    rows = x_h.shape[0]
    steps, blocks, held = rows // chunk, wg.shape[0] // block, xs.shape[0] // chunk
    loads = [
        pltpu.make_async_copy(src, dst, w_sem.at[j])
        for j, (src, dst) in enumerate(((wg_h, wg), (wu_h, wu), (wd_h, wd)))
    ]

    def tokens(i):
        src = pl.ds(pl.multiple_of(i * chunk, chunk), chunk)
        dst = pl.ds(pl.multiple_of(i % held * chunk, chunk), chunk)
        return [
            pltpu.make_async_copy(x_h.at[src], xs.at[dst], in_sem.at[i % held, 0]),
            pltpu.make_async_copy(c_h.at[src], cs.at[dst], in_sem.at[i % held, 1]),
        ]

    def results(b, slot):
        at = pl.ds(pl.multiple_of(b * block, 16), block)
        return [
            pltpu.make_async_copy(acc.at[slot, j], out.at[at], out_sem.at[slot, j])
            for j, out in enumerate((og_h, ou_h, od_h))
        ]

    resident = held == steps
    for copy in tokens(0) + loads:
        copy.start()
    for i in range(1, held if resident else 1):
        for copy in tokens(i):
            copy.start()
    for copy in loads:
        copy.wait()
    slots = acc.shape[0]

    @pl.loop(0, blocks)
    def _(b):
        slot = b % slots
        at = pl.ds(pl.multiple_of(b * block, 16), block)

        @pl.when(b >= slots)
        def _():
            for copy in results(b - slots, slot):
                copy.wait()

        @pl.loop(0, steps)
        def _(i):
            if resident:

                @pl.when(b == 0)
                def _():
                    for copy in tokens(i):
                        copy.wait()

            else:
                for copy in tokens(i):
                    copy.wait()

                @pl.when((i + 1 < steps) | (b + 1 < blocks))
                def _():
                    for copy in tokens(lax.rem(i + 1, steps)):
                        copy.start()

            t = pl.ds(pl.multiple_of(i % held * chunk, chunk), chunk)
            x, cot = xs[t], cs[t]
            act, g_gate, g_up = hidden_units(x, cot, wg[at], wu[at], wd[at])

            @pl.when(i == 0)
            def _():
                acc[slot, 0] = plain_dot(g_gate, x)
                acc[slot, 1] = plain_dot(g_up, x)
                acc[slot, 2] = plain_dot(act, cot)

            @pl.when(i > 0)
            def _():
                acc[slot, 0] += plain_dot(g_gate, x)
                acc[slot, 1] += plain_dot(g_up, x)
                acc[slot, 2] += plain_dot(act, cot)

        for copy in results(b, slot):
            copy.start()

    for b in range(max(0, blocks - slots), blocks):
        for copy in results(b, b % slots):
            copy.wait()


def hidden_grads(x, cot, wg, wu, wd):
    rows, width = x.shape
    units = wg.shape[0]
    chunk = math.gcd(rows, 1024)
    block = units // 2
    held = min(rows // chunk, 4)
    any_spec = pl.BlockSpec(memory_space=pl.ANY)
    dma = pltpu.SemaphoreType.DMA
    return pl.pallas_call(
        functools.partial(hidden_body, chunk, block),
        out_shape=(jax.ShapeDtypeStruct((units, width), f32),) * 3,
        in_specs=[any_spec] * 5,
        out_specs=(any_spec,) * 3,
        scratch_shapes=[pltpu.VMEM((held * chunk, width), bf16)] * 2
        + [pltpu.VMEM((units, width), bf16)] * 3
        + [pltpu.VMEM((2, 3, block, width), f32), dma((held, 2)), dma((3,)), dma((2, 3))],
        compiler_params=pltpu.CompilerParams(vmem_limit_bytes=62 << 20),
        cost_estimate=pl.CostEstimate(
            flops=12 * rows * width * units, bytes_accessed=4 * rows * width + 18 * units * width, transcendentals=0
        ),
        name="hidden_grads",
    )(x, cot, wg, wu, wd)


def shards(
    layer_input,
    seq_ids,
    positions,
    norm_gain,
    w_query,
    b_query,
    w_key,
    b_key,
    w_value,
    b_value,
    w_output,
    mlp_gain,
    w_gate,
    w_up,
    w_down,
    cotangent,
):
    tok = layer_input.shape[1]
    width = layer_input.shape[2]
    group = H // KV
    query_width = H * HD
    key_width = KV * HD
    ctx = lax.axis_size("ctx")
    fsdp = lax.axis_size("fsdp")
    depth = width // fsdp
    lines = ctx // 2
    c, f = lax.axis_index("ctx"), lax.axis_index("fsdp")
    dma = pltpu.SemaphoreType.DMA
    sds = jax.ShapeDtypeStruct
    input_rows = layer_input[0]
    grad_out = cotangent[0]
    own_positions = positions[0]
    query_rows = c * tok + jnp.arange(tok, dtype=jnp.int32)

    cot_all = lax.all_gather(grad_out, ("ctx", "fsdp"), axis=0, tiled=True)

    cosine, sine_table = rope_tables(own_positions, HD)
    own_positions = own_positions[None]
    step = math.gcd(ctx, 4)
    columns = query_width + 2 * key_width
    hbm = pl.BlockSpec(memory_space=pltpu.HBM)
    (w_project, wo_full, gains, n1_t, q_t, kv_all, cot_group, att_t, log_total, hidden_state, normed_second) = (
        pl.pallas_call(
            functools.partial(front_body, lines, step),
            out_shape=(
                sds((width, columns), bf16),
                sds((query_width, width), bf16),
                sds((8, width), f32),
                sds((width, tok), bf16),
                sds((query_width, tok), bf16),
                sds((ctx, tok, 2 * key_width), bf16),
                sds((fsdp, tok, width), bf16),
                sds((query_width, tok), f32),
                sds((H, tok), f32),
                sds((tok, width), f32),
                sds((tok, width), bf16),
            ),
            in_specs=[VMEM] * 10 + [hbm] * 4,
            out_specs=(VMEM,) * 11,
            scratch_shapes=[
                pltpu.VMEM((tok, 2 * key_width), bf16),
                pltpu.VMEM((8, 256), f32),
                pltpu.VMEM((fsdp, 8, 256), f32),
                dma((3,)),
                dma((3,)),
            ]
            + gather_sems(4)
            + [dma((2, lines)), dma((2, lines))]
            + gather_sems(1),
            compiler_params=pltpu.CompilerParams(
                collective_id=0, has_side_effects=True, vmem_limit_bytes=62 << 20
            ),
            cost_estimate=pl.CostEstimate(flops=4 * 10**9, bytes_accessed=10**7, transcendentals=0),
            name="front",
        )(
            input_rows, grad_out, norm_gain, mlp_gain, b_query, b_key, b_value, own_positions, cosine, sine_table,
            w_query, w_key, w_value, w_output,
        )
    )
    units = w_down.shape[0]
    any_spec = pl.BlockSpec(memory_space=pltpu.HBM)
    wg_t, wu_t = w_gate.T, w_up.T
    grad_normed2, block_out, x_all = pl.pallas_call(
        functools.partial(mid_body, lines),
        out_shape=(
            sds((tok, width), f32),
            sds((tok, width), bf16),
            sds((ctx, fsdp, tok, width), bf16),
        ),
        in_specs=[VMEM, VMEM, VMEM, any_spec, any_spec, any_spec],
        out_specs=(VMEM, VMEM, any_spec),
        scratch_shapes=[pltpu.VMEM((fsdp, tok, width), bf16)]
        + [pltpu.VMEM((units, width), bf16)] * 3
        + [
            pltpu.VMEM((3, 2 * tok, units), bf16),
            pltpu.VMEM((2, tok, width), f32),
            pltpu.VMEM((8, tok, width), bf16),
            pltpu.VMEM((2, tok, width), bf16),
            pltpu.VMEM((2, tok, width), bf16),
            dma((3,)),
            dma,
            dma((5,)),
            dma((5,)),
            dma((6,)),
            dma((6,)),
        ]
        + spread_sems(lines),
        compiler_params=pltpu.CompilerParams(
            collective_id=2, has_side_effects=True, vmem_limit_bytes=62 << 20
        ),
        cost_estimate=pl.CostEstimate(
            flops=12 * fsdp * tok * width * units, bytes_accessed=6 * units * width, transcendentals=0
        ),
        name="mid",
    )(normed_second, cot_group, hidden_state, wg_t, wu_t, w_down)
    block_out = block_out[None]
    x_all = x_all.reshape(ctx * fsdp * tok, width)
    params = pltpu.CompilerParams(collective_id=3, has_side_effects=True, vmem_limit_bytes=62 << 20)
    input_grad, weight_grads = pl.pallas_call(
        functools.partial(back_body, ctx, step),
        out_shape=(sds((tok, width), bf16), sds((depth + 16, columns + width), bf16)),
        in_specs=[VMEM] * 15,
        out_specs=(VMEM, VMEM),
        scratch_shapes=[
            pltpu.VMEM((tok, width), f32),
            pltpu.VMEM((query_width, tok), bf16),
            pltpu.VMEM((ctx, tok, 2 * key_width), bf16),
            pltpu.VMEM((KV, HD, group * tok), f32),
            pltpu.VMEM((ctx - 1, tok, 2 * key_width), bf16),
            pltpu.VMEM((tok, width), bf16),
            pltpu.VMEM((fsdp, tok, width), bf16),
            pltpu.VMEM((query_width, tok), bf16),
            pltpu.VMEM((fsdp, depth, tok), bf16),
            pltpu.VMEM((fsdp, depth, tok), bf16),
            pltpu.VMEM((tok, columns), bf16),
            pltpu.VMEM((fsdp, tok, columns), bf16),
            pltpu.VMEM((8, columns + width), f32),
            pltpu.VMEM((3, 8, columns + width), f32),
            dma((ctx - 1,)),
            dma((ctx - 1,)),
            dma((2, 1, 6)),
            dma((2, 1, 6)),
            dma((2, 3)),
            dma((2, 3)),
            dma((3,)),
            dma((3,)),
        ],
        compiler_params=params,
        cost_estimate=pl.CostEstimate(flops=10**10, bytes_accessed=10**7, transcendentals=0),
        name="back",
    )(
        grad_normed2,
        hidden_state,
        gains,
        grad_out,
        wo_full,
        att_t,
        q_t,
        kv_all,
        own_positions,
        log_total,
        cosine,
        sine_table,
        n1_t,
        input_rows,
        w_project,
    )
    input_grad = input_grad[None]
    weight_grads = lax.psum(weight_grads, "ctx")
    weight_grads = weight_grads.astype(f32)
    starts = ((0, 0, width), (1, 0, width), (2, 0, query_width), (2, query_width, key_width),
              (2, query_width + key_width, key_width))

    def piece(row, start, size):
        share = size // fsdp
        return lax.dynamic_slice_in_dim(weight_grads[depth + row], start + f * share, share, 0)

    own = [piece(*at) for at in starts]
    weight_grads = weight_grads[:depth]

    gate_grad, up_grad, down_grad = hidden_grads(x_all, cot_all, wg_t, wu_t, w_down)
    return (
        block_out,
        input_grad,
        own[0],
        weight_grads[:, :query_width],
        own[2],
        weight_grads[:, query_width : query_width + key_width],
        own[3],
        weight_grads[:, query_width + key_width : query_width + 2 * key_width],
        own[4],
        weight_grads[:, query_width + 2 * key_width :],
        own[1],
        gate_grad.T,
        up_grad.T,
        down_grad,
        log_total[None],
    )


def solution(mesh):
    in_specs = (
        P("fsdp", "ctx", None),
        P("fsdp", "ctx"),
        P("fsdp", "ctx"),
        P("fsdp"),
        P("fsdp", None),
        P("fsdp"),
        P("fsdp", None),
        P("fsdp"),
        P("fsdp", None),
        P("fsdp"),
        P("fsdp", None),
        P("fsdp"),
        P(None, "fsdp"),
        P(None, "fsdp"),
        P("fsdp", None),
        P("fsdp", "ctx", None),
    )
    out_specs = (
        P("fsdp", "ctx", None),
        P("fsdp", "ctx", None),
        P("fsdp"),
        P("fsdp", None),
        P("fsdp"),
        P("fsdp", None),
        P("fsdp"),
        P("fsdp", None),
        P("fsdp"),
        P("fsdp", None),
        P("fsdp"),
        P(None, "fsdp"),
        P(None, "fsdp"),
        P("fsdp", None),
        P("fsdp", None, "ctx"),
    )

    return jax.shard_map(shards, mesh=mesh, in_specs=in_specs, out_specs=out_specs, check_vma=False)
```

time: 476 us -> 328 us (0.69)
  waiting for transfers between devices: 216 us -> 92.8 us
  Pallas kernels: 168 us -> 209 us
  local copies, waits for them, and re-layouts: 35.9 us -> 8.67 us
  matrix products: 22.5 us -> 0 us
  other arithmetic: 16 us -> 1.43 us
    all_gather x1, waiting for transfers between devices: 74.5 us -> 0.01 us  [shards(): cot_all = lax.all_gather(grad_out, ('ctx', 'fsdp'), axis=0, tiled=True)]
    all_gather x1 -> x0, waiting for transfers between devices: 66.3 us -> none  [shards(): x_all = lax.all_gather(normed_second, ('ctx', 'fsdp'), axis=0, tiled=True)]
    pallas_call x5 -> x3, Pallas kernels: 90.6 us -> 131 us  [the longest x1 51.3 us: shards(): pl.pallas_call(functools.partial(mid_body, lines), out_shape=(sds((tok, w...]
    dot_general x12 -> x0, matrix products: 22.5 us -> none  [the longest x1 5.7 us: shards(): jnp.einsum('tkgd,nkd->kgtn', grad_attention, values, preferred_element_ty...]
    psum x1, waiting for transfers between devices: 73.7 us -> 92.5 us  [shards(): weight_grads = lax.psum(weight_grads, 'ctx')]
    unnamed x115 -> x9, local copies, waits for them, and re-layouts: 14.9 us -> 1.99 us
    slice x17 -> x1, local copies, waits for them, and re-layouts: 6.6 us -> 0.89 us  [piece(): weight_grads[depth + row]]
    convert_element_type x7 -> x0, local copies, waits for them, and re-layouts: 5.13 us -> none  [the longest x2 2.12 us: shards(): residual_in = input_rows.astype(f32)]
  transfers between devices with their start and end apart: 4 -> 2, of which waited for: 3 -> 1; matrix products, arithmetic and copies ran while one was open for 2% -> 2% of each run, Pallas kernels for 0% -> 0%
where the time goes in v2:
time: 328 us; the launch traced here: 327 us
  Pallas kernels  209 us (64%)
  waiting for transfers between devices  92.8 us (28%)
  between operations  15.6 us (5%)
  local copies, waits for them, and re-layouts  8.67 us (3%)
    psum x1, waiting for transfers between devices, shards(): weight_grads = lax.psum(weight_grads, 'ctx')  92.5 us
    pallas_call x1, Pallas kernels, hidden_grads(): pl.pallas_call(functools.partial(hidden_body, chunk, block), out_shape=(j...  77.6 us
    pallas_call x1, Pallas kernels, shards(): pl.pallas_call(functools.partial(mid_body, lines), out_shape=(sds((tok, w...  51.3 us
    pallas_call x1, Pallas kernels, shards(): pl.pallas_call(functools.partial(front_body, lines, step), out_shape=(sds...  44.7 us
    pallas_call x1, Pallas kernels, shards(): pl.pallas_call(functools.partial(back_body, ctx, step), out_shape=(sds((t...  35 us
  transfers between devices with their start and end apart: 2, of which 1 were waited for; matrix products, arithmetic and copies ran while one was open for 2% of the time, Pallas kernels for 0%

profile of v2, /device:TPU:0, one launch (start us, length us, event | category | flops | bytes accessed | tf_op | source)
XLA Modules:
  0.0 327.3 jit_solution(3893267492135637269)
XLA Ops:
  8.0 0.0 all-reduce.2.cloned.1.call-start
  8.1 0.7 convert_bitcast_fusion
  8.7 0.8 multiply_sine_fusion
  9.5 44.7 %front.1 = (bf16[896,1152]{1,0:T(8,128)(2,1)}, bf16[896,896]{1,0:T(8,128)(2,1)}, f32[8,896]{1,0:T(8,128)}, bf16[896,128]{1,0:T(8,128)(2,1)}, bf16[896,128]{1,0:T...) custom-call(bf16[128,896]{1,0:T(8,128)(2,1)} %bitcast.33, ...), custom_call_target="tpu_custom_call" | custom-call | flops 4000000000 | bytes 10000000 | tf_op jit(solution)/shard_map/front/pallas_call | solution.py:831
  54.2 51.3 %mid.1 = (f32[128,896]{1,0:T(8,128)}, bf16[128,896]{1,0:T(8,128)(2,1)}, bf16[8,4,128,896]{3,2,1,0:T(8,128)(2,1)}) custom-call(bf16[128,896]{1,0:T(8,128)(2,1)} %get-tuple-element.34.x, bf16[4,128,896]{2,1,0:T(8,128)(2,1)} %get-tuple-element.35.cot, f32[128,896]{1,0:T(8,128)} %get-tuple-element.36.hid, bf16[1216,896]{1,0:T(8,128)(2,1)} %bitcast.29, ...), custom_call_target="tpu_custom_call" | custom-call | flops 6694109184 | bytes 6537216 | tf_op jit(solution)/shard_map/mid/pallas_call | solution.py:871
  105.5 0.0 copy-start.2
  105.5 35.0 %back.1 = (bf16[128,896]{1,0:T(8,128)(2,1)}, bf16[240,2048]{1,0:T(8,128)(2,1)}) custom-call(f32[128,896]{1,0:T(8,128)} %get-tuple-element.38.gn, f32[128,896]{1,0:T(8,128)} %get-tuple-element.36.hid, f32[8,896]{1,0:T(8,128)} %get-tuple-element.39.gains, bf16[128,896]{1,0:T(8,128)(2,1)} %bitcast.21, bf16[896,896]{1,0:T(8,128)(2,1)} %get-tuple-element.40.wo, ...), custom_call_target="tpu_custom_call" | custom-call | flops 10000000000 | bytes 10000000 | tf_op jit(solution)/shard_map/back/pallas_call | solution.py:907
  140.5 0.0 all-reduce.2.cloned.1.call-update
  140.5 0.3 all-gather.3.cloned.1.call-start
  140.8 0.3 all-gather.3.cloned.1.call-update
  141.1 0.0 copy-done.2
  141.1 0.6 copy.30
  141.7 92.5 %all-reduce.2.cloned.1.call-done = bf16[240,2048]{1,0:T(8,128)(2,1)} async-done(((bf16[240,2048]{1,0:T(8,128)(2,1)}), bf16[240,2048]{1,0:T(8,128)(2,1)}) %all-reduce.2.cloned.1.call-update) | async-done | bytes 983056 | tf_op jit(solution)/shard_map/psum | solution.py:957
  234.2 0.9 fusion.2
  235.1 0.6 constant_dynamic-slice_fusion.4
  235.7 0.6 fusion.1
  236.3 0.6 constant_dynamic-slice_fusion
  237.0 1.5 fusion.4
  238.5 2.4 fusion.3
  240.9 0.0 all-gather.3.cloned.1.call-done
  240.9 0.0 copy-start
  240.9 0.0 copy-start.1
  240.9 77.6 %hidden_grads.1 = (f32[1216,896]{1,0:T(8,128)}, f32[1216,896]{1,0:T(8,128)}, f32[1216,896]{1,0:T(8,128)}) custom-call(bf16[4096,896]{1,0:T(8,128)(2,1)} %bitcast.35, bf16[4096,896]{1,0:T(8,128)(2,1)} %bitcast.28, bf16[1216,896]{1,0:T(8,128)(2,1)} %bitcast.30, bf16[1216,896]{1,0:T(8,128)(2,1)} %bitcast.32, bf16[1216,896]{1,0:T(8,128)(2,1)} %wd_h.3), custom_call_target="tpu_custom_call" | custom-call | flops 53552873472 | bytes 34291712 | tf_op jit(solution)/shard_map/hidden_grads/pallas_call | solution.py:772
  318.5 0.0 copy-done
  318.5 0.7 copy.34
  319.2 0.0 copy-done.1
  319.2 0.7 copy.35
  (1 shorter events, 0.0 us)
Async XLA Ops:
  8.0 226.2 %all-reduce.2.cloned.1.call-start = ((), (), s32[]{:S(2)}) async-start(), calls=%async_computation | async-start | bytes 1966080 | tf_op jit(solution)/shard_map/psum | solution.py:957
  105.5 35.6 %copy-start.2 = (f32[14,128]{1,0:T(8,128)S(1)}, f32[14,128]{1,0:T(8,128)}, u32[]{:S(2)}) copy-start(f32[14,128]{1,0:T(8,128)} %get-tuple-element.44.lse) | copy-start | bytes 21508
  140.5 100.3 %all-gather.3.cloned.1.call-start = ((), (), s32[]{:S(2)}) async-start(), calls=%async_computation.1 | async-start | bytes 7569408 | tf_op jit(solution)/shard_map/all_gather | solution.py:823
  240.9 77.6 %copy-start = (bf16[128,896]{1,0:T(8,128)(2,1)S(1)}, bf16[128,896]{1,0:T(8,128)(2,1)}, u32[]{:S(2)}) copy-start(bf16[128,896]{1,0:T(8,128)(2,1)} %get-tuple-element.37) | copy-start | bytes 688132
  240.9 78.3 %copy-start.1 = (bf16[128,896]{1,0:T(8,128)(2,1)S(1)}, bf16[128,896]{1,0:T(8,128)(2,1)}, u32[]{:S(2)}) copy-start(bf16[128,896]{1,0:T(8,128)(2,1)} %get-tuple-element.47) | copy-start | bytes 688132
Sparse Core Ops, SparseCore 0:
  140.7 93.4 all-reduce.1
Sparse Core Ops, SparseCore 1:
  143.9 79.2 all-gather.2

commit v3 on v2

--- a/solution.py
+++ b/solution.py
@@ -7,7 +7,6 @@
 from jax.experimental import pallas as pl
 from jax.experimental.pallas import tpu as pltpu
 from jax.sharding import PartitionSpec as P
-
 
 H = 14
 KV = 2
@@ -53,7 +52,7 @@
 
 
 def gather_start(items, ss, rs, place):
-    c, f, _, m, n = place
+    c, f, c2, m, n = place
     h = c % 2
     for i, (src, dst) in enumerate(items):
         half = src.shape[0] // 2
@@ -91,7 +90,7 @@
 
 
 def tokens_start(items, ss, rs, place):
-    c, f, _, m, n = place
+    c, f, c2, m, n = place
     for i, (src, dst) in enumerate(items):
         half = src.shape[0] // 2
         for j in range(2):
@@ -104,7 +103,7 @@
 
 
 def tokens_finish(items, ss, rs, place):
-    c, f, _, m, n = place
+    c, f, c2, m, n = place
     far = (m + 2) % 4
     for i, (src, dst) in enumerate(items):
         half = src.shape[0] // 2
@@ -125,8 +124,57 @@
     return [pltpu.SemaphoreType.DMA((count, 6)), pltpu.SemaphoreType.DMA((count, 6))]
 
 
+def staged_call(body, args, in_hbm, out_shape, out_hbm, scratch, ident, name, cost):
+    hbm = pl.BlockSpec(memory_space=pltpu.HBM)
+    staged_in = [i for i in range(len(args)) if i not in in_hbm]
+    staged_out = [i for i in range(len(out_shape)) if i not in out_hbm]
+
+    def kernel(*refs):
+        ins, outs = list(refs[: len(args)]), list(refs[len(args) : len(args) + len(out_shape)])
+        rest = list(refs[len(args) + len(out_shape) :])
+        own, rest = rest[: len(scratch)], rest[len(scratch) :]
+        in_sem, out_sem = rest[-2:]
+        copies_in, copies_out = [], []
+        for j, i in enumerate(staged_in):
+            buffer = rest.pop(0)
+            copies_in.append(pltpu.make_async_copy(ins[i], buffer, in_sem.at[j]))
+            ins[i] = buffer
+        for j, i in enumerate(staged_out):
+            buffer = rest.pop(0)
+            copies_out.append(pltpu.make_async_copy(buffer, outs[i], out_sem.at[j]))
+            outs[i] = buffer
+        for copy in copies_in:
+            copy.start()
+
+        def ready():
+            for copy in copies_in:
+                copy.wait()
+
+        body(ready, *ins, *outs, *own)
+        for copy in copies_out:
+            copy.start()
+        for copy in copies_out:
+            copy.wait()
+
+    buffers = [pltpu.VMEM(args[i].shape, args[i].dtype) for i in staged_in]
+    buffers += [pltpu.VMEM(out_shape[i].shape, out_shape[i].dtype) for i in staged_out]
+    sems = [pltpu.SemaphoreType.DMA((len(staged_in),)), pltpu.SemaphoreType.DMA((len(staged_out),))]
+    return pl.pallas_call(
+        kernel,
+        out_shape=out_shape,
+        in_specs=[hbm] * len(args),
+        out_specs=(hbm,) * len(out_shape),
+        scratch_shapes=scratch + buffers + sems,
+        compiler_params=pltpu.CompilerParams(
+            collective_id=ident, has_side_effects=True, vmem_limit_bytes=62 << 20
+        ),
+        cost_estimate=cost,
+        name=name,
+    )(*args)
+
+
 def spread_start(src, dst, ss, rs, place, lines):
-    c, f, c2, _, _ = place
+    c, f, c2, m, n = place
     for k in range(1, lines):
         p = lax.rem(c // 2 + k, lines) * 2 + c % 2
         remote(src, dst.at[c], ss.at[0, k], rs.at[0, k], (p, f)).start()
@@ -134,7 +182,7 @@
 
 
 def spread_finish(src, dst, ss, rs, place, lines):
-    c, f, c2, _, _ = place
+    c, f, c2, m, n = place
     for k in range(1, lines):
         giver = lax.rem(c // 2 + lines - k, lines) * 2 + c % 2
         block = dst.at[giver]
@@ -148,7 +196,7 @@
 
 
 def line_devices(place, lines):
-    c, f, c2, _, _ = place
+    c, f, c2, m, n = place
     return [(lax.rem(c // 2 + k, lines) * 2 + c % 2, f) for k in range(1, lines)] + [(c2, f)]
 
 
@@ -162,18 +210,14 @@
 
 
 class Spread:
-    def __init__(self, place, lines, x, group, full, sems):
-        self.place, self.lines, self.x, self.group, self.full = place, lines, x, group, full
+    def __init__(self, place, lines, x, group, into, sems):
+        self.place, self.lines, self.x, self.group, self.into = place, lines, x, group, into
         self.half = x.shape[0] // 2
-        self.line_s, self.line_r, self.pair_s, self.pair_r, self.y_s, self.y_r, self.mate_s, self.mate_r = sems
-
-    def column(self, k):
-        c = self.place[0]
-        return lax.rem(c // 2 + self.lines - k, self.lines) * 2 + c % 2
-
-    def ahead(self, k):
-        c = self.place[0]
-        return lax.rem(c // 2 + k, self.lines) * 2 + c % 2
+        self.core = place[1] % 2
+        self.line_s, self.line_r, self.pair_s, self.pair_r, self.y_s, self.y_r, self.mate_s, self.mate_r, self.own = sems
+
+    def at(self, k):
+        return lax.rem(self.place[0] // 2 + self.lines - k, self.lines)
 
     def each(self, first, act):
         if self.lines <= 4:
@@ -182,123 +226,115 @@
         else:
             pl.loop(first, self.lines)(act)
 
-    def view(self, b, g, j):
-        return self.full.at[b, g, pl.ds(j * self.half, self.half)]
-
     def source(self, way):
-        _, _, _, _, n = self.place
+        n = self.place[4]
         rows = pl.ds((0 if way == 0 else 1) * self.half, self.half)
         return self.x.at[rows] if way < 2 else self.group.at[n, rows]
 
-    def slot(self, b, way):
-        _, f, _, _, n = self.place
-        return self.view(b, n if way == 2 else f, 0 if way == 0 else 1)
+    def slot(self, way, side, k, core=None):
+        return self.into[(0, 1, 3, 2)[way]][side].at[self.at(k), self.core if core is None else core]
 
     def line(self, way, k):
-        c, f, _, _, _ = self.place
-        return remote(
-            self.source(way), self.slot(c, way), self.line_s.at[way, k], self.line_r.at[way, k], (self.ahead(k), f)
-        )
+        c, f = self.place[:2]
+        sems = self.line_s.at[way, k], self.line_r.at[way, k]
+        device = (lax.rem(c // 2 + k, self.lines) * 2 + c % 2, f)
+        return remote(self.source(way), self.slot(way, 0, 0), *sems, device)
 
     def arrived(self, way, k):
-        here = self.slot(self.column(k), way)
-        f = self.place[1]
-        return remote(here, here, self.line_s.at[way, k], self.line_r.at[way, k], (self.ahead(k), f))
+        here = self.slot(way, 0, k)
+        c, f, c2 = self.place[:3]
+        return remote(here, here, self.line_s.at[way, k], self.line_r.at[way, k], (c2, f))
 
     def pair(self, way, k):
-        c, f, c2, _, _ = self.place
-        here = self.slot(self.column(k), way) if not isinstance(k, int) or k else None
-        src = self.source(way) if here is None else here
-        dst = self.slot(c, way) if here is None else here
-        return remote(src, dst, self.pair_s.at[way, k], self.pair_r.at[way, k], (c2, f))
-
-    def other(self, k):
-        b = self.column(k)
-        return b + 1 - 2 * (b % 2)
-
-    def paired(self, way, k):
-        _, f, c2, _, _ = self.place
-        here = self.slot(self.other(k), way)
-        return remote(here, here, self.pair_s.at[way, k], self.pair_r.at[way, k], (c2, f))
-
-    def block(self, side, k):
-        return self.other(k) if side else self.column(k)
+        c, f, c2 = self.place[:3]
+        src = self.source(way) if isinstance(k, int) and k == 0 else self.slot(way, 0, k)
+        return remote(src, self.slot(way, 1, k), self.pair_s.at[way, k], self.pair_r.at[way, k], (c2, f))
 
     def across(self, side, k):
-        c, _, _, _, n = self.place
-        here = self.slot(self.block(side, k), 0)
-        return remote(here, here, self.y_s.at[side, k], self.y_r.at[side, k], (c, n))
-
-    def crossed(self, side, k):
-        c, _, _, _, n = self.place
-        here = self.view(self.block(side, k), n, 0)
-        return remote(here, here, self.y_s.at[side, k], self.y_r.at[side, k], (c, n))
-
-    def hand(self, way, side, k):
-        c, _, _, m, n = self.place
-        b = self.block(side, k)
-        here = self.view(b, n, 0) if way == 3 else self.slot(b, way)
+        c, n = self.place[0], self.place[4]
+        sems = self.y_s.at[side, k], self.y_r.at[side, k]
+        return remote(self.slot(0, side, k), self.slot(3, side, k), *sems, (c, n))
+
+    def hand(self, way, side, k, core=None):
+        c, m = self.place[0], self.place[3]
+        here = self.slot(way, side, k, core)
         return remote(here, here, self.mate_s.at[way, side, k], self.mate_r.at[way, side, k], (c, m))
 
-    def handed(self, way, side, k):
-        c, _, _, m, _ = self.place
-        far = (m + 2) % 4
-        b = self.block(side, k)
-        here = self.view(b, far if way > 1 else m, 1 if way in (1, 2) else 0)
-        return remote(here, here, self.mate_s.at[way, side, k], self.mate_r.at[way, side, k], (c, m))
-
-    def start(self, way):
+    def lines_out(self, way):
         self.each(1, lambda k: self.line(way, k).start())
-        self.pair(way, 0).start()
-
-    def on_line(self, way):
+
+    def on_line(self, way, forward):
         def act(k):
             self.arrived(way, k).wait_recv()
-            self.pair(way, k).start()
+            if forward:
+                self.pair(way, k).start()
             self.hand(way, 0, k).start()
-            if way == 0:
-                self.across(0, k).start()
-
+
+        if forward:
+            self.pair(way, 0).start()
         self.each(1, act)
+
+    def pairs_out(self, way):
+        self.pair(way, 0).start()
+        self.each(1, lambda k: self.pair(way, k).start())
 
     def on_pair(self, way):
         def act(k):
-            self.paired(way, k).wait_recv()
+            self.pair(way, k).wait_recv()
             self.hand(way, 1, k).start()
-            if way == 0:
-                self.across(1, k).start()
 
         self.each(0, act)
+
+    def cross(self, side):
+        self.each(1 - side, lambda k: self.across(side, k).start())
 
     def on_y(self, side):
         def act(k):
-            self.crossed(side, k).wait_recv()
+            self.across(side, k).wait_recv()
             self.hand(3, side, k).start()
 
         self.each(1 - side, act)
 
-    def finish(self):
-        for way in range(3):
-            self.each(1, lambda k: self.line(way, k).wait_send())
-            self.each(0, lambda k: self.pair(way, k).wait_send())
+    def keep(self, group, *parts):
+        c, f = self.place[:2]
+        copies = []
+        for part in parts:
+            pair = pl.ds((f // 2 if part < 2 else 1 - f // 2) * 2, 2)
+            rows = pl.ds(part % 2 * self.half, self.half)
+            into = self.into[part][0].at[c // 2]
+            copies.append(pltpu.make_async_copy(group.at[pair, rows], into, self.own.at[part]))
+        return copies
+
+    def handed(self, way, side):
+        self.each(1 - side, lambda k: self.hand(way, side, k).wait_send())
+        self.each(1 - side, lambda k: self.hand(way, side, k, 1 - self.core).wait_recv())
+
+    def finish_line(self, way):
+        self.each(1, lambda k: self.line(way, k).wait_send())
+        self.handed(way, 0)
+
+    def finish_pair(self, way):
+        self.each(0, lambda k: self.pair(way, k).wait_send())
+        self.handed(way, 1)
+
+    def finish_cross(self):
         for side in range(2):
             self.each(1 - side, lambda k: self.across(side, k).wait_send())
-            for way in range(4):
-                self.each(1 - side, lambda k: self.hand(way, side, k).wait_send())
-                self.each(1 - side, lambda k: self.handed(way, side, k).wait_recv())
+            self.handed(3, side)
 
 
 def spread_sems(lines):
     dma = pltpu.SemaphoreType.DMA
-    return [dma(shape) for shape in ((3, lines), (3, lines), (2, lines), (4, 2, lines)) for _ in range(2)]
+    return [dma(shape) for shape in ((3, lines), (3, lines), (2, lines), (4, 2, lines)) for _ in range(2)] + [dma((4,))]
 
 
 def mid_body(
-    lines, x, cot, hid, wg_h, wu_h, wd_h, gn_o, block_o, x_o,
-    xg, wg, wu, wd, act, back, near, sums, far_in, ws, os, ss, rs, ns, nr, *spread
+    lines, ready, x, cot, own_cot, a0, a1, b0, hid, wg_h, wu_h, wd_h,
+    gn_o, block_o, xg, b1_o, fa0_o, fa1_o, fb0_o, fb1_o, xa0_o,
+    wg, wu, wd, act, back, near, sums, far_in, ws, ss, rs, ns, nr, *sems
 ):
     place = where_am_i()
-    c, f, _, m, n = place
+    c, f, c2, m, n = place
     far = (m + 2) % 4
     tok, width = x.shape
     loads = [
@@ -308,15 +344,21 @@
     for copy in loads:
         copy.start()
     greet(line_devices(place, lines) + [(c, m), (c, n)])
+    ready()
     half = tok // 2
     own = remote(x, xg.at[f], ss.at[0], rs.at[0], (c, m))
     own.start()
     for j in range(2):
         rows = pl.ds(j * half, half)
         remote(x.at[rows], xg.at[f, rows], ss.at[1 + j], rs.at[1 + j], (c, n)).start()
-    everyone = Spread(place, lines, x, xg, x_o, spread)
-    everyone.start(0)
-    everyone.start(1)
+    rest = Spread(place, lines, own_cot, cot, ((a0, a1), (b0, b1_o), (fa0_o, fa1_o), (fb0_o, fb1_o)), sems[:9])
+    spread = Spread(place, lines, x, xg, ((xa0_o,),), sems[9:])
+    rest.pairs_out(1)
+    rest.lines_out(2)
+    spread.lines_out(0)
+    kept = rest.keep(cot, 2, 3)
+    for copy in kept:
+        copy.start()
     xg[f] = x[...]
     for copy in loads:
         copy.wait()
@@ -360,41 +402,45 @@
         here = xg.at[n, pl.ds(j * half, half)]
         remote(here, here, ss.at[1 + j], rs.at[1 + j], (c, n)).wait_recv()
         remote(here, here, ss.at[3 + j], rs.at[3 + j], (c, m)).start()
-    everyone.start(2)
+    rest.cross(0)
     give(0, backward())
     gn_o[...] = back[core]
     give(1, down())
     down_own = hid[...] + back[core]
-    everyone.on_line(0)
     for j in range(2):
         rows = pl.ds(j * half, half)
         remote(x.at[rows], xg.at[far, rows], ss.at[3 + j], rs.at[3 + j], (c, m)).wait_recv()
-    keep = pltpu.make_async_copy(xg, x_o.at[c], os)
-    keep.start()
+    kept += spread.keep(xg, 0)
+    kept[-1].start()
     forward(1 - y)
     give(2, backward())
     send_over(0, 2)
-    everyone.on_line(1)
+    rest.on_line(2, True)
     give(3, down())
     send_over(1, 3)
-    everyone.on_pair(0)
-    everyone.on_pair(1)
-    everyone.on_y(0)
+    rest.cross(1)
+    rest.on_y(0)
+    rest.on_pair(1)
     cross(0).wait()
     swap(0).wait()
     gn_o[...] += near[1].astype(f32) + far_in[0].astype(f32)
-    everyone.on_line(2)
     cross(1).wait()
     swap(1).wait()
     block_o[...] = (down_own + near[3].astype(f32) + far_in[1].astype(f32)).astype(bf16)
-    everyone.on_y(1)
-    everyone.on_pair(2)
+    spread.on_line(0, False)
+    rest.on_pair(2)
+    rest.on_y(1)
     for j in range(2):
         rows = pl.ds(j * half, half)
         remote(x.at[rows], xg.at[f, rows], ss.at[1 + j], rs.at[1 + j], (c, n)).wait_send()
         remote(x.at[rows], xg.at[far, rows], ss.at[3 + j], rs.at[3 + j], (c, m)).wait_send()
-    keep.wait()
-    everyone.finish()
+    for copy in kept:
+        copy.wait()
+    rest.finish_pair(1)
+    rest.finish_line(2)
+    rest.finish_pair(2)
+    rest.finish_cross()
+    spread.finish_line(0)
 
 
 def turn(values, cos, sin, size):
@@ -415,16 +461,16 @@
 
 
 def front_body(
-    lines, step,
+    lines, step, ready,
     inp, cot, v0, v1, v2, v3, v4, pos, cos_r, sin_r, wq, wk, wv, wo,
-    wp_o, wo_o, gains_o, n1_o, q_o, kv_o, cot_o, att_o, lse_o, hid_o, n2_o,
-    kv, small, small_g, ms, mr, gs, gr, ks, kr, ts, tr,
+    wp_o, wo_o, gains_o, n1_o, q_o, kv_o, cot_o, att_o, lse_o, hid_o, n2_o, a0_o, a1_o, b0_o,
+    kv, small, small_g, ms, mr, gs, gr, ks, kr, ts, tr, *sems
 ):
     place = where_am_i()
-    c, f, _, m, n = place
+    c, f, c2, m, n = place
     far = (m + 2) % 4
     greet(line_devices(place, lines) + [(c, m), (c, n), (c, far)])
-    tok, _ = inp.shape
+    tok, width = inp.shape
     depth, query_width = wq.shape
     key_width = wk.shape[1]
     group = H // KV
@@ -433,12 +479,6 @@
     def rows(g):
         return pl.ds(pl.multiple_of(g * depth, 16), depth)
 
-    small[...] = jnp.zeros_like(small)
-    for k, v in enumerate((v0, v1, v2, v3, v4)):
-        small[k : k + 1, : v.shape[0]] = v[...].astype(f32).reshape(1, v.shape[0])
-    smalls = [remote(small, small_g.at[f], ms.at[k], mr.at[k], (c, g)) for k, g in enumerate((m, n, far))]
-    for copy in smalls:
-        copy.start()
     project = [
         (wq, lambda g: wp_o.at[rows(g), pl.ds(0, query_width)]),
         (wk, lambda g: wp_o.at[rows(g), pl.ds(query_width, key_width)]),
@@ -446,6 +486,15 @@
     ]
     output = [(wo, lambda g: wo_o.at[rows(g)])]
     gather_start(project, gs.at[pl.ds(0, 3)], gr.at[pl.ds(0, 3)], place)
+    ready()
+    small[...] = jnp.zeros_like(small)
+    for k, v in enumerate((v0, v1, v2, v3, v4)):
+        small[k : k + 1, : v.shape[0]] = v[...].astype(f32).reshape(1, v.shape[0])
+    smalls = [remote(small, small_g.at[f], ms.at[k], mr.at[k], (c, g)) for k, g in enumerate((m, n, far))]
+    for copy in smalls:
+        copy.start()
+    spread = Spread(place, lines, cot, cot_o, ((a0_o, a1_o), (b0_o,)), sems)
+    spread.lines_out(0)
     values = inp[...].astype(f32)
     unit = values * lax.rsqrt(jnp.mean(values * values, -1, keepdims=True) + EPSILON)
     small_g[f] = small[...]
@@ -474,7 +523,11 @@
     tokens_start(items, ts, tr, place)
     gather_finish(output, gs.at[pl.ds(3, 1)], gr.at[pl.ds(3, 1)], place)
     spread_finish(kv, kv_o, ks, kr, place, lines)
+    spread.lines_out(1)
+    spread.on_line(0, True)
     for g in range(KV):
+        if g == 1:
+            spread.on_pair(0)
         queries = heads(q_o, g, group, HD)
 
         def visit(i, state):
@@ -516,6 +569,15 @@
     inverse = lax.rsqrt(jnp.mean(hidden * hidden, -1, keepdims=True) + EPSILON)
     n2_o[...] = (hidden * inverse * gains_o[1:2]).astype(bf16)
     tokens_finish(items, ts, tr, place)
+    kept = spread.keep(cot_o, 0, 1)
+    for copy in kept:
+        copy.start()
+    spread.on_line(1, False)
+    spread.finish_line(0)
+    spread.finish_pair(0)
+    spread.finish_line(1)
+    for copy in kept:
+        copy.wait()
 
 
 def heads(ref, g, group, size):
@@ -539,15 +601,100 @@
     return back, jnp.sum(grads * scaled, 0, keepdims=True)
 
 
+class Total:
+    def __init__(self, place, lines, pay, total, a_in, a_sum, a_line, b_line, b_sum, b_in, ss, rs):
+        self.place, self.lines, self.pay, self.total = place, lines, pay, total
+        self.a_in, self.a_sum, self.a_line, self.b_line, self.b_sum, self.b_in = a_in, a_sum, a_line, b_line, b_sum, b_in
+        self.ss, self.rs = ss, rs
+        self.p, self.x = place[0] // 2, place[0] % 2
+        self.height, self.half = pay.shape[0] // lines, pay.shape[1] // 2
+        self.wide = pl.ds(self.half, self.half)
+
+    def rows(self, p):
+        return pl.ds(pl.multiple_of(p * self.height, 16), self.height)
+
+    def columns(self, h, x):
+        return pl.ds(pl.multiple_of(h * self.half + x * (self.half // 2), 128), self.half // 2)
+
+    def ahead(self, k):
+        return lax.rem(self.p + k, self.lines)
+
+    def behind(self, k):
+        return lax.rem(self.p + self.lines - k, self.lines)
+
+    def to_pair(self, way, stage, src, dst):
+        c, f, c2 = self.place[:3]
+        return remote(src, dst, self.ss.at[way, stage, 0], self.rs.at[way, stage, 0], (c2, f))
+
+    def to_line(self, way, stage, k, src, dst):
+        f = self.place[1]
+        device = (self.ahead(k) * 2 + self.x, f)
+        return remote(src, dst, self.ss.at[way, stage, k], self.rs.at[way, stage, k], device)
+
+    def copies(self, way, stage):
+        pay, total, p, x = self.pay, self.total, self.p, self.x
+        every = range(1, self.lines)
+        if way == 0:
+            own = total.at[self.rows(p), self.columns(0, x)]
+            group = total.at[:, self.columns(0, x)]
+            if stage == 0:
+                return [self.to_pair(0, 0, pay.at[:, self.columns(0, 1 - x)], self.a_in)]
+            if stage == 1:
+                return [
+                    self.to_line(0, 1, k, self.a_sum.at[self.rows(self.ahead(k))], self.a_line.at[k - 1]) for k in every
+                ]
+            if stage == 2:
+                return [self.to_line(0, 2, k, own, own) for k in every]
+            return [self.to_pair(0, 3, group, group)]
+        own = total.at[self.rows(p), self.columns(1, x)]
+        both = total.at[self.rows(p), self.wide]
+        if stage == 0:
+            return [
+                self.to_line(1, 0, k, pay.at[self.rows(self.ahead(k)), self.wide], self.b_line.at[k - 1]) for k in every
+            ]
+        if stage == 1:
+            return [self.to_pair(1, 1, self.b_sum.at[:, self.columns(0, 1 - x)], self.b_in)]
+        if stage == 2:
+            return [self.to_pair(1, 2, own, own)]
+        return [self.to_line(1, 3, k, both, both) for k in every]
+
+    def start(self, stage):
+        for way in range(2):
+            for copy in self.copies(way, stage):
+                copy.start()
+
+    def wait(self, stage):
+        pay, total, p, x = self.pay, self.total, self.p, self.x
+        for way in range(2):
+            for copy in self.copies(way, stage):
+                copy.wait()
+        if stage == 0:
+            self.a_sum[...] = (pay[:, self.columns(0, x)].astype(f32) + self.a_in[...].astype(f32)).astype(bf16)
+            value = pay[self.rows(p), self.wide].astype(f32)
+            for k in range(1, self.lines):
+                value = value + self.b_line[k - 1].astype(f32)
+            self.b_sum[...] = value.astype(bf16)
+        if stage == 1:
+            value = self.a_sum[self.rows(p)].astype(f32)
+            for k in range(1, self.lines):
+                value = value + self.a_line[k - 1].astype(f32)
+            total[self.rows(p), self.columns(0, x)] = value.astype(bf16)
+            value = self.b_sum[:, self.columns(0, x)].astype(f32) + self.b_in[...].astype(f32)
+            total[self.rows(p), self.columns(1, x)] = value.astype(bf16)
+
+
 def back_body(
-    ctx, step,
-    gn, hid, gains, cot, wo, att_t, q_t, kv, pos, lse, cos_r, sin_r, n1_t, inp, wp,
-    inp_o, sums_o,
+    ctx, step, block, chunk, ready,
+    gn, hid, gains, cot, wo, att_t, q_t, kv, pos, lse, cos_r, sin_r, n1_t, inp, wp, n2, n2_g,
+    cot_a0, cot_a1, cot_b0, cot_b1, x_a0, wg_h, wu_h, wd_h,
+    inp_o, grads_o, acc_g, acc_u, acc_d, x_a1, x_b0, x_b1, x_fa0, x_fa1, x_fb0, x_fb1,
     gh, do_t, part, dq, held, ghl, ghl_g, low_t, n1_g, low_g, gp, gp_g, vec, vec_g,
-    ks, kr, ts, tr, as_, ar, vs, vr,
+    pay, total_r, a_in, a_sum, a_line, b_line, b_sum, b_in,
+    xs, cs, wg, wu, wd, acc,
+    ks, kr, ts, tr, as_, ar, vs, vr, sum_s, sum_r, ws, ins, outs, *sems
 ):
     place = where_am_i()
-    c, f, _, m, n = place
+    c, f, c2, m, n = place
     far = (m + 2) % 4
     peers = [lax.rem(c + k, ctx) for k in range(1, ctx)]
     greet([(p, f) for p in peers] + [(c, m), (c, n), (c, far)])
@@ -566,6 +713,17 @@
             for k, g in enumerate((n, far, m))
         ]
 
+    ready()
+    spread = Spread(place, ctx // 2, n2, n2_g, ((x_a0, x_a1), (x_b0, x_b1), (x_fa0, x_fa1), (x_fb0, x_fb1)), sems)
+    spread.pairs_out(0)
+    spread.lines_out(1)
+    kept = spread.keep(n2_g, 1, 2, 3)
+    loads = [
+        pltpu.make_async_copy(src, dst, ws.at[j])
+        for j, (src, dst) in enumerate(((wg_h, wg), (wu_h, wu), (wd_h, wd)))
+    ]
+    for copy in kept + loads:
+        copy.start()
     low_t[...] = att_t[...].astype(bf16)
     back, gain_two = norm_grad(hid[...], gains[1:2], gn[...])
     gh[...] = cot[...].astype(f32) + back
@@ -625,7 +783,7 @@
     gp[:, :query_width] = g_q.T.astype(bf16)
     columns = gp.shape[1]
     low_all = jnp.concatenate([low_g[g] for g in range(4)], 1)
-    sums_o[pl.ds(0, depth), pl.ds(columns, width)] = plain_dot(low_all, ghl_g[...].reshape(4 * tok, width)).astype(
+    pay[pl.ds(0, depth), pl.ds(columns, width)] = plain_dot(low_all, ghl_g[...].reshape(4 * tok, width)).astype(
         bf16
     )
     pairs = part[c].astype(f32)
@@ -648,14 +806,104 @@
     vectors = [remote(vec, vec_g.at[k], vs.at[k], vr.at[k], (c, g)) for k, g in enumerate((m, n, far))]
     for copy in vectors:
         copy.start()
+    spread.on_pair(0)
+    spread.on_line(1, True)
+    spread.lines_out(2)
     tokens_finish(items, ts.at[1], tr.at[1], place)
     n1_all = jnp.concatenate([n1_g[g] for g in range(4)], 1)
-    sums_o[pl.ds(0, depth), pl.ds(0, columns)] = plain_dot(n1_all, gp_g[...].reshape(4 * tok, columns)).astype(bf16)
+    pay[pl.ds(0, depth), pl.ds(0, columns)] = plain_dot(n1_all, gp_g[...].reshape(4 * tok, columns)).astype(bf16)
     total = vec[...]
     for k, copy in enumerate(vectors):
         copy.wait()
         total = total + vec_g[k]
-    sums_o[pl.ds(depth, 16)] = jnp.concatenate([total, total], 0).astype(bf16)
+    pay[pl.ds(depth, 8)] = total.astype(bf16)
+    pay[pl.ds(depth + 8, pay.shape[0] - depth - 8)] = jnp.zeros_like(pay[pl.ds(depth + 8, pay.shape[0] - depth - 8)])
+    summed = Total(place, ctx // 2, pay, total_r, a_in, a_sum, a_line, b_line, b_sum, b_in, sum_s, sum_r)
+    summed.start(0)
+    spread.cross(0)
+    spread.cross(1)
+    for copy in loads:
+        copy.wait()
+    parts = (((x_a0, x_a1), (cot_a0, cot_a1)), ((x_b0, x_b1), (cot_b0, cot_b1)))
+    blocks = wg.shape[0] // block
+    per_part = ctx * tok // chunk
+    for way, sides in enumerate(parts):
+        if way == 1:
+            spread.finish_line(1)
+            kept[0].wait()
+        spread.finish_pair(way)
+        for i in range(per_part):
+            count = chunk // tok // 2
+            at = pl.ds(i * count, count)
+            fetch = [
+                pltpu.make_async_copy(sides[j][side].at[at], into.at[side], ins.at[j, side])
+                for j, into in enumerate((xs, cs))
+                for side in range(2)
+            ]
+            for copy in fetch:
+                copy.start()
+            for copy in fetch:
+                copy.wait()
+            tokens = xs[...].reshape(chunk, width), cs[...].reshape(chunk, width)
+            first = way == 0 and i == 0
+            last = way == 1 and i == per_part - 1
+
+            @pl.loop(0, blocks)
+            def _(b):
+                at = pl.ds(pl.multiple_of(b * block, 16), block)
+                act, g_gate, g_up = hidden_units(*tokens, wg[at], wu[at], wd[at])
+                for j, (left, right) in enumerate(((g_gate, 0), (g_up, 0), (act, 1))):
+                    value = plain_dot(left, tokens[right])
+                    if first:
+                        acc[j, at] = value
+                    else:
+                        acc[j, at] += value
+                for stage in range(3 if first else 0):
+
+                    @pl.when(b == stage)
+                    def _():
+                        summed.wait(stage)
+                        summed.start(stage + 1)
+
+                if way == 0 and i == 0:
+
+                    @pl.when(b == 1)
+                    def _():
+                        spread.on_pair(1)
+
+                    @pl.when(b == 3)
+                    def _():
+                        spread.on_line(2, True)
+
+                if way == 1 and i == 0:
+
+                    @pl.when(b == 0)
+                    def _():
+                        spread.on_y(0)
+
+                    @pl.when(b == 1)
+                    def _():
+                        spread.on_y(1)
+
+                    @pl.when(b == 2)
+                    def _():
+                        spread.on_pair(2)
+
+                if last:
+                    for j, out in enumerate((acc_g, acc_u, acc_d)):
+                        pltpu.make_async_copy(acc.at[j, at], out.at[at], outs.at[b, j]).start()
+
+    summed.wait(3)
+    grads_o[...] = total_r[...].astype(f32)
+    spread.finish_line(2)
+    spread.finish_pair(2)
+    spread.finish_cross()
+    for b in range(blocks):
+        at = pl.ds(b * block, block)
+        for j, out in enumerate((acc_g, acc_u, acc_d)):
+            pltpu.make_async_copy(acc.at[j, at], out.at[at], outs.at[b, j]).wait()
+    for copy in kept[1:]:
+        copy.wait()
 
 
 def over_last(a, b):
@@ -675,22 +923,51 @@
 
 
 def hidden_body(
-    chunk, block, x_h, c_h, wg_h, wu_h, wd_h, og_h, ou_h, od_h, xs, cs, wg, wu, wd, acc, in_sem, w_sem, out_sem
+    chunk, block, x0_h, x1_h, x2_h, x3_h, c0_h, c1_h, c2_h, c3_h, wg_h, wu_h, wd_h, ig_h, iu_h, id_h, og_h, ou_h, od_h, xs, cs, wg, wu, wd, acc, in_sem, w_sem, out_sem, init_sem
 ):
-    rows = x_h.shape[0]
+    parts = (((x0_h, x1_h), (c0_h, c1_h)), ((x2_h, x3_h), (c2_h, c3_h)))
+    rows = 4 * x0_h.shape[0]
     steps, blocks, held = rows // chunk, wg.shape[0] // block, xs.shape[0] // chunk
-    loads = [
-        pltpu.make_async_copy(src, dst, w_sem.at[j])
-        for j, (src, dst) in enumerate(((wg_h, wg), (wu_h, wu), (wd_h, wd)))
-    ]
-
-    def tokens(i):
-        src = pl.ds(pl.multiple_of(i * chunk, chunk), chunk)
-        dst = pl.ds(pl.multiple_of(i % held * chunk, chunk), chunk)
+    def weights(b):
+        at = pl.ds(b * block, block)
         return [
-            pltpu.make_async_copy(x_h.at[src], xs.at[dst], in_sem.at[i % held, 0]),
-            pltpu.make_async_copy(c_h.at[src], cs.at[dst], in_sem.at[i % held, 1]),
+            pltpu.make_async_copy(src.at[at], dst.at[at], w_sem.at[b, j])
+            for j, (src, dst) in enumerate(((wg_h, wg), (wu_h, wu), (wd_h, wd)))
         ]
+
+    def fetch(i, begin, part):
+        half = chunk // 2
+        src = pl.ds(pl.multiple_of(begin * half, half), half)
+        slot = i % held
+        return [
+            pltpu.make_async_copy(
+                part[j][side].at[src],
+                into.at[pl.ds(pl.multiple_of(slot * chunk + side * half, half), half)],
+                in_sem.at[slot, j, side],
+            )
+            for j, into in enumerate((xs, cs))
+            for side in range(2)
+        ]
+
+    def start_tokens(i):
+        begin = 0
+        for part in parts:
+            count = 2 * x0_h.shape[0] // chunk
+
+            def go(begin=begin, part=part):
+                for copy in fetch(i, i - begin, part):
+                    copy.start()
+
+            if isinstance(i, int):
+                if begin <= i < begin + count:
+                    go()
+            else:
+                pl.when((i >= begin) & (i < begin + count))(go)
+            begin += count
+
+    def wait_tokens(i):
+        for copy in fetch(i, 0, parts[0]):
+            copy.wait()
 
     def results(b, slot):
         at = pl.ds(pl.multiple_of(b * block, 16), block)
@@ -699,24 +976,36 @@
             for j, out in enumerate((og_h, ou_h, od_h))
         ]
 
+    def initial(b, slot):
+        at = pl.ds(pl.multiple_of(b * block, 16), block)
+        return [
+            pltpu.make_async_copy(src.at[at], acc.at[slot, j], init_sem.at[slot, j])
+            for j, src in enumerate((ig_h, iu_h, id_h))
+        ]
+
     resident = held == steps
-    for copy in tokens(0) + loads:
+    slots = acc.shape[0]
+    start_tokens(0)
+    for copy in weights(0):
+        copy.start()
+    for copy in weights(0):
+        copy.wait()
+    for copy in initial(0, 0):
         copy.start()
     for i in range(1, held if resident else 1):
-        for copy in tokens(i):
+        start_tokens(i)
+    for b in range(1, slots):
+        for copy in weights(b) + initial(b, b):
             copy.start()
-    for copy in loads:
-        copy.wait()
-    slots = acc.shape[0]
 
     @pl.loop(0, blocks)
     def _(b):
         slot = b % slots
         at = pl.ds(pl.multiple_of(b * block, 16), block)
 
-        @pl.when(b >= slots)
+        @pl.when(b == 1)
         def _():
-            for copy in results(b - slots, slot):
+            for copy in weights(1):
                 copy.wait()
 
         @pl.loop(0, steps)
@@ -725,17 +1014,14 @@
 
                 @pl.when(b == 0)
                 def _():
-                    for copy in tokens(i):
-                        copy.wait()
+                    wait_tokens(i)
 
             else:
-                for copy in tokens(i):
-                    copy.wait()
+                wait_tokens(i)
 
                 @pl.when((i + 1 < steps) | (b + 1 < blocks))
                 def _():
-                    for copy in tokens(lax.rem(i + 1, steps)):
-                        copy.start()
+                    start_tokens(lax.rem(i + 1, steps))
 
             t = pl.ds(pl.multiple_of(i % held * chunk, chunk), chunk)
             x, cot = xs[t], cs[t]
@@ -743,15 +1029,12 @@
 
             @pl.when(i == 0)
             def _():
-                acc[slot, 0] = plain_dot(g_gate, x)
-                acc[slot, 1] = plain_dot(g_up, x)
-                acc[slot, 2] = plain_dot(act, cot)
-
-            @pl.when(i > 0)
-            def _():
-                acc[slot, 0] += plain_dot(g_gate, x)
-                acc[slot, 1] += plain_dot(g_up, x)
-                acc[slot, 2] += plain_dot(act, cot)
+                for copy in initial(b, slot):
+                    copy.wait()
+
+            acc[slot, 0] += plain_dot(g_gate, x)
+            acc[slot, 1] += plain_dot(g_up, x)
+            acc[slot, 2] += plain_dot(act, cot)
 
         for copy in results(b, slot):
             copy.start()
@@ -761,10 +1044,12 @@
             copy.wait()
 
 
-def hidden_grads(x, cot, wg, wu, wd):
-    rows, width = x.shape
+def hidden_grads(xs, cots, wg, wu, wd, initial):
+    width = wg.shape[1]
+    xs, cots = [[part.reshape(-1, width) for part in parts] for parts in (xs, cots)]
+    rows = sum(part.shape[0] for part in xs)
     units = wg.shape[0]
-    chunk = math.gcd(rows, 1024)
+    chunk = math.gcd(rows // 2, 1024)
     block = units // 2
     held = min(rows // chunk, 4)
     any_spec = pl.BlockSpec(memory_space=pl.ANY)
@@ -772,17 +1057,17 @@
     return pl.pallas_call(
         functools.partial(hidden_body, chunk, block),
         out_shape=(jax.ShapeDtypeStruct((units, width), f32),) * 3,
-        in_specs=[any_spec] * 5,
+        in_specs=[any_spec] * 14,
         out_specs=(any_spec,) * 3,
         scratch_shapes=[pltpu.VMEM((held * chunk, width), bf16)] * 2
         + [pltpu.VMEM((units, width), bf16)] * 3
-        + [pltpu.VMEM((2, 3, block, width), f32), dma((held, 2)), dma((3,)), dma((2, 3))],
+        + [pltpu.VMEM((2, 3, block, width), f32), dma((held, 2, 2)), dma((2, 3)), dma((2, 3)), dma((2, 3))],
         compiler_params=pltpu.CompilerParams(vmem_limit_bytes=62 << 20),
         cost_estimate=pl.CostEstimate(
             flops=12 * rows * width * units, bytes_accessed=4 * rows * width + 18 * units * width, transcendentals=0
         ),
         name="hidden_grads",
-    )(x, cot, wg, wu, wd)
+    )(*xs, *cots, wg, wu, wd, *initial)
 
 
 def shards(
@@ -808,29 +1093,37 @@
     group = H // KV
     query_width = H * HD
     key_width = KV * HD
+    score_scale = HD ** (-0.5)
     ctx = lax.axis_size("ctx")
     fsdp = lax.axis_size("fsdp")
     depth = width // fsdp
     lines = ctx // 2
     c, f = lax.axis_index("ctx"), lax.axis_index("fsdp")
+    seq_length = ctx * tok
     dma = pltpu.SemaphoreType.DMA
     sds = jax.ShapeDtypeStruct
     input_rows = layer_input[0]
     grad_out = cotangent[0]
+    own_segment = seq_ids[0]
     own_positions = positions[0]
     query_rows = c * tok + jnp.arange(tok, dtype=jnp.int32)
-
-    cot_all = lax.all_gather(grad_out, ("ctx", "fsdp"), axis=0, tiled=True)
 
     cosine, sine_table = rope_tables(own_positions, HD)
     own_positions = own_positions[None]
     step = math.gcd(ctx, 4)
     columns = query_width + 2 * key_width
     hbm = pl.BlockSpec(memory_space=pltpu.HBM)
-    (w_project, wo_full, gains, n1_t, q_t, kv_all, cot_group, att_t, log_total, hidden_state, normed_second) = (
-        pl.pallas_call(
+    half_blocks = sds((lines, 2, tok // 2, width), bf16)
+    (w_project, wo_full, gains, n1_t, q_t, kv_all, cot_group, att_t, log_total, hidden_state, normed_second,
+     cot_a0, cot_a1, cot_b0) = (
+        staged_call(
             functools.partial(front_body, lines, step),
-            out_shape=(
+            (
+                input_rows, grad_out, norm_gain, mlp_gain, b_query, b_key, b_value, own_positions, cosine, sine_table,
+                w_query, w_key, w_value, w_output,
+            ),
+            (10, 11, 12, 13),
+            (
                 sds((width, columns), bf16),
                 sds((query_width, width), bf16),
                 sds((8, width), f32),
@@ -842,10 +1135,12 @@
                 sds((H, tok), f32),
                 sds((tok, width), f32),
                 sds((tok, width), bf16),
+                half_blocks,
+                half_blocks,
+                half_blocks,
             ),
-            in_specs=[VMEM] * 10 + [hbm] * 4,
-            out_specs=(VMEM,) * 11,
-            scratch_shapes=[
+            (11, 12, 13),
+            [
                 pltpu.VMEM((tok, 2 * key_width), bf16),
                 pltpu.VMEM((8, 256), f32),
                 pltpu.VMEM((fsdp, 8, 256), f32),
@@ -854,31 +1149,27 @@
             ]
             + gather_sems(4)
             + [dma((2, lines)), dma((2, lines))]
-            + gather_sems(1),
-            compiler_params=pltpu.CompilerParams(
-                collective_id=0, has_side_effects=True, vmem_limit_bytes=62 << 20
-            ),
-            cost_estimate=pl.CostEstimate(flops=4 * 10**9, bytes_accessed=10**7, transcendentals=0),
-            name="front",
-        )(
-            input_rows, grad_out, norm_gain, mlp_gain, b_query, b_key, b_value, own_positions, cosine, sine_table,
-            w_query, w_key, w_value, w_output,
+            + gather_sems(1)
+            + spread_sems(lines),
+            0,
+            "front",
+            pl.CostEstimate(flops=4 * 10**9, bytes_accessed=10**7, transcendentals=0),
         )
     )
     units = w_down.shape[0]
-    any_spec = pl.BlockSpec(memory_space=pltpu.HBM)
     wg_t, wu_t = w_gate.T, w_up.T
-    grad_normed2, block_out, x_all = pl.pallas_call(
+    (grad_normed2, block_out, x_group, cot_b1, cot_fa0, cot_fa1, cot_fb0, cot_fb1, x_a0) = staged_call(
         functools.partial(mid_body, lines),
-        out_shape=(
+        (normed_second, cot_group, grad_out, cot_a0, cot_a1, cot_b0, hidden_state, wg_t, wu_t, w_down),
+        (3, 4, 5, 7, 8, 9),
+        (
             sds((tok, width), f32),
             sds((tok, width), bf16),
-            sds((ctx, fsdp, tok, width), bf16),
-        ),
-        in_specs=[VMEM, VMEM, VMEM, any_spec, any_spec, any_spec],
-        out_specs=(VMEM, VMEM, any_spec),
-        scratch_shapes=[pltpu.VMEM((fsdp, tok, width), bf16)]
-        + [pltpu.VMEM((units, width), bf16)] * 3
+            sds((fsdp, tok, width), bf16),
+        )
+        + (half_blocks,) * 6,
+        (3, 4, 5, 6, 7, 8),
+        [pltpu.VMEM((units, width), bf16)] * 3
         + [
             pltpu.VMEM((3, 2 * tok, units), bf16),
             pltpu.VMEM((2, tok, width), f32),
@@ -886,30 +1177,36 @@
             pltpu.VMEM((2, tok, width), bf16),
             pltpu.VMEM((2, tok, width), bf16),
             dma((3,)),
-            dma,
             dma((5,)),
             dma((5,)),
             dma((6,)),
             dma((6,)),
         ]
+        + spread_sems(lines)
         + spread_sems(lines),
-        compiler_params=pltpu.CompilerParams(
-            collective_id=2, has_side_effects=True, vmem_limit_bytes=62 << 20
-        ),
-        cost_estimate=pl.CostEstimate(
+        2,
+        "mid",
+        pl.CostEstimate(
             flops=12 * fsdp * tok * width * units, bytes_accessed=6 * units * width, transcendentals=0
         ),
-        name="mid",
-    )(normed_second, cot_group, hidden_state, wg_t, wu_t, w_down)
+    )
     block_out = block_out[None]
-    x_all = x_all.reshape(ctx * fsdp * tok, width)
-    params = pltpu.CompilerParams(collective_id=3, has_side_effects=True, vmem_limit_bytes=62 << 20)
-    input_grad, weight_grads = pl.pallas_call(
-        functools.partial(back_body, ctx, step),
-        out_shape=(sds((tok, width), bf16), sds((depth + 16, columns + width), bf16)),
-        in_specs=[VMEM] * 15,
-        out_specs=(VMEM, VMEM),
-        scratch_shapes=[
+    tall, everything = 256, columns + width
+    height = tall // lines
+    block = units // 4
+    chunk = math.gcd(ctx * tok, 1024)
+    big = sds((units, width), f32)
+    (input_grad, weight_grads, acc_g, acc_u, acc_d, x_a1, x_b0, x_b1, x_fa0, x_fa1, x_fb0, x_fb1) = staged_call(
+        functools.partial(back_body, ctx, step, block, chunk),
+        (
+            grad_normed2, hidden_state, gains, grad_out, wo_full, att_t, q_t, kv_all, own_positions, log_total,
+            cosine, sine_table, n1_t, input_rows, w_project, normed_second, x_group, cot_a0, cot_a1,
+            cot_b0, cot_b1, x_a0, wg_t, wu_t, w_down,
+        ),
+        (17, 18, 19, 20, 21, 22, 23, 24),
+        (sds((tok, width), bf16), sds((tall, everything), f32), big, big, big) + (half_blocks,) * 7,
+        (2, 3, 4, 5, 6, 7, 8, 9, 10, 11),
+        [
             pltpu.VMEM((tok, width), f32),
             pltpu.VMEM((query_width, tok), bf16),
             pltpu.VMEM((ctx, tok, 2 * key_width), bf16),
@@ -922,8 +1219,22 @@
             pltpu.VMEM((fsdp, depth, tok), bf16),
             pltpu.VMEM((tok, columns), bf16),
             pltpu.VMEM((fsdp, tok, columns), bf16),
-            pltpu.VMEM((8, columns + width), f32),
-            pltpu.VMEM((3, 8, columns + width), f32),
+            pltpu.VMEM((8, everything), f32),
+            pltpu.VMEM((3, 8, everything), f32),
+            pltpu.VMEM((tall, everything), bf16),
+            pltpu.VMEM((tall, everything), bf16),
+            pltpu.VMEM((tall, everything // 4), bf16),
+            pltpu.VMEM((tall, everything // 4), bf16),
+            pltpu.VMEM((lines - 1, height, everything // 4), bf16),
+            pltpu.VMEM((lines - 1, height, everything // 2), bf16),
+            pltpu.VMEM((height, everything // 2), bf16),
+            pltpu.VMEM((height, everything // 4), bf16),
+            pltpu.VMEM((2, chunk // tok // 2, 2, tok // 2, width), bf16),
+            pltpu.VMEM((2, chunk // tok // 2, 2, tok // 2, width), bf16),
+            pltpu.VMEM((units, width), bf16),
+            pltpu.VMEM((units, width), bf16),
+            pltpu.VMEM((units, width), bf16),
+            pltpu.VMEM((3, units, width), f32),
             dma((ctx - 1,)),
             dma((ctx - 1,)),
             dma((2, 1, 6)),
@@ -932,30 +1243,18 @@
             dma((2, 3)),
             dma((3,)),
             dma((3,)),
-        ],
-        compiler_params=params,
-        cost_estimate=pl.CostEstimate(flops=10**10, bytes_accessed=10**7, transcendentals=0),
-        name="back",
-    )(
-        grad_normed2,
-        hidden_state,
-        gains,
-        grad_out,
-        wo_full,
-        att_t,
-        q_t,
-        kv_all,
-        own_positions,
-        log_total,
-        cosine,
-        sine_table,
-        n1_t,
-        input_rows,
-        w_project,
+            dma((2, 4, lines)),
+            dma((2, 4, lines)),
+            dma((3,)),
+            dma((2, 2)),
+            dma((4, 3)),
+        ]
+        + spread_sems(lines),
+        3,
+        "back",
+        pl.CostEstimate(flops=4 * 10**10, bytes_accessed=6 * 10**7, transcendentals=0),
     )
     input_grad = input_grad[None]
-    weight_grads = lax.psum(weight_grads, "ctx")
-    weight_grads = weight_grads.astype(f32)
     starts = ((0, 0, width), (1, 0, width), (2, 0, query_width), (2, query_width, key_width),
               (2, query_width + key_width, key_width))
 
@@ -966,7 +1265,9 @@
     own = [piece(*at) for at in starts]
     weight_grads = weight_grads[:depth]
 
-    gate_grad, up_grad, down_grad = hidden_grads(x_all, cot_all, wg_t, wu_t, w_down)
+    gate_grad, up_grad, down_grad = hidden_grads(
+        (x_fa0, x_fa1, x_fb0, x_fb1), (cot_fa0, cot_fa1, cot_fb0, cot_fb1), wg_t, wu_t, w_down, (acc_g, acc_u, acc_d)
+    )
     return (
         block_out,
         input_grad,

time: 328 us -> 249 us (0.76)
  waiting for transfers between devices: 92.8 us -> 0 us
  Pallas kernels: 209 us -> 237 us
  between operations: 15.6 us -> 0.71 us
    psum x1 -> x0, waiting for transfers between devices: 92.5 us -> none  [shards(): weight_grads = lax.psum(weight_grads, 'ctx')]
    pallas_call x3, Pallas kernels: 131 us -> 197 us  [staged_call(): pl.pallas_call(kernel, out_shape=out_shape, in_specs=[hbm] * len(args), o...]
    pallas_call x1, Pallas kernels: 77.6 us -> 40.1 us  [hidden_grads(): pl.pallas_call(functools.partial(hidden_body, chunk, block), out_shape=(j...]
  transfers between devices with their start and end apart: 2 -> 0, of which waited for: 1 -> 0; matrix products, arithmetic and copies ran while one was open for 2% -> 0% of each run, Pallas kernels for 0% -> 0%
where the time goes in v3:
time: 249 us
  Pallas kernels  237 us (95%)
  local copies, waits for them, and re-layouts  9.14 us (4%)
    pallas_call x3, Pallas kernels, staged_call(): pl.pallas_call(kernel, out_shape=out_shape, in_specs=[hbm] * len(args), o...  197 us
    pallas_call x1, Pallas kernels, hidden_grads(): pl.pallas_call(functools.partial(hidden_body, chunk, block), out_shape=(j...  40.1 us

profile of v3, /device:TPU:0, one launch (start us, length us, event | category | flops | bytes accessed | tf_op | source)
XLA Modules:
  0.0 248.7 jit_solution(2159480182182901403)
XLA Ops:
  0.6 0.7 convert_bitcast_fusion
  1.3 0.8 multiply_sine_fusion
  2.1 59.4 %front.1 = (bf16[896,1152]{1,0:T(8,128)(2,1)}, bf16[896,896]{1,0:T(8,128)(2,1)}, f32[8,896]{1,0:T(8,128)}, bf16[896,128]{1,0:T(8,128)(2,1)}, bf16[896,128]{1,0:T...) custom-call(bf16[128,896]{1,0:T(8,128)(2,1)} %bitcast.38, ...), custom_call_target="tpu_custom_call" | custom-call | flops 4000000000 | bytes 10000000 | tf_op jit(solution)/shard_map/front/pallas_call | solution.py:162
  61.4 45.1 %mid.1 = (f32[128,896]{1,0:T(8,128)}, bf16[128,896]{1,0:T(8,128)(2,1)}, bf16[4,128,896]{2,1,0:T(8,128)(2,1)}, bf16[4,2,64,896]{3,2,1,0:T(8,128)(2,1)}, bf16[4,2,...) custom-call(bf16[128,896]{1,0:T(8,128)(2,1)} %get-tuple-element.50.r, ...), custom_call_target="tpu_custom_call" | custom-call | flops 6694109184 | bytes 6537216 | tf_op jit(solution)/shard_map/mid/pallas_call | solution.py:162
  106.6 92.8 %back.1 = (bf16[128,896]{1,0:T(8,128)(2,1)}, f32[256,2048]{1,0:T(8,128)}, f32[1216,896]{1,0:T(8,128)}, f32[1216,896]{1,0:T(8,128)}, f32[1216,896]{1,0:T(8,128)},...) custom-call(f32[128,896]{1,0:T(8,128)} %get-tuple-element.57.refs_0_, ...), custom_call_target="tpu_custom_call" | custom-call | flops 40000000000 | bytes 60000000 | tf_op jit(solution)/shard_map/back/pallas_call | solution.py:162
  199.4 40.1 %hidden_grads.1 = (f32[1216,896]{1,0:T(8,128)}, f32[1216,896]{1,0:T(8,128)}, f32[1216,896]{1,0:T(8,128)}) custom-call(bf16[512,896]{1,0:T(8,128)(2,1)} %bitcast.49, bf16[512,896]{1,0:T(8,128)(2,1)} %bitcast.50, bf16[512,896]{1,0:T(8,128)(2,1)} %bitcast.51, bf16[512,896]{1,0:T(8,128)(2,1)} %bitcast.52, bf16[512,896]{1,0:T(8,128)(2,1)} %bitcast.45, ...), custom_call_target="tpu_custom_call" | custom-call | flops 26776436736 | bytes 26951680 | tf_op jit(solution)/shard_map/hidden_grads/pallas_call | solution.py:1057
  239.5 0.0 copy-start.2
  239.5 0.0 copy-start
  239.5 0.0 copy-start.1
  239.5 1.0 fusion.2
  240.5 0.6 constant_dynamic-slice_fusion
  241.2 2.6 %fusion.3 = (f32[224,896]{1,0:T(8,128)}, f32[224,896]{1,0:T(8,128)}) fusion(f32[256,2048]{1,0:T(8,128)} %get-tuple-element.70), kind=kLoop, calls=%fused_computation.12 | loop fusion | bytes 3211264 | tf_op jit(solution)/shard_map/slice | solution.py:1281
  243.8 1.7 fusion.4
  245.4 0.6 fusion.1
  246.0 0.6 constant_dynamic-slice_fusion.4
  246.7 0.0 copy-done.2
  246.7 0.6 copy.30
  247.3 0.0 copy-done
  247.3 0.7 copy.33
  248.0 0.0 copy-done.1
  248.0 0.7 copy.34
  (1 shorter events, 0.0 us)
Async XLA Ops:
  239.5 7.2 %copy-start.2 = (f32[14,128]{1,0:T(8,128)S(1)}, f32[14,128]{1,0:T(8,128)}, u32[]{:S(2)}) copy-start(f32[14,128]{1,0:T(8,128)} %get-tuple-element.63.refs_9_) | copy-start | bytes 21508
  239.5 7.8 %copy-start = (bf16[128,896]{1,0:T(8,128)(2,1)S(1)}, bf16[128,896]{1,0:T(8,128)(2,1)}, u32[]{:S(2)}) copy-start(bf16[128,896]{1,0:T(8,128)(2,1)} %get-tuple-element.56) | copy-start | bytes 688132
  239.5 8.5 %copy-start.1 = (bf16[128,896]{1,0:T(8,128)(2,1)S(1)}, bf16[128,896]{1,0:T(8,128)(2,1)}, u32[]{:S(2)}) copy-start(bf16[128,896]{1,0:T(8,128)(2,1)} %get-tuple-element.69) | copy-start | bytes 688132

commit v4 on v3

--- a/solution.py
+++ b/solution.py
@@ -166,7 +166,7 @@
         out_specs=(hbm,) * len(out_shape),
         scratch_shapes=scratch + buffers + sems,
         compiler_params=pltpu.CompilerParams(
-            collective_id=ident, has_side_effects=True, vmem_limit_bytes=62 << 20
+            collective_id=ident, has_side_effects=True, vmem_limit_bytes=67_043_328
         ),
         cost_estimate=cost,
         name=name,
@@ -220,11 +220,7 @@
         return lax.rem(self.place[0] // 2 + self.lines - k, self.lines)
 
     def each(self, first, act):
-        if self.lines <= 4:
-            for k in range(first, self.lines):
-                act(k)
-        else:
-            pl.loop(first, self.lines)(act)
+        pl.loop(first, self.lines)(act)
 
     def source(self, way):
         n = self.place[4]
@@ -306,8 +302,11 @@
         return copies
 
     def handed(self, way, side):
-        self.each(1 - side, lambda k: self.hand(way, side, k).wait_send())
-        self.each(1 - side, lambda k: self.hand(way, side, k, 1 - self.core).wait_recv())
+        def act(k):
+            self.hand(way, side, k).wait_send()
+            self.hand(way, side, k, 1 - self.core).wait_recv()
+
+        self.each(1 - side, act)
 
     def finish_line(self, way):
         self.each(1, lambda k: self.line(way, k).wait_send())
@@ -330,7 +329,7 @@
 
 def mid_body(
     lines, ready, x, cot, own_cot, a0, a1, b0, hid, wg_h, wu_h, wd_h,
-    gn_o, block_o, xg, b1_o, fa0_o, fa1_o, fb0_o, fb1_o, xa0_o,
+    gn_o, block_o, xg, b1_o, fb0_o, xa0_o, xa1_o,
     wg, wu, wd, act, back, near, sums, far_in, ws, ss, rs, ns, nr, *sems
 ):
     place = where_am_i()
@@ -351,12 +350,11 @@
     for j in range(2):
         rows = pl.ds(j * half, half)
         remote(x.at[rows], xg.at[f, rows], ss.at[1 + j], rs.at[1 + j], (c, n)).start()
-    rest = Spread(place, lines, own_cot, cot, ((a0, a1), (b0, b1_o), (fa0_o, fa1_o), (fb0_o, fb1_o)), sems[:9])
-    spread = Spread(place, lines, x, xg, ((xa0_o,),), sems[9:])
+    rest = Spread(place, lines, own_cot, cot, ((a0, a1), (b0, b1_o), None, (fb0_o,)), sems[:9])
+    spread = Spread(place, lines, x, xg, ((xa0_o, xa1_o),), sems[9:])
     rest.pairs_out(1)
-    rest.lines_out(2)
     spread.lines_out(0)
-    kept = rest.keep(cot, 2, 3)
+    kept = rest.keep(cot, 3)
     for copy in kept:
         copy.start()
     xg[f] = x[...]
@@ -402,7 +400,7 @@
         here = xg.at[n, pl.ds(j * half, half)]
         remote(here, here, ss.at[1 + j], rs.at[1 + j], (c, n)).wait_recv()
         remote(here, here, ss.at[3 + j], rs.at[3 + j], (c, m)).start()
-    rest.cross(0)
+    rest.lines_out(2)
     give(0, backward())
     gn_o[...] = back[core]
     give(1, down())
@@ -415,11 +413,9 @@
     forward(1 - y)
     give(2, backward())
     send_over(0, 2)
-    rest.on_line(2, True)
+    spread.on_line(0, True)
     give(3, down())
     send_over(1, 3)
-    rest.cross(1)
-    rest.on_y(0)
     rest.on_pair(1)
     cross(0).wait()
     swap(0).wait()
@@ -427,9 +423,8 @@
     cross(1).wait()
     swap(1).wait()
     block_o[...] = (down_own + near[3].astype(f32) + far_in[1].astype(f32)).astype(bf16)
-    spread.on_line(0, False)
-    rest.on_pair(2)
-    rest.on_y(1)
+    rest.on_line(2, False)
+    spread.on_pair(0)
     for j in range(2):
         rows = pl.ds(j * half, half)
         remote(x.at[rows], xg.at[f, rows], ss.at[1 + j], rs.at[1 + j], (c, n)).wait_send()
@@ -438,9 +433,8 @@
         copy.wait()
     rest.finish_pair(1)
     rest.finish_line(2)
-    rest.finish_pair(2)
-    rest.finish_cross()
     spread.finish_line(0)
+    spread.finish_pair(0)
 
 
 def turn(values, cos, sin, size):
@@ -526,8 +520,6 @@
     spread.lines_out(1)
     spread.on_line(0, True)
     for g in range(KV):
-        if g == 1:
-            spread.on_pair(0)
         queries = heads(q_o, g, group, HD)
 
         def visit(i, state):
@@ -572,6 +564,7 @@
     kept = spread.keep(cot_o, 0, 1)
     for copy in kept:
         copy.start()
+    spread.on_pair(0)
     spread.on_line(1, False)
     spread.finish_line(0)
     spread.finish_pair(0)
@@ -602,25 +595,19 @@
 
 
 class Total:
-    def __init__(self, place, lines, pay, total, a_in, a_sum, a_line, b_line, b_sum, b_in, ss, rs):
+    def __init__(self, place, lines, low, wide, rest, pay, total, bufs, ss, rs):
         self.place, self.lines, self.pay, self.total = place, lines, pay, total
-        self.a_in, self.a_sum, self.a_line, self.b_line, self.b_sum, self.b_in = a_in, a_sum, a_line, b_line, b_sum, b_in
+        self.a_in, self.a_sum, self.a_line, self.b_line, self.b_sum, self.b_in = bufs
         self.ss, self.rs = ss, rs
         self.p, self.x = place[0] // 2, place[0] % 2
-        self.height, self.half = pay.shape[0] // lines, pay.shape[1] // 2
-        self.wide = pl.ds(self.half, self.half)
-
-    def rows(self, p):
-        return pl.ds(pl.multiple_of(p * self.height, 16), self.height)
-
-    def columns(self, h, x):
-        return pl.ds(pl.multiple_of(h * self.half + x * (self.half // 2), 128), self.half // 2)
+        self.height = pay.shape[0] // (2 * lines)
+        self.a, self.b = pl.ds(low, wide), pl.ds(low + wide, rest)
+
+    def rows(self, first, count=1):
+        return pl.ds(pl.multiple_of(first * self.height, 16), count * self.height)
 
     def ahead(self, k):
         return lax.rem(self.p + k, self.lines)
-
-    def behind(self, k):
-        return lax.rem(self.p + self.lines - k, self.lines)
 
     def to_pair(self, way, stage, src, dst):
         c, f, c2 = self.place[:3]
@@ -632,13 +619,13 @@
         return remote(src, dst, self.ss.at[way, stage, k], self.rs.at[way, stage, k], device)
 
     def copies(self, way, stage):
-        pay, total, p, x = self.pay, self.total, self.p, self.x
-        every = range(1, self.lines)
+        pay, total, p, x, n = self.pay, self.total, self.p, self.x, self.lines
+        every = range(1, n)
         if way == 0:
-            own = total.at[self.rows(p), self.columns(0, x)]
-            group = total.at[:, self.columns(0, x)]
+            own = total.at[self.rows(x * n + p), self.a]
+            group = total.at[self.rows(x * n, n), self.a]
             if stage == 0:
-                return [self.to_pair(0, 0, pay.at[:, self.columns(0, 1 - x)], self.a_in)]
+                return [self.to_pair(0, 0, pay.at[self.rows((1 - x) * n, n), self.a], self.a_in)]
             if stage == 1:
                 return [
                     self.to_line(0, 1, k, self.a_sum.at[self.rows(self.ahead(k))], self.a_line.at[k - 1]) for k in every
@@ -646,14 +633,15 @@
             if stage == 2:
                 return [self.to_line(0, 2, k, own, own) for k in every]
             return [self.to_pair(0, 3, group, group)]
-        own = total.at[self.rows(p), self.columns(1, x)]
-        both = total.at[self.rows(p), self.wide]
+        own = total.at[self.rows(p * 2 + x), self.b]
+        both = total.at[self.rows(p * 2, 2), self.b]
         if stage == 0:
             return [
-                self.to_line(1, 0, k, pay.at[self.rows(self.ahead(k)), self.wide], self.b_line.at[k - 1]) for k in every
+                self.to_line(1, 0, k, pay.at[self.rows(self.ahead(k) * 2, 2), self.b], self.b_line.at[k - 1])
+                for k in every
             ]
         if stage == 1:
-            return [self.to_pair(1, 1, self.b_sum.at[:, self.columns(0, 1 - x)], self.b_in)]
+            return [self.to_pair(1, 1, self.b_sum.at[self.rows(1 - x)], self.b_in)]
         if stage == 2:
             return [self.to_pair(1, 2, own, own)]
         return [self.to_line(1, 3, k, both, both) for k in every]
@@ -664,32 +652,42 @@
                 copy.start()
 
     def wait(self, stage):
-        pay, total, p, x = self.pay, self.total, self.p, self.x
+        pay, total, p, x, n = self.pay, self.total, self.p, self.x, self.lines
         for way in range(2):
             for copy in self.copies(way, stage):
                 copy.wait()
         if stage == 0:
-            self.a_sum[...] = (pay[:, self.columns(0, x)].astype(f32) + self.a_in[...].astype(f32)).astype(bf16)
-            value = pay[self.rows(p), self.wide].astype(f32)
-            for k in range(1, self.lines):
+            value = pay[self.rows(x * n, n), self.a].astype(f32) + self.a_in[...].astype(f32)
+            self.a_sum[...] = value.astype(bf16)
+            value = pay[self.rows(p * 2, 2), self.b].astype(f32)
+            for k in range(1, n):
                 value = value + self.b_line[k - 1].astype(f32)
             self.b_sum[...] = value.astype(bf16)
         if stage == 1:
             value = self.a_sum[self.rows(p)].astype(f32)
-            for k in range(1, self.lines):
+            for k in range(1, n):
                 value = value + self.a_line[k - 1].astype(f32)
-            total[self.rows(p), self.columns(0, x)] = value.astype(bf16)
-            value = self.b_sum[:, self.columns(0, x)].astype(f32) + self.b_in[...].astype(f32)
-            total[self.rows(p), self.columns(1, x)] = value.astype(bf16)
+            total[self.rows(x * n + p), self.a] = value.astype(bf16)
+            value = self.b_sum[self.rows(x)].astype(f32) + self.b_in[...].astype(f32)
+            total[self.rows(p * 2 + x), self.b] = value.astype(bf16)
+
+
+def sum_buffers(lines, tall, wide, rest):
+    height = tall // (2 * lines)
+    shapes = (
+        (lines * height, wide), (lines * height, wide), (lines - 1, height, wide),
+        (lines - 1, 2 * height, rest), (2 * height, rest), (height, rest),
+    )
+    return [pltpu.VMEM(shape, bf16) for shape in shapes]
 
 
 def back_body(
     ctx, step, block, chunk, ready,
     gn, hid, gains, cot, wo, att_t, q_t, kv, pos, lse, cos_r, sin_r, n1_t, inp, wp, n2, n2_g,
-    cot_a0, cot_a1, cot_b0, cot_b1, x_a0, wg_h, wu_h, wd_h,
-    inp_o, grads_o, acc_g, acc_u, acc_d, x_a1, x_b0, x_b1, x_fa0, x_fa1, x_fb0, x_fb1,
+    cot_g, cot_a0, cot_a1, cot_b0, cot_b1, cot_fb0, x_a0, x_a1, wg_h, wu_h, wd_h,
+    inp_o, grads_o, acc_g, acc_u, acc_d, x_b0, x_b1, x_fa0, x_fa1, x_fb0, x_fb1, cot_fa0, cot_fa1, cot_fb1,
     gh, do_t, part, dq, held, ghl, ghl_g, low_t, n1_g, low_g, gp, gp_g, vec, vec_g,
-    pay, total_r, a_in, a_sum, a_line, b_line, b_sum, b_in,
+    pay, total_r, p0, p1, p2, p3, p4, p5, q0, q1, q2, q3, q4, q5,
     xs, cs, wg, wu, wd, acc,
     ks, kr, ts, tr, as_, ar, vs, vr, sum_s, sum_r, ws, ins, outs, *sems
 ):
@@ -714,10 +712,15 @@
         ]
 
     ready()
-    spread = Spread(place, ctx // 2, n2, n2_g, ((x_a0, x_a1), (x_b0, x_b1), (x_fa0, x_fa1), (x_fb0, x_fb1)), sems)
-    spread.pairs_out(0)
+    spread = Spread(place, ctx // 2, n2, n2_g, ((x_a0, x_a1), (x_b0, x_b1), (x_fa0, x_fa1), (x_fb0, x_fb1)), sems[:9])
+    rest = Spread(
+        place, ctx // 2, cot, cot_g, ((cot_a0, cot_a1), None, (cot_fa0, cot_fa1), (cot_fb0, cot_fb1)), sems[9:]
+    )
+    rest.pairs_out(2)
     spread.lines_out(1)
-    kept = spread.keep(n2_g, 1, 2, 3)
+    rest.cross(0)
+    rest.cross(1)
+    kept = spread.keep(n2_g, 1, 2, 3) + rest.keep(cot_g, 2)
     loads = [
         pltpu.make_async_copy(src, dst, ws.at[j])
         for j, (src, dst) in enumerate(((wg_h, wg), (wu_h, wu), (wd_h, wd)))
@@ -786,15 +789,26 @@
     pay[pl.ds(0, depth), pl.ds(columns, width)] = plain_dot(low_all, ghl_g[...].reshape(4 * tok, width)).astype(
         bf16
     )
+    pay[pl.ds(depth, pay.shape[0] - depth)] = jnp.zeros((pay.shape[0] - depth, pay.shape[1]), bf16)
+    third = width // 7
+    early = Total(
+        place, ctx // 2, columns, 5 * third, 2 * third, pay, total_r, (p0, p1, p2, p3, p4, p5), sum_s.at[0], sum_r.at[0]
+    )
+    late = Total(
+        place, ctx // 2, 0, 6 * third, 3 * third, pay, total_r, (q0, q1, q2, q3, q4, q5), sum_s.at[1], sum_r.at[1]
+    )
     pairs = part[c].astype(f32)
     for k, copy in enumerate(owners):
         copy.wait()
         pairs = pairs + held[k].astype(f32)
+    early.start(0)
+    spread.lines_out(2)
     g_k = turn_back(pairs[:, :key_width].T, cos, sin, HD)
     gp[:, query_width : query_width + key_width] = g_k.T.astype(bf16)
     gp[:, query_width + key_width :] = pairs[:, key_width:].astype(bf16)
     items = [(gp, lambda g, at: gp_g.at[g, at])]
     tokens_start(items, ts.at[1], tr.at[1], place)
+    spread.on_line(1, True)
     g_normed = over_last(gp[...], wp[...])
     values = inp[...].astype(f32)
     back, gain_one = norm_grad(values, gains[0:1], g_normed)
@@ -806,9 +820,8 @@
     vectors = [remote(vec, vec_g.at[k], vs.at[k], vr.at[k], (c, g)) for k, g in enumerate((m, n, far))]
     for copy in vectors:
         copy.start()
-    spread.on_pair(0)
-    spread.on_line(1, True)
-    spread.lines_out(2)
+    early.wait(0)
+    early.start(1)
     tokens_finish(items, ts.at[1], tr.at[1], place)
     n1_all = jnp.concatenate([n1_g[g] for g in range(4)], 1)
     pay[pl.ds(0, depth), pl.ds(0, columns)] = plain_dot(n1_all, gp_g[...].reshape(4 * tok, columns)).astype(bf16)
@@ -816,10 +829,10 @@
     for k, copy in enumerate(vectors):
         copy.wait()
         total = total + vec_g[k]
-    pay[pl.ds(depth, 8)] = total.astype(bf16)
-    pay[pl.ds(depth + 8, pay.shape[0] - depth - 8)] = jnp.zeros_like(pay[pl.ds(depth + 8, pay.shape[0] - depth - 8)])
-    summed = Total(place, ctx // 2, pay, total_r, a_in, a_sum, a_line, b_line, b_sum, b_in, sum_s, sum_r)
-    summed.start(0)
+    pay[pl.ds(depth, 8), :columns] = total[:, :columns].astype(bf16)
+    early.wait(1)
+    early.start(2)
+    late.start(0)
     spread.cross(0)
     spread.cross(1)
     for copy in loads:
@@ -831,7 +844,7 @@
         if way == 1:
             spread.finish_line(1)
             kept[0].wait()
-        spread.finish_pair(way)
+            spread.finish_pair(1)
         for i in range(per_part):
             count = chunk // tok // 2
             at = pl.ds(i * count, count)
@@ -858,22 +871,36 @@
                         acc[j, at] = value
                     else:
                         acc[j, at] += value
-                for stage in range(3 if first else 0):
-
-                    @pl.when(b == stage)
+                if first:
+
+                    @pl.when(b == 0)
                     def _():
-                        summed.wait(stage)
-                        summed.start(stage + 1)
-
-                if way == 0 and i == 0:
+                        early.wait(2)
+                        early.start(3)
+                        rest.on_y(0)
+                        rest.on_y(1)
 
                     @pl.when(b == 1)
                     def _():
-                        spread.on_pair(1)
+                        late.wait(0)
+                        late.start(1)
+
+                    @pl.when(b == 2)
+                    def _():
+                        early.wait(3)
+                        rest.on_pair(2)
+                        spread.on_line(2, True)
 
                     @pl.when(b == 3)
                     def _():
-                        spread.on_line(2, True)
+                        late.wait(1)
+                        late.start(2)
+
+                if way == 0 and i == 0:
+
+                    @pl.when(b == 2)
+                    def _():
+                        spread.on_pair(1)
 
                 if way == 1 and i == 0:
 
@@ -883,9 +910,11 @@
 
                     @pl.when(b == 1)
                     def _():
+                        late.wait(2)
+                        late.start(3)
                         spread.on_y(1)
 
-                    @pl.when(b == 2)
+                    @pl.when(b == 3)
                     def _():
                         spread.on_pair(2)
 
@@ -893,11 +922,13 @@
                     for j, out in enumerate((acc_g, acc_u, acc_d)):
                         pltpu.make_async_copy(acc.at[j, at], out.at[at], outs.at[b, j]).start()
 
-    summed.wait(3)
+    late.wait(3)
     grads_o[...] = total_r[...].astype(f32)
     spread.finish_line(2)
     spread.finish_pair(2)
     spread.finish_cross()
+    rest.finish_pair(2)
+    rest.finish_cross()
     for b in range(blocks):
         at = pl.ds(b * block, block)
         for j, out in enumerate((acc_g, acc_u, acc_d)):
@@ -923,8 +954,22 @@
 
 
 def hidden_body(
-    chunk, block, x0_h, x1_h, x2_h, x3_h, c0_h, c1_h, c2_h, c3_h, wg_h, wu_h, wd_h, ig_h, iu_h, id_h, og_h, ou_h, od_h, xs, cs, wg, wu, wd, acc, in_sem, w_sem, out_sem, init_sem
+    chunk, block, windows, x0_h, x1_h, x2_h, x3_h, c0_h, c1_h, c2_h, c3_h, wg_h, wu_h, wd_h, ig_h, iu_h, id_h, *refs
 ):
+    passed, refs = refs[:4], refs[4:]
+    og_h, ou_h, od_h = refs[:3]
+    results_out, refs = refs[3 : 3 + len(windows)], refs[3 + len(windows) :]
+    xs, cs, wg, wu, wd, acc, in_sem, w_sem, out_sem, init_sem, pass_sem = refs[:11]
+    through = []
+    for j, (which, at) in enumerate(windows):
+        src = passed[which] if at is None else passed[which].at[at]
+        buffer = refs[11 + j]
+        through.append(
+            (
+                pltpu.make_async_copy(src, buffer, pass_sem.at[0, j]),
+                pltpu.make_async_copy(buffer, results_out[j], pass_sem.at[1, j]),
+            )
+        )
     parts = (((x0_h, x1_h), (c0_h, c1_h)), ((x2_h, x3_h), (c2_h, c3_h)))
     rows = 4 * x0_h.shape[0]
     steps, blocks, held = rows // chunk, wg.shape[0] // block, xs.shape[0] // chunk
@@ -997,6 +1042,8 @@
     for b in range(1, slots):
         for copy in weights(b) + initial(b, b):
             copy.start()
+    for copy, _ in through:
+        copy.start()
 
     @pl.loop(0, blocks)
     def _(b):
@@ -1007,6 +1054,9 @@
         def _():
             for copy in weights(1):
                 copy.wait()
+            for into, out in through:
+                into.wait()
+                out.start()
 
         @pl.loop(0, steps)
         def _(i):
@@ -1042,9 +1092,11 @@
     for b in range(max(0, blocks - slots), blocks):
         for copy in results(b, b % slots):
             copy.wait()
-
-
-def hidden_grads(xs, cots, wg, wu, wd, initial):
+    for _, out in through:
+        out.wait()
+
+
+def hidden_grads(xs, cots, wg, wu, wd, initial, passed, windows):
     width = wg.shape[1]
     xs, cots = [[part.reshape(-1, width) for part in parts] for parts in (xs, cots)]
     rows = sum(part.shape[0] for part in xs)
@@ -1055,19 +1107,22 @@
     any_spec = pl.BlockSpec(memory_space=pl.ANY)
     dma = pltpu.SemaphoreType.DMA
     return pl.pallas_call(
-        functools.partial(hidden_body, chunk, block),
-        out_shape=(jax.ShapeDtypeStruct((units, width), f32),) * 3,
-        in_specs=[any_spec] * 14,
-        out_specs=(any_spec,) * 3,
+        functools.partial(hidden_body, chunk, block, [window[:2] for window in windows]),
+        out_shape=(jax.ShapeDtypeStruct((units, width), f32),) * 3
+        + tuple(jax.ShapeDtypeStruct(shape, dtype) for _, _, shape, dtype in windows),
+        in_specs=[any_spec] * 18,
+        out_specs=(any_spec,) * (3 + len(windows)),
         scratch_shapes=[pltpu.VMEM((held * chunk, width), bf16)] * 2
         + [pltpu.VMEM((units, width), bf16)] * 3
-        + [pltpu.VMEM((2, 3, block, width), f32), dma((held, 2, 2)), dma((2, 3)), dma((2, 3)), dma((2, 3))],
+        + [pltpu.VMEM((2, 3, block, width), f32), dma((held, 2, 2)), dma((2, 3)), dma((2, 3)), dma((2, 3))]
+        + [dma((2, len(windows)))]
+        + [pltpu.VMEM(shape, dtype) for _, _, shape, dtype in windows],
         compiler_params=pltpu.CompilerParams(vmem_limit_bytes=62 << 20),
         cost_estimate=pl.CostEstimate(
             flops=12 * rows * width * units, bytes_accessed=4 * rows * width + 18 * units * width, transcendentals=0
         ),
         name="hidden_grads",
-    )(*xs, *cots, wg, wu, wd, *initial)
+    )(*xs, *cots, wg, wu, wd, *initial, *passed)
 
 
 def shards(
@@ -1158,7 +1213,7 @@
     )
     units = w_down.shape[0]
     wg_t, wu_t = w_gate.T, w_up.T
-    (grad_normed2, block_out, x_group, cot_b1, cot_fa0, cot_fa1, cot_fb0, cot_fb1, x_a0) = staged_call(
+    grad_normed2, block_out, x_group, cot_b1, cot_fb0, x_a0, x_a1 = staged_call(
         functools.partial(mid_body, lines),
         (normed_second, cot_group, grad_out, cot_a0, cot_a1, cot_b0, hidden_state, wg_t, wu_t, w_down),
         (3, 4, 5, 7, 8, 9),
@@ -1167,8 +1222,8 @@
             sds((tok, width), bf16),
             sds((fsdp, tok, width), bf16),
         )
-        + (half_blocks,) * 6,
-        (3, 4, 5, 6, 7, 8),
+        + (half_blocks,) * 4,
+        (3, 4, 5, 6),
         [pltpu.VMEM((units, width), bf16)] * 3
         + [
             pltpu.VMEM((3, 2 * tok, units), bf16),
@@ -1190,22 +1245,24 @@
             flops=12 * fsdp * tok * width * units, bytes_accessed=6 * units * width, transcendentals=0
         ),
     )
-    block_out = block_out[None]
-    tall, everything = 256, columns + width
-    height = tall // lines
+    tall, everything = max(256, 16 * ctx), columns + width
+    third = width // 7
     block = units // 4
     chunk = math.gcd(ctx * tok, 1024)
     big = sds((units, width), f32)
-    (input_grad, weight_grads, acc_g, acc_u, acc_d, x_a1, x_b0, x_b1, x_fa0, x_fa1, x_fb0, x_fb1) = staged_call(
+    (
+        input_grad, weight_grads, acc_g, acc_u, acc_d, x_b0, x_b1, x_fa0, x_fa1, x_fb0, x_fb1, cot_fa0, cot_fa1,
+        cot_fb1,
+    ) = staged_call(
         functools.partial(back_body, ctx, step, block, chunk),
         (
             grad_normed2, hidden_state, gains, grad_out, wo_full, att_t, q_t, kv_all, own_positions, log_total,
-            cosine, sine_table, n1_t, input_rows, w_project, normed_second, x_group, cot_a0, cot_a1,
-            cot_b0, cot_b1, x_a0, wg_t, wu_t, w_down,
+            cosine, sine_table, n1_t, input_rows, w_project, normed_second, x_group, cot_group, cot_a0,
+            cot_a1, cot_b0, cot_b1, cot_fb0, x_a0, x_a1, wg_t, wu_t, w_down,
         ),
-        (17, 18, 19, 20, 21, 22, 23, 24),
-        (sds((tok, width), bf16), sds((tall, everything), f32), big, big, big) + (half_blocks,) * 7,
-        (2, 3, 4, 5, 6, 7, 8, 9, 10, 11),
+        (18, 19, 20, 21, 22, 23, 24, 25, 26, 27),
+        (sds((tok, width), bf16), sds((tall, everything), f32), big, big, big) + (half_blocks,) * 9,
+        tuple(range(2, 14)),
         [
             pltpu.VMEM((tok, width), f32),
             pltpu.VMEM((query_width, tok), bf16),
@@ -1223,12 +1280,8 @@
             pltpu.VMEM((3, 8, everything), f32),
             pltpu.VMEM((tall, everything), bf16),
             pltpu.VMEM((tall, everything), bf16),
-            pltpu.VMEM((tall, everything // 4), bf16),
-            pltpu.VMEM((tall, everything // 4), bf16),
-            pltpu.VMEM((lines - 1, height, everything // 4), bf16),
-            pltpu.VMEM((lines - 1, height, everything // 2), bf16),
-            pltpu.VMEM((height, everything // 2), bf16),
-            pltpu.VMEM((height, everything // 4), bf16),
+            *sum_buffers(lines, tall, 5 * third, 2 * third),
+            *sum_buffers(lines, tall, 6 * third, 3 * third),
             pltpu.VMEM((2, chunk // tok // 2, 2, tok // 2, width), bf16),
             pltpu.VMEM((2, chunk // tok // 2, 2, tok // 2, width), bf16),
             pltpu.VMEM((units, width), bf16),
@@ -1243,18 +1296,18 @@
             dma((2, 3)),
             dma((3,)),
             dma((3,)),
-            dma((2, 4, lines)),
-            dma((2, 4, lines)),
+            dma((2, 2, 4, lines)),
+            dma((2, 2, 4, lines)),
             dma((3,)),
             dma((2, 2)),
             dma((4, 3)),
         ]
+        + spread_sems(lines)
         + spread_sems(lines),
         3,
         "back",
         pl.CostEstimate(flops=4 * 10**10, bytes_accessed=6 * 10**7, transcendentals=0),
     )
-    input_grad = input_grad[None]
     starts = ((0, 0, width), (1, 0, width), (2, 0, query_width), (2, query_width, key_width),
               (2, query_width + key_width, key_width))
 
@@ -1263,27 +1316,34 @@
         return lax.dynamic_slice_in_dim(weight_grads[depth + row], start + f * share, share, 0)
 
     own = [piece(*at) for at in starts]
-    weight_grads = weight_grads[:depth]
-
-    gate_grad, up_grad, down_grad = hidden_grads(
-        (x_fa0, x_fa1, x_fb0, x_fb1), (cot_fa0, cot_fa1, cot_fb0, cot_fb1), wg_t, wu_t, w_down, (acc_g, acc_u, acc_d)
+
+    ends = (0, query_width, query_width + key_width, columns, columns + width)
+    windows = [
+        (0, (slice(0, depth), slice(ends[j], ends[j + 1])), (depth, ends[j + 1] - ends[j]), f32) for j in range(4)
+    ]
+    windows += [(1, None, (tok, width), bf16), (2, None, (tok, width), bf16), (3, None, (H, tok), f32)]
+    gate_grad, up_grad, down_grad, query_grad, key_grad, value_grad, output_grad, block_out, input_grad, lse = (
+        hidden_grads(
+            (x_fa0, x_fa1, x_fb0, x_fb1), (cot_fa0, cot_fa1, cot_fb0, cot_fb1), wg_t, wu_t, w_down,
+            (acc_g, acc_u, acc_d), (weight_grads, block_out, input_grad, log_total), windows,
+        )
     )
     return (
-        block_out,
-        input_grad,
+        block_out[None],
+        input_grad[None],
         own[0],
-        weight_grads[:, :query_width],
+        query_grad,
         own[2],
-        weight_grads[:, query_width : query_width + key_width],
+        key_grad,
         own[3],
-        weight_grads[:, query_width + key_width : query_width + 2 * key_width],
+        value_grad,
         own[4],
-        weight_grads[:, query_width + 2 * key_width :],
+        output_grad,
         own[1],
         gate_grad.T,
         up_grad.T,
         down_grad,
-        log_total[None],
+        lse[None],
     )
 
 

time: 249 us -> 238 us (0.956)
  Pallas kernels: 237 us -> 231 us
  local copies, waits for them, and re-layouts: 9.14 us -> 4.13 us
    pallas_call x3, Pallas kernels: 197 us -> 191 us  [staged_call(): pl.pallas_call(kernel, out_shape=out_shape, in_specs=[hbm] * len(args), o...]
    slice x2 -> x0, local copies, waits for them, and re-layouts: 4.29 us -> none  [the longest x1 2.63 us: shards(): weight_grads[:, query_width + 2 * key_width:]]
where the time goes in v4:
time: 238 us
  Pallas kernels  231 us (97%)
  local copies, waits for them, and re-layouts  4.13 us (2%)
    pallas_call x3, Pallas kernels, staged_call(): pl.pallas_call(kernel, out_shape=out_shape, in_specs=[hbm] * len(args), o...  191 us
    pallas_call x1, Pallas kernels, hidden_grads(): pl.pallas_call(functools.partial(hidden_body, chunk, block, [window[:2] f...  40.6 us

profile of v4, /device:TPU:0, one launch (start us, length us, event | category | flops | bytes accessed | tf_op | source)
XLA Modules:
  0.0 237.7 jit_solution(5350239851904373270)
XLA Ops:
  0.6 0.7 convert_bitcast_fusion
  1.3 0.8 multiply_sine_fusion
  2.1 56.1 %front.1 = (bf16[896,1152]{1,0:T(8,128)(2,1)}, bf16[896,896]{1,0:T(8,128)(2,1)}, f32[8,896]{1,0:T(8,128)}, bf16[896,128]{1,0:T(8,128)(2,1)}, bf16[896,128]{1,0:T...) custom-call(bf16[128,896]{1,0:T(8,128)(2,1)} %bitcast.36, ...), custom_call_target="tpu_custom_call" | custom-call | flops 4000000000 | bytes 10000000 | tf_op jit(solution)/shard_map/front/pallas_call | solution.py:162
  58.1 36.2 %mid.1 = (f32[128,896]{1,0:T(8,128)}, bf16[128,896]{1,0:T(8,128)(2,1)}, bf16[4,128,896]{2,1,0:T(8,128)(2,1)}, bf16[4,2,64,896]{3,2,1,0:T(8,128)(2,1)}, bf16[4,2,...) custom-call(bf16[128,896]{1,0:T(8,128)(2,1)} %get-tuple-element.58.refs_0_.refs_15_, ...), custom_call_target="tpu_custom_call" | custom-call | flops 6694109184 | bytes 6537216 | tf_op jit(solution)/shard_map/mid/pallas_call | solution.py:162
  94.4 98.7 %back.1 = (bf16[128,896]{1,0:T(8,128)(2,1)}, f32[256,2048]{1,0:T(8,128)}, f32[1216,896]{1,0:T(8,128)}, f32[1216,896]{1,0:T(8,128)}, f32[1216,896]{1,0:T(8,128)},...) custom-call(f32[128,896]{1,0:T(8,128)} %get-tuple-element.64.refs_0_, ...), custom_call_target="tpu_custom_call" | custom-call | flops 40000000000 | bytes 60000000 | tf_op jit(solution)/shard_map/back/pallas_call | solution.py:162
  193.0 1.0 fusion.2
  194.0 0.6 constant_dynamic-slice_fusion
  194.6 40.6 %hidden_grads.1 = (f32[1216,896]{1,0:T(8,128)}, f32[1216,896]{1,0:T(8,128)}, f32[1216,896]{1,0:T(8,128)}, f32[224,896]{1,0:T(8,128)}, f32[224,128]{1,0:T(8,128)}...) custom-call(bf16[512,896]{1,0:T(8,128)(2,1)} %bitcast.44, ...), custom_call_target="tpu_custom_call" | custom-call | flops 26776436736 | bytes 26951680 | tf_op jit(solution)/shard_map/hidden_grads/pallas_call | solution.py:1109
  235.2 1.3 copy.30
  236.5 0.6 fusion.1
  237.1 0.6 constant_dynamic-slice_fusion.4
  (1 shorter events, 0.0 us)

commit v5 on v4

--- a/solution.py
+++ b/solution.py
@@ -555,7 +555,7 @@
             at = slice(j * tok, (j + 1) * tok)
             h = g * group + j
             att_o[h * HD : (h + 1) * HD] = attention[:, at]
-            lse_o[h : h + 1] = logs[:, at]
+            lse_o[h] = logs[:, at]
     hidden = values + plain_dot(att_o[...].T.astype(bf16), wo_o[...])
     hid_o[...] = hidden
     inverse = lax.rsqrt(jnp.mean(hidden * hidden, -1, keepdims=True) + EPSILON)
@@ -742,7 +742,7 @@
     for g in range(KV):
         queries, grads = heads(q_t, g, group, HD), heads(do_t, g, group, HD)
         delta = jnp.sum(grads.astype(f32) * heads(att_t, g, group, HD), 0, keepdims=True)
-        total = jnp.concatenate([lse[pl.ds(g * group + j, 1)] for j in range(group)], 1)
+        total = jnp.concatenate([lse[g * group + j] for j in range(group)], 1)
 
         @pl.loop(0, kv.shape[0] // step)
         def _(i):
@@ -1187,7 +1187,7 @@
                 sds((ctx, tok, 2 * key_width), bf16),
                 sds((fsdp, tok, width), bf16),
                 sds((query_width, tok), f32),
-                sds((H, tok), f32),
+                sds((H, 1, tok), f32),
                 sds((tok, width), f32),
                 sds((tok, width), bf16),
                 half_blocks,
@@ -1321,7 +1321,7 @@
     windows = [
         (0, (slice(0, depth), slice(ends[j], ends[j + 1])), (depth, ends[j + 1] - ends[j]), f32) for j in range(4)
     ]
-    windows += [(1, None, (tok, width), bf16), (2, None, (tok, width), bf16), (3, None, (H, tok), f32)]
+    windows += [(1, None, (tok, width), bf16), (2, None, (tok, width), bf16), (3, None, (H, 1, tok), f32)]
     gate_grad, up_grad, down_grad, query_grad, key_grad, value_grad, output_grad, block_out, input_grad, lse = (
         hidden_grads(
             (x_fa0, x_fa1, x_fb0, x_fb1), (cot_fa0, cot_fa1, cot_fb0, cot_fb1), wg_t, wu_t, w_down,
@@ -1343,7 +1343,7 @@
         gate_grad.T,
         up_grad.T,
         down_grad,
-        lse[None],
+        lse.transpose(1, 0, 2),
     )
 
 

time: 238 us -> 237 us (level)
  no operation moved by 1% of the time
where the time goes in v5:
time: 237 us
  Pallas kernels  232 us (98%)
  local copies, waits for them, and re-layouts  2.84 us (1%)
    pallas_call x3, Pallas kernels, staged_call(): pl.pallas_call(kernel, out_shape=out_shape, in_specs=[hbm] * len(args), o...  191 us
    pallas_call x1, Pallas kernels, hidden_grads(): pl.pallas_call(functools.partial(hidden_body, chunk, block, [window[:2] f...  40.6 us

profile of v5, /device:TPU:0, one launch (start us, length us, event | category | flops | bytes accessed | tf_op | source)
XLA Modules:
  0.0 236.5 jit_solution(5302830135235057374)
XLA Ops:
  0.6 0.7 convert_bitcast_fusion
  1.3 0.8 multiply_sine_fusion
  2.1 56.1 %front.1 = (bf16[896,1152]{1,0:T(8,128)(2,1)}, bf16[896,896]{1,0:T(8,128)(2,1)}, f32[8,896]{1,0:T(8,128)}, bf16[896,128]{1,0:T(8,128)(2,1)}, bf16[896,128]{1,0:T...) custom-call(bf16[128,896]{1,0:T(8,128)(2,1)} %bitcast.35, ...), custom_call_target="tpu_custom_call" | custom-call | flops 4000000000 | bytes 10000000 | tf_op jit(solution)/shard_map/front/pallas_call | solution.py:162
  58.2 36.2 %mid.1 = (f32[128,896]{1,0:T(8,128)}, bf16[128,896]{1,0:T(8,128)(2,1)}, bf16[4,128,896]{2,1,0:T(8,128)(2,1)}, bf16[4,2,64,896]{3,2,1,0:T(8,128)(2,1)}, bf16[4,2,...) custom-call(bf16[128,896]{1,0:T(8,128)(2,1)} %get-tuple-element.58.refs_0_.refs_15_, ...), custom_call_target="tpu_custom_call" | custom-call | flops 6694109184 | bytes 6537216 | tf_op jit(solution)/shard_map/mid/pallas_call | solution.py:162
  94.4 98.6 %back.1 = (bf16[128,896]{1,0:T(8,128)(2,1)}, f32[256,2048]{1,0:T(8,128)}, f32[1216,896]{1,0:T(8,128)}, f32[1216,896]{1,0:T(8,128)}, f32[1216,896]{1,0:T(8,128)},...) custom-call(f32[128,896]{1,0:T(8,128)} %get-tuple-element.64.refs_0_, ...), custom_call_target="tpu_custom_call" | custom-call | flops 40000000000 | bytes 60000000 | tf_op jit(solution)/shard_map/back/pallas_call | solution.py:162
  193.0 1.0 fusion.2
  194.0 0.6 constant_dynamic-slice_fusion
  194.6 40.6 %hidden_grads.1 = (f32[1216,896]{1,0:T(8,128)}, f32[1216,896]{1,0:T(8,128)}, f32[1216,896]{1,0:T(8,128)}, f32[224,896]{1,0:T(8,128)}, f32[224,128]{1,0:T(8,128)}...) custom-call(bf16[512,896]{1,0:T(8,128)(2,1)} %bitcast.43, ...), custom_call_target="tpu_custom_call" | custom-call | flops 26776436736 | bytes 26951680 | tf_op jit(solution)/shard_map/hidden_grads/pallas_call | solution.py:1109
  235.3 0.6 fusion.1
  235.9 0.6 constant_dynamic-slice_fusion.4
  (1 shorter events, 0.0 us)
